TPU v7x, 32 devices: a whole 2x2x4 slice. The times are simulated.
32 devices in a mesh: batch: 16 (over z, x, core), space: 2 (over y).
Axes of the slice: x: 2, y: 2, z: 4, core: 2. Of those that a mesh axis runs over, the one named last changes fastest.
Arguments:
- latents: float32 [16, 32, 64, 4], P('batch', 'space'), may hold values from -16 to 16
- noise_draw: float32 [16, 32, 64, 4], P('batch', 'space'), may hold values from -5 to 5
- timesteps: int32 [16], P('batch'), may hold values from 200 to 799
- inlet_conv: bfloat16 [36, 320], replicated, may hold values from -1 to 1
- time_first: bfloat16 [320, 1280], P(None, 'batch'), may hold values from -0.3125 to 0.3125
- time_first_bias: float32 [1280], replicated, may hold values from -4 to 4
- time_second: bfloat16 [1280, 320], P(None, 'batch'), may hold values from -0.3125 to 0.3125
- time_second_bias: float32 [320], replicated, may hold values from -4 to 4
- conv_first: bfloat16 [2880, 320], P(None, 'batch'), may hold values from -0.109375 to 0.109375
- conv_second: bfloat16 [2880, 320], P(None, 'batch'), may hold values from -0.109375 to 0.109375
- proj_inner: bfloat16 [320, 320], P(None, 'batch'), may hold values from -0.3125 to 0.3125
- query_weight: bfloat16 [320, 320], P(None, 'batch'), may hold values from -30 to 30
- key_weight: bfloat16 [320, 320], P(None, 'batch'), may hold values from -1 to 1
- value_weight: bfloat16 [320, 320], P(None, 'batch'), may hold values from -0.625 to 0.625
- attn_out: bfloat16 [320, 320], P(None, 'batch'), may hold values from -0.625 to 0.625
- proj_outer: bfloat16 [320, 320], P(None, 'batch'), may hold values from -0.3125 to 0.3125
- outlet_conv: bfloat16 [2880, 4], replicated, may hold values from -0.109375 to 0.109375
- first_gain: float32 [320], replicated, may hold values from 0.1 to 1.9
- second_gain: float32 [320], replicated, may hold values from 0.1 to 1.9
- third_gain: float32 [320], replicated, may hold values from 0.1 to 1.9
- final_gain: float32 [320], replicated, may hold values from 0.1 to 1.9
- layer_gain: float32 [320], replicated, may hold values from 0.1 to 1.9
Outputs:
- guidance: float32 [16, 32, 64, 4], P('batch', 'space')
All inputs are finite; a program needn't handle non-finite values.
Results may differ from a plain program's by a relative error of at most 0.029.
Values may be sent and summed in bfloat16 or wider, within the bound.
No kernel may reach another device: no remote copies, remote signals or barrier semaphores. Data moves between devices by JAX's collectives and lax.ppermute only.
A program may use at most 128 MiB of HBM per device.

v0:
```python
import math

import jax
import jax.numpy as jnp
from jax import lax
from jax.sharding import PartitionSpec as P

HEADS = 8
HEAD_SIZE = 40
GROUPS = 32
STEPS = 1000


EPS_GROUP = 1e-06
EPS_BLOCK = 1e-05
EPS_LAYER = 1e-05


def extended(cells, sides, width):
    for axis, dim in sides:
        count = lax.axis_size(axis)
        ends = count - 1
        head = lax.slice_in_dim(cells, 0, width, axis=dim)
        tail = lax.slice_in_dim(cells, cells.shape[dim] - width, cells.shape[dim], axis=dim)
        cells = jnp.concatenate(
            [
                lax.ppermute(tail, axis, [(i, (i + 1) % count) for i in range(ends)]),
                cells,
                lax.ppermute(head, axis, [((i + 1) % count, i) for i in range(ends)]),
            ],
            axis=dim,
        )
    return cells


def plan():
    fraction = jnp.arange(STEPS, dtype=jnp.float32) / (STEPS - 1)
    beta_root = math.sqrt(0.00085) + fraction * (math.sqrt(0.012) - math.sqrt(0.00085))
    return jnp.cumprod(1.0 - beta_root * beta_root)


def lookup(timesteps):
    plan_tab = plan()
    matches = jnp.arange(STEPS, dtype=jnp.int32)[None, :] == timesteps[:, None]
    return jnp.sum(jnp.where(matches, plan_tab[None, :], 0.0), axis=1)


def waveform_of(timesteps, halfway):
    frequency = jnp.exp(-math.log(10000.0) * jnp.arange(halfway, dtype=jnp.float32) / halfway)
    angles = timesteps.astype(jnp.float32)[:, None] * frequency[None, :]
    return jnp.concatenate([jnp.cos(angles), jnp.sin(angles)], axis=1).astype(jnp.bfloat16)


def embed_sharded(timesteps, first, first_bias, second, second_bias):
    all_steps = lax.all_gather(timesteps, "batch", axis=0, tiled=True)
    position = lax.axis_index("batch")
    width_one = first.shape[1]
    width_two = second.shape[1]
    waveform = waveform_of(all_steps, first.shape[0] // 2)
    bias_one = lax.dynamic_slice_in_dim(first_bias, position * width_one, width_one, 0)
    inner = jax.nn.silu(jnp.dot(waveform, first, preferred_element_type=jnp.float32) + bias_one)
    hidden = jax.nn.silu(inner).astype(jnp.bfloat16)
    hidden_all = lax.all_gather(hidden, "batch", axis=1, tiled=True)
    bias_two = lax.dynamic_slice_in_dim(second_bias, position * width_two, width_two, 0)
    columns = jnp.dot(hidden_all, second, preferred_element_type=jnp.float32) + bias_two
    return lax.all_to_all(columns, "batch", split_axis=0, concat_axis=1, tiled=True)


def convolve(padded, kernel):
    height = padded.shape[1] - 2
    breadth = padded.shape[2] - 2
    width_in = padded.shape[3]
    result = None
    for offset in range(9):
        row_off, col_off = (offset // 3, offset % 3)
        window = padded[:, row_off : row_off + height, col_off : col_off + breadth, :]
        partial_sum = jnp.einsum(
            "bhwc,cd->bhwd",
            window,
            kernel[offset * width_in : (offset + 1) * width_in],
            preferred_element_type=jnp.float32,
        )
        result = partial_sum if result is None else result + partial_sum
    return result


def with_rims(field):
    padded = extended(field, (("space", 1),), 1)
    return jnp.pad(padded, ((0, 0), (0, 0), (1, 1), (0, 0)))


def with_latent_rims(field):
    padded = extended(field, (("space", 1),), 1)
    return jnp.pad(padded, ((0, 0), (0, 0), (1, 1), (0, 0)))


def group_norm(field, gain_vec, epsilon):
    view_n, height, breadth, chan_n = field.shape
    grouped = field.reshape(view_n, height, breadth, GROUPS, chan_n // GROUPS)
    sums_local = jnp.sum(grouped, axis=(1, 2, 4))
    squares_local = jnp.sum(grouped * grouped, axis=(1, 2, 4))
    sums_all, squares_all = lax.psum((sums_local, squares_local), "space")
    number = height * lax.axis_size("space") * breadth * (chan_n // GROUPS)
    means = sums_all / number
    squares = squares_all / number
    factor = lax.rsqrt(squares - means * means + epsilon)
    normal_f = (grouped - means[:, None, None, :, None]) * factor[:, None, None, :, None]
    return normal_f.reshape(view_n, height, breadth, chan_n) * gain_vec


def layer_norm(field, gain_vec):
    means = jnp.mean(field, axis=-1, keepdims=True)
    centred = field - means
    spread = jnp.mean(centred * centred, axis=-1, keepdims=True)
    return centred * lax.rsqrt(spread + EPS_LAYER) * gain_vec


def keys_everywhere(queries, key_rows, value_rows):
    view_n, token_n, chan_n = queries.shape
    factor = 1.0 / math.sqrt(HEAD_SIZE)
    query_heads = queries.reshape(view_n, token_n, HEADS, HEAD_SIZE)
    row_max = jnp.full((view_n, HEADS, token_n), -jnp.inf, jnp.float32)
    row_sum = jnp.zeros((view_n, HEADS, token_n), jnp.float32)
    accum = jnp.zeros((view_n, HEADS, token_n, HEAD_SIZE), jnp.float32)
    key_part = lax.all_gather(key_rows, "space", axis=1, tiled=True)
    value_part = lax.all_gather(value_rows, "space", axis=1, tiled=True)
    length = key_part.shape[1]
    block_n = min(512, length)
    for offset in range(0, length, block_n):
        key_blk = key_part[:, offset : offset + block_n]
        value_blk = value_part[:, offset : offset + block_n]
        rows_here = key_blk.shape[1]
        key_blk = key_blk.reshape(view_n, rows_here, HEADS, HEAD_SIZE)
        value_blk = value_blk.reshape(view_n, rows_here, HEADS, HEAD_SIZE)
        scores = (
            jnp.einsum("bqhd,bkhd->bhqk", query_heads, key_blk, preferred_element_type=jnp.float32)
            * factor
        )
        new_max = jnp.maximum(row_max, jnp.max(scores, axis=-1))
        shrink = jnp.exp(row_max - new_max)
        weights = jnp.exp(scores - new_max[..., None])
        row_sum = row_sum * shrink + jnp.sum(weights, axis=-1)
        accum = accum * shrink[..., None] + jnp.einsum(
            "bhqk,bkhd->bhqd",
            weights.astype(jnp.bfloat16),
            value_blk,
            preferred_element_type=jnp.float32,
        )
        row_max = new_max
    row_max, row_sum, accum = (row_max, row_sum, accum)
    result = accum / row_sum[..., None]
    return result.transpose(0, 2, 1, 3).reshape(view_n, token_n, chan_n).astype(jnp.bfloat16)


def project(field, matrix):
    return jnp.einsum("btc,cd->btd", field, matrix, preferred_element_type=jnp.float32)


def body(
    latents,
    noise_draw,
    timesteps,
    inlet_conv,
    time_first,
    time_first_bias,
    time_second,
    time_second_bias,
    conv_first,
    conv_second,
    proj_inner,
    query_weight,
    key_weight,
    value_weight,
    attn_out,
    proj_outer,
    outlet_conv,
    first_gain,
    second_gain,
    third_gain,
    final_gain,
    layer_gain,
):
    gathered = (
        lax.all_gather(conv_first, "batch", axis=1, tiled=True),
        lax.all_gather(conv_second, "batch", axis=1, tiled=True),
        lax.all_gather(proj_inner, "batch", axis=1, tiled=True),
        lax.all_gather(query_weight, "batch", axis=1, tiled=True),
        lax.all_gather(key_weight, "batch", axis=1, tiled=True),
        lax.all_gather(value_weight, "batch", axis=1, tiled=True),
        lax.all_gather(attn_out, "batch", axis=1, tiled=True),
        lax.all_gather(proj_outer, "batch", axis=1, tiled=True),
    )
    conv_one, conv_two, inner_w, query_w, key_w, value_w, output_w, outer_w = gathered
    embedded = embed_sharded(timesteps, time_first, time_first_bias, time_second, time_second_bias)
    alpha_bar = lookup(timesteps)[:, None, None, None]
    noisy = (jnp.sqrt(alpha_bar) * latents + jnp.sqrt(1.0 - alpha_bar) * noise_draw).astype(
        jnp.bfloat16
    )
    opening = convolve(with_latent_rims(noisy), inlet_conv).astype(jnp.bfloat16)
    active = jax.nn.silu(group_norm(opening.astype(jnp.float32), first_gain, EPS_BLOCK)).astype(
        jnp.bfloat16
    )
    middle = (convolve(with_rims(active), conv_one) + embedded[:, None, None, :]).astype(
        jnp.bfloat16
    )
    active = jax.nn.silu(group_norm(middle.astype(jnp.float32), second_gain, EPS_BLOCK)).astype(
        jnp.bfloat16
    )
    block_one = (opening.astype(jnp.float32) + convolve(with_rims(active), conv_two)).astype(
        jnp.bfloat16
    )
    normed = group_norm(block_one.astype(jnp.float32), third_gain, EPS_GROUP).astype(jnp.bfloat16)
    view_n, height, breadth, chan_n = normed.shape
    flattened = normed.reshape(view_n, height * breadth, chan_n)
    projected = project(flattened, inner_w)
    tokens_in = layer_norm(projected, layer_gain).astype(jnp.bfloat16)
    queries = project(tokens_in, query_w).astype(jnp.bfloat16)
    key_rows = project(tokens_in, key_w).astype(jnp.bfloat16)
    value_rows = project(tokens_in, value_w).astype(jnp.bfloat16)
    attended = keys_everywhere(queries, key_rows, value_rows)
    mixture = (project(attended, output_w) + projected).astype(jnp.bfloat16)
    outer = project(mixture, outer_w).reshape(view_n, height, breadth, chan_n)
    block_two = (block_one.astype(jnp.float32) + outer).astype(jnp.bfloat16)
    active = jax.nn.silu(group_norm(block_two.astype(jnp.float32), final_gain, EPS_BLOCK)).astype(
        jnp.bfloat16
    )
    predicted = convolve(with_rims(active), outlet_conv)
    return (1.0 - alpha_bar) * (predicted - noise_draw)


def solution(mesh):
    in_specs = (
        P("batch", "space", None, None),
        P("batch", "space", None, None),
        P("batch"),
        P(),
        P(None, "batch"),
        P(),
        P(None, "batch"),
        P(),
        P(None, "batch"),
        P(None, "batch"),
        P(None, "batch"),
        P(None, "batch"),
        P(None, "batch"),
        P(None, "batch"),
        P(None, "batch"),
        P(None, "batch"),
        P(),
        P(),
        P(),
        P(),
        P(),
        P(),
    )
    out_specs = P("batch", "space", None, None)
    return jax.shard_map(body, mesh=mesh, in_specs=in_specs, out_specs=out_specs, check_vma=False)
```

profile of v0, /device:TPU:0, one launch (start us, length us, event | category | flops | bytes accessed | tf_op | source)
XLA Modules:
  0.0 384.6 jit_solution(9081348142568697016)
XLA Ops:
  11.3 4.9 %collective-permute-start = (bf16[1,1,64,4]{2,3,1,0:T(4,128)(2,1)S(1)}, bf16[1,1,64,4]{2,3,1,0:T(4,128)(2,1)S(1)}, u32[]{:S(2)}, u32[]{:S(2)}) collective-permute-start(bf16[1,1,64,4]{2,3,1,0:T(4,128)(2,1)S(1)} %get-tuple-element.43), channel_id=1, source_target_pairs={{0,1},{2,3},{4,5},{6,7},{8,9},{10,11},{12,13},{14,15},{16,17},{18,... | collective-permute-start | bytes 1544 | tf_op jit(solution)/shard_map/ppermute | solution.py:27
  19.5 12.3 %all-reduce.5 = s32[16]{0:T(128)S(1)} all-reduce(s32[16]{0:T(128)S(1)} %dynamic-update-slice), channel_id=1, replica_groups=mesh['batch'=16,'space'=2] {'batch'}, use_global_device_ids=true, to_apply=%add.5 | all-reduce | flops 16 | bytes 128
  33.0 18.3 %all-gather.3 = bf16[16,80,16]{1,2,0:T(8,128)(2,1)S(1)} all-gather(bf16[1,80,16]{1,2,0:T(8,128)(2,1)S(1)} %fusion.146), channel_id=1, replica_groups=mesh['batch'=16,'space'=2] {'batch'}, dimensions={0}, use_global_device_ids=true | all-gather | bytes 43520 | tf_op jit(solution)/shard_map/all_gather | solution.py:63
  53.8 3.5 all-to-all-start
  59.2 22.5 %all-gather.5 = bf16[16,20,320]{2,1,0:T(8,128)(2,1)S(1)} all-gather(bf16[1,20,320]{2,1,0:T(8,128)(2,1)S(1)} %bitcast.386), channel_id=1, replica_groups=mesh['batch'=16,'space'=2] {'batch'}, dimensions={0}, use_global_device_ids=true | all-gather | bytes 217600 | tf_op jit(solution)/shard_map/all_gather | solution.py:186
  86.4 5.9 %all-reduce.9 = (f32[1,32]{1,0:T(1,128)S(1)}, f32[1,32]{1,0:T(1,128)S(1)}) all-reduce(f32[1,32]{1,0:T(1,128)S(1)} %bitcast.397, f32[1,32]{1,0:T(1,128)S(1)} %bitcast.395), channel_id=1, replica_groups=mesh['batch'=16,'space'=2] {'space'}, use_global_device_ids=true, to_apply=%region_8.9 | all-reduce | flops 64 | bytes 512 | tf_op jit(solution)/shard_map/psum | solution.py:102
  93.2 3.9 %collective-permute-start.2 = (bf16[1,1,64,320]{3,2,1,0:T(8,128)(2,1)S(1)}, bf16[1,1,64,320]{3,2,1,0:T(8,128)(2,1)S(1)}, u32[]{:S(2)}, u32[]{:S(2)}) collective-permute-start(bf16[1,1,64,320]{3,2,1,0:T(8,128)(2,1)S(1)} %get-tuple-element.40), channel_id=1, source_target_pairs={{0,1},{2,3},{4,5},{6,7},{8,9},{10,11},{12,13},{14,15},{16,17},{18,... | collective-permute-start | bytes 122888 | tf_op jit(solution)/shard_map/ppermute | solution.py:27
  98.5 18.6 %all-gather.7 = bf16[16,20,320]{2,1,0:T(8,128)(2,1)S(1)} all-gather(bf16[1,20,320]{2,1,0:T(8,128)(2,1)S(1)} %bitcast.387), channel_id=1, replica_groups=mesh['batch'=16,'space'=2] {'batch'}, dimensions={0}, use_global_device_ids=true | all-gather | bytes 217600 | tf_op jit(solution)/shard_map/all_gather | solution.py:188
  119.7 4.0 %reshape.775 = bf16[320,2880]{1,0:T(8,128)(2,1)} reshape(bf16[16,20,2880]{2,1,0:T(8,128)(2,1)} %all-gather.20.cloned.1.call-done) | data formatting | bytes 3686400
  123.7 4.0 %copy.38 = bf16[320,2880]{0,1:T(8,128)(2,1)} copy(bf16[320,2880]{1,0:T(8,128)(2,1)} %reshape.775) | data formatting | bytes 3686400
  135.7 5.4 %all-reduce.8 = (f32[1,32]{1,0:T(1,128)S(1)}, f32[1,32]{1,0:T(1,128)S(1)}) all-reduce(f32[1,32]{1,0:T(1,128)S(1)} %bitcast.398, f32[1,32]{1,0:T(1,128)S(1)} %bitcast.393), channel_id=1, replica_groups=mesh['batch'=16,'space'=2] {'space'}, use_global_device_ids=true, to_apply=%region_14.15 | all-reduce | flops 64 | bytes 512 | tf_op jit(solution)/shard_map/psum | solution.py:102
  142.0 3.9 %collective-permute-start.4 = (bf16[1,1,64,320]{3,2,1,0:T(8,128)(2,1)S(1)}, bf16[1,1,64,320]{3,2,1,0:T(8,128)(2,1)S(1)}, u32[]{:S(2)}, u32[]{:S(2)}) collective-permute-start(bf16[1,1,64,320]{3,2,1,0:T(8,128)(2,1)S(1)} %get-tuple-element.38), channel_id=1, source_target_pairs={{0,1},{2,3},{4,5},{6,7},{8,9},{10,11},{12,13},{14,15},{16,17},{18,... | collective-permute-start | bytes 122888 | tf_op jit(solution)/shard_map/ppermute | solution.py:27
  145.9 4.0 %reshape.779 = bf16[320,2880]{1,0:T(8,128)(2,1)} reshape(bf16[16,20,2880]{2,1,0:T(8,128)(2,1)} %all-gather.22.cloned.1.call-done) | data formatting | bytes 3686400
  149.9 4.0 %copy.41 = bf16[320,2880]{0,1:T(8,128)(2,1)} copy(bf16[320,2880]{1,0:T(8,128)(2,1)} %reshape.779) | data formatting | bytes 3686400
  157.2 2.7 collective-permute-done.5
  166.4 4.9 %all-reduce.7 = (f32[1,32]{1,0:T(1,128)S(1)}, f32[1,32]{1,0:T(1,128)S(1)}) all-reduce(f32[1,32]{1,0:T(1,128)S(1)} %bitcast.399, f32[1,32]{1,0:T(1,128)S(1)} %bitcast.394), channel_id=1, replica_groups=mesh['batch'=16,'space'=2] {'space'}, use_global_device_ids=true, to_apply=%region_20.21 | all-reduce | flops 64 | bytes 512 | tf_op jit(solution)/shard_map/psum | solution.py:102
  174.4 20.0 %all-gather.6 = bf16[16,20,320]{2,1,0:T(8,128)(2,1)S(1)} all-gather(bf16[1,20,320]{2,1,0:T(8,128)(2,1)S(1)} %bitcast.388), channel_id=1, replica_groups=mesh['batch'=16,'space'=2] {'batch'}, dimensions={0}, use_global_device_ids=true | all-gather | bytes 217600 | tf_op jit(solution)/shard_map/all_gather | solution.py:187
  194.5 18.2 %all-gather.8 = bf16[16,20,320]{2,1,0:T(8,128)(2,1)S(1)} all-gather(bf16[1,20,320]{2,1,0:T(8,128)(2,1)S(1)} %bitcast.389), channel_id=1, replica_groups=mesh['batch'=16,'space'=2] {'batch'}, dimensions={0}, use_global_device_ids=true | all-gather | bytes 217600 | tf_op jit(solution)/shard_map/all_gather | solution.py:189
  212.9 19.6 %all-gather.9 = bf16[16,20,320]{2,1,0:T(8,128)(2,1)S(1)} all-gather(bf16[1,20,320]{2,1,0:T(8,128)(2,1)S(1)} %bitcast.390), channel_id=1, replica_groups=mesh['batch'=16,'space'=2] {'batch'}, dimensions={0}, use_global_device_ids=true | all-gather | bytes 217600 | tf_op jit(solution)/shard_map/all_gather | solution.py:190
  233.3 18.4 %all-gather.10 = bf16[16,20,320]{2,1,0:T(8,128)(2,1)S(1)} all-gather(bf16[1,20,320]{2,1,0:T(8,128)(2,1)S(1)} %bitcast.391), channel_id=1, replica_groups=mesh['batch'=16,'space'=2] {'batch'}, dimensions={0}, use_global_device_ids=true | all-gather | bytes 217600 | tf_op jit(solution)/shard_map/all_gather | solution.py:191
  255.7 8.3 %multiply_reduce_fusion.2 = (f32[8,1024]{1,0:T(8,128)S(1)}, f32[8,1024,512]{1,2,0:T(8,128)}) fusion(bf16[1024,8,40]{0,2,1:T(8,128)(2,1)S(1)} %bitcast.350, bf16[512,8,40]{0,2,1:T(8,128)(2,1)S(1)} %bitcast.381), kind=kOutput, calls=%fused_computation.6 | convolution fusion | flops 343924736 | bytes 17793024 | tf_op jit(solution)/shard_map/bqhd,bkhd->bhqk/dot_general | solution.py:136
  264.1 8.1 %multiply_reduce_fusion.3 = (f32[8,1024]{1,0:T(8,128)S(1)}, f32[8,1024,512]{1,2,0:T(8,128)}) fusion(bf16[1024,8,40]{0,2,1:T(8,128)(2,1)S(1)} %bitcast.351, bf16[512,8,40]{0,2,1:T(8,128)(2,1)S(1)} %bitcast.380), kind=kOutput, calls=%fused_computation.7 | convolution fusion | flops 343924736 | bytes 17793024 | tf_op jit(solution)/shard_map/bqhd,bkhd->bhqk/dot_general | solution.py:136
  272.2 8.1 %multiply_reduce_fusion.1 = (f32[8,1024]{1,0:T(8,128)S(1)}, f32[8,1024,512]{1,2,0:T(8,128)}) fusion(bf16[1024,8,40]{0,2,1:T(8,128)(2,1)S(1)} %bitcast.352, bf16[512,8,40]{0,2,1:T(8,128)(2,1)S(1)} %bitcast.378), kind=kOutput, calls=%fused_computation.5 | convolution fusion | flops 343924736 | bytes 17793024 | tf_op jit(solution)/shard_map/bqhd,bkhd->bhqk/dot_general | solution.py:136
  280.3 8.1 %multiply_reduce_fusion = (f32[8,1024]{1,0:T(8,128)S(1)}, f32[8,1024,512]{1,2,0:T(8,128)}) fusion(bf16[1024,8,40]{0,2,1:T(8,128)(2,1)S(1)} %bitcast.353, bf16[512,8,40]{0,2,1:T(8,128)(2,1)S(1)} %bitcast.377), kind=kOutput, calls=%fused_computation.4 | convolution fusion | flops 343924736 | bytes 17793024 | tf_op jit(solution)/shard_map/bqhd,bkhd->bhqk/dot_general | solution.py:136
  290.6 7.5 %fusion.12 = f32[8,1024,40]{1,2,0:T(8,128)S(1)} fusion(bf16[512,8,40]{0,2,1:T(8,128)(2,1)} %bitcast.379, f32[8,1024,512]{1,2,0:T(8,128)} %get-tuple-element.67, f32[8,1024]{1,0:T(8,128)S(1)} %get-tuple-element.27), kind=kOutput, calls=%fused_computation.18 | convolution fusion | flops 348127232 | bytes 18448384 | tf_op jit(solution)/shard_map/bhqk,bkhd->bhqd/dot_general | solution.py:143
  298.1 12.4 %fusion.2 = (f32[8,1024]{1,0:T(8,128)S(1)}, f32[8,1024]{1,0:T(8,128)S(1)}) fusion(f32[8,1024,512]{1,2,0:T(8,128)} %get-tuple-element.67, f32[8,1024]{1,0:T(8,128)S(1)} %get-tuple-element.27, f32[8,1024]{1,0:T(8,128)S(1)} %get-tuple-element.26, f32[8,1024,512]{1,2,0:T(8,128)} %get-tuple-element.63), kind=kLoop, calls=%fused_computation.10 | loop fusion | flops 25149440 | bytes 33685504 | tf_op jit(solution)/shard_map/reduce_sum | solution.py:142
  310.6 8.3 %fusion.10 = f32[8,1024,40]{1,2,0:T(8,128)} fusion(bf16[512,8,40]{0,2,1:T(8,128)(2,1)S(1)} %bitcast.376, f32[8,1024,512]{1,2,0:T(8,128)} %get-tuple-element.63, f32[8,1024]{1,0:T(8,128)S(1)} %get-tuple-element.26), kind=kOutput, calls=%fused_computation.17 | convolution fusion | flops 348127232 | bytes 18448384 | tf_op jit(solution)/shard_map/bhqk,bkhd->bhqd/dot_general | solution.py:143
  318.9 12.4 %fusion = (f32[8,1024]{1,0:T(8,128)S(1)}, f32[8,1024]{1,0:T(8,128)S(1)}) fusion(f32[8,1024,512]{1,2,0:T(8,128)} %get-tuple-element.65, f32[8,1024]{1,0:T(8,128)S(1)} %get-tuple-element.64, f32[8,1024]{1,0:T(8,128)S(1)} %get-tuple-element.25, f32[8,1024,512]{1,2,0:T(8,128)} %get-tuple-element.61), kind=kLoop, calls=%fused_computation.8 | loop fusion | flops 25149440 | bytes 33685504 | tf_op jit(solution)/shard_map/reduce_sum | solution.py:142
  331.3 8.3 %fusion.8 = f32[8,1024,40]{1,2,0:T(8,128)} fusion(bf16[512,8,40]{0,2,1:T(8,128)(2,1)S(1)} %bitcast.375, f32[8,1024,512]{1,2,0:T(8,128)} %get-tuple-element.61, f32[8,1024]{1,0:T(8,128)S(1)} %get-tuple-element.25), kind=kOutput, calls=%fused_computation.16 | convolution fusion | flops 348127232 | bytes 18448384 | tf_op jit(solution)/shard_map/bhqk,bkhd->bhqd/dot_general | solution.py:143
  339.6 10.6 %divide_convert_fusion = bf16[8,1024,40]{1,2,0:T(8,128)(2,1)} fusion(f32[8,1024,40]{1,2,0:T(8,128)} %fusion.8, f32[8,1024,40]{1,2,0:T(8,128)} %fusion.10, f32[8,1024,40]{1,2,0:T(8,128)S(1)} %fusion.12, bf16[512,8,40]{0,2,1:T(8,128)(2,1)} %bitcast.383, f32[8,1024,512]{1,2,0:T(8,128)} %get-tuple-element.65, f32[8,1024]{1,0:T(8,128)S(1)} %get-tuple-element.64, ...), kind=kOutput, calls=%fused_computation.82 | convolution fusion | flops 351076352 | bytes 21889024 | tf_op jit(solution)/shard_map/bhqk,bkhd->bhqd/dot_general | solution.py:143
  357.5 5.4 %all-reduce.6 = (f32[1,32]{1,0:T(1,128)S(1)}, f32[1,32]{1,0:T(1,128)S(1)}) all-reduce(f32[1,32]{1,0:T(1,128)S(1)} %bitcast.396, f32[1,32]{1,0:T(1,128)S(1)} %bitcast.392), channel_id=1, replica_groups=mesh['batch'=16,'space'=2] {'space'}, use_global_device_ids=true, to_apply=%region_36.37 | all-reduce | flops 64 | bytes 512 | tf_op jit(solution)/shard_map/psum | solution.py:102
  367.7 4.3 %collective-permute-done.7 = bf16[1,1,64,320]{3,2,1,0:T(8,128)(2,1)S(1)} collective-permute-done((bf16[1,1,64,320]{3,2,1,0:T(8,128)(2,1)S(1)}, bf16[1,1,64,320]{3,2,1,0:T(8,128)(2,1)S(1)}, u32[]{:S(2)}, u32[]{:S(2)}) %collective-permute-start.7) | collective-permute-done | bytes 40992 | tf_op jit(solution)/shard_map/ppermute | solution.py:29
  (199 shorter events, 67.7 us)
Async XLA Ops:
  6.5 26.3 %copy-start = (bf16[320,80]{0,1:T(8,128)(2,1)S(1)}, bf16[320,80]{0,1:T(8,128)(2,1)}, u32[]{:S(2)}) copy-start(bf16[320,80]{0,1:T(8,128)(2,1)} %param.26) | copy-start | bytes 153604
  6.5 75.3 %copy-start.9 = (bf16[36,320]{1,0:T(8,128)(2,1)S(1)}, bf16[36,320]{1,0:T(8,128)(2,1)}, u32[]{:S(2)}) copy-start(bf16[36,320]{1,0:T(8,128)(2,1)} %param.25) | copy-start | bytes 69124
  6.5 52.6 %copy-start.11 = (bf16[320,20]{0,1:T(8,128)(2,1)S(1)}, bf16[320,20]{0,1:T(8,128)(2,1)}, u32[]{:S(2)}) copy-start(bf16[320,20]{0,1:T(8,128)(2,1)} %param.32) | copy-start | bytes 38404
  6.5 113.2 %all-gather.20.cloned.1.call-start = ((), (), s32[]{:S(2)}) async-start(), calls=%async_computation.3 | async-start | bytes 2402304 | tf_op jit(solution)/shard_map/all_gather | solution.py:184
  11.3 70.4 %collective-permute-start = (bf16[1,1,64,4]{2,3,1,0:T(4,128)(2,1)S(1)}, bf16[1,1,64,4]{2,3,1,0:T(4,128)(2,1)S(1)}, u32[]{:S(2)}, u32[]{:S(2)}) collective-permute-start(bf16[1,1,64,4]{2,3,1,0:T(4,128)(2,1)S(1)} %get-tuple-element.43), channel_id=1, source_target_pairs={{0,1},{2,3},{4,5},{6,7},{8,9},{10,11},{12,13},{14,15},{16,17},{18,... | collective-permute-start | bytes 1544 | tf_op jit(solution)/shard_map/ppermute | solution.py:27
  18.2 63.5 %collective-permute-start.1 = (bf16[1,1,64,4]{2,3,1,0:T(4,128)(2,1)S(1)}, bf16[1,1,64,4]{2,3,1,0:T(4,128)(2,1)S(1)}, u32[]{:S(2)}, u32[]{:S(2)}) collective-permute-start(bf16[1,1,64,4]{2,3,1,0:T(4,128)(2,1)S(1)} %get-tuple-element.44), channel_id=1, source_target_pairs={{1,0},{3,2},{5,4},{7,6},{9,8},{11,10},{13,12},{15,14},{17,16},{19,... | collective-permute-start | bytes 1544 | tf_op jit(solution)/shard_map/ppermute | solution.py:29
  53.8 64.2 %all-to-all-start = ((f32[16,1,20]{2,1,0:T(1,128)}), f32[16,1,20]{2,1,0:T(1,128)S(1)}, u32[]{:S(2)}, u32[]{:S(2)}) async-start(f32[16,1,20]{2,1,0:T(1,128)} %bitcast.50), calls=%async_computation | async-start | bytes 16384 | tf_op jit(solution)/shard_map/all_to_all | solution.py:66
  57.3 88.7 %all-gather.22.cloned.1.call-start = ((), (), s32[]{:S(2)}) async-start(), calls=%async_computation.4 | async-start | bytes 2402304 | tf_op jit(solution)/shard_map/all_gather | solution.py:185
  58.0 196.3 %all-gather.16.cloned.1.call-start = ((), (), s32[]{:S(2)}) async-start(), calls=%async_computation.1 | async-start | bytes 1966080 | tf_op jit(solution)/shard_map/all_gather | solution.py:125
  85.1 7.6 %copy-start.17 = (f32[320]{0:T(512)S(1)}, f32[320]{0:T(512)}, u32[]{:S(2)}) copy-start(f32[320]{0:T(512)} %param.39) | copy-start | bytes 3844
  86.0 12.5 %copy-start.12 = (bf16[320,20]{0,1:T(8,128)(2,1)S(1)}, bf16[320,20]{0,1:T(8,128)(2,1)}, u32[]{:S(2)}) copy-start(bf16[320,20]{0,1:T(8,128)(2,1)} %param.34) | copy-start | bytes 38404
  93.2 26.1 %collective-permute-start.2 = (bf16[1,1,64,320]{3,2,1,0:T(8,128)(2,1)S(1)}, bf16[1,1,64,320]{3,2,1,0:T(8,128)(2,1)S(1)}, u32[]{:S(2)}, u32[]{:S(2)}) collective-permute-start(bf16[1,1,64,320]{3,2,1,0:T(8,128)(2,1)S(1)} %get-tuple-element.40), channel_id=1, source_target_pairs={{0,1},{2,3},{4,5},{6,7},{8,9},{10,11},{12,13},{14,15},{16,17},{18,... | collective-permute-start | bytes 122888 | tf_op jit(solution)/shard_map/ppermute | solution.py:27
  97.2 22.1 %collective-permute-start.3 = (bf16[1,1,64,320]{3,2,1,0:T(8,128)(2,1)S(1)}, bf16[1,1,64,320]{3,2,1,0:T(8,128)(2,1)S(1)}, u32[]{:S(2)}, u32[]{:S(2)}) collective-permute-start(bf16[1,1,64,320]{3,2,1,0:T(8,128)(2,1)S(1)} %get-tuple-element.41), channel_id=1, source_target_pairs={{1,0},{3,2},{5,4},{7,6},{9,8},{11,10},{13,12},{15,14},{17,16},{19,... | collective-permute-start | bytes 122888 | tf_op jit(solution)/shard_map/ppermute | solution.py:29
  134.0 7.5 %copy-start.18 = (f32[320]{0:T(512)S(1)}, f32[320]{0:T(512)}, u32[]{:S(2)}) copy-start(f32[320]{0:T(512)} %param.40) | copy-start | bytes 3844
  142.0 15.2 %collective-permute-start.4 = (bf16[1,1,64,320]{3,2,1,0:T(8,128)(2,1)S(1)}, bf16[1,1,64,320]{3,2,1,0:T(8,128)(2,1)S(1)}, u32[]{:S(2)}, u32[]{:S(2)}) collective-permute-start(bf16[1,1,64,320]{3,2,1,0:T(8,128)(2,1)S(1)} %get-tuple-element.38), channel_id=1, source_target_pairs={{0,1},{2,3},{4,5},{6,7},{8,9},{10,11},{12,13},{14,15},{16,17},{18,... | collective-permute-start | bytes 122888 | tf_op jit(solution)/shard_map/ppermute | solution.py:27
  153.9 6.0 %collective-permute-start.5 = (bf16[1,1,64,320]{3,2,1,0:T(8,128)(2,1)S(1)}, bf16[1,1,64,320]{3,2,1,0:T(8,128)(2,1)S(1)}, u32[]{:S(2)}, u32[]{:S(2)}) collective-permute-start(bf16[1,1,64,320]{3,2,1,0:T(8,128)(2,1)S(1)} %get-tuple-element.39), channel_id=1, source_target_pairs={{1,0},{3,2},{5,4},{7,6},{9,8},{11,10},{13,12},{15,14},{17,16},{19,... | collective-permute-start | bytes 122888 | tf_op jit(solution)/shard_map/ppermute | solution.py:29
  155.4 4.9 %copy-start.4 = (bf16[320,2880]{0,1:T(8,128)(2,1)S(1)}, bf16[320,2880]{0,1:T(8,128)(2,1)}, u32[]{:S(2)}) copy-start(bf16[320,2880]{0,1:T(8,128)(2,1)} %copy.41) | copy-start | bytes 5529604
  164.7 7.0 %copy-start.21 = (f32[320]{0:T(512)S(1)}, f32[320]{0:T(512)}, u32[]{:S(2)}) copy-start(f32[320]{0:T(512)} %param.41) | copy-start | bytes 3844
  166.0 5.8 %copy-start.2 = (f32[16,64,320]{2,1,0:T(8,128)}, f32[16,64,320]{2,1,0:T(8,128)S(1)}, u32[]{:S(2)}) copy-start(f32[16,64,320]{2,1,0:T(8,128)S(1)} %get-tuple-element.57) | copy-start | bytes 3932164
  166.0 6.0 %copy-start.6 = (bf16[320,320]{1,0:T(8,128)(2,1)S(1)}, bf16[320,320]{1,0:T(8,128)(2,1)}, u32[]{:S(2)}) copy-start(bf16[320,320]{1,0:T(8,128)(2,1)} %reshape.781) | copy-start | bytes 614404
  172.9 21.6 %copy-start.14 = (bf16[320,20]{0,1:T(8,128)(2,1)S(1)}, bf16[320,20]{0,1:T(8,128)(2,1)}, u32[]{:S(2)}) copy-start(bf16[320,20]{0,1:T(8,128)(2,1)} %param.35) | copy-start | bytes 38404
  174.3 38.6 %copy-start.15 = (bf16[320,20]{0,1:T(8,128)(2,1)S(1)}, bf16[320,20]{0,1:T(8,128)(2,1)}, u32[]{:S(2)}) copy-start(bf16[320,20]{0,1:T(8,128)(2,1)} %param.36) | copy-start | bytes 38404
  174.3 59.0 %copy-start.16 = (bf16[320,20]{0,1:T(8,128)(2,1)S(1)}, bf16[320,20]{0,1:T(8,128)(2,1)}, u32[]{:S(2)}) copy-start(bf16[320,20]{0,1:T(8,128)(2,1)} %param.37) | copy-start | bytes 38404
  174.3 114.0 %all-gather.18.cloned.1.call-start = ((), (), s32[]{:S(2)}) async-start(), calls=%async_computation.2 | async-start | bytes 1966080 | tf_op jit(solution)/shard_map/all_gather | solution.py:126
  339.6 10.6 %copy-start.8 = (bf16[320,320]{1,0:T(8,128)(2,1)S(1)}, bf16[320,320]{1,0:T(8,128)(2,1)}, u32[]{:S(2)}) copy-start(bf16[320,320]{1,0:T(8,128)(2,1)} %reshape.789) | copy-start | bytes 614404
  350.2 4.8 %copy-start.3 = (f32[16,64,320]{2,1,0:T(8,128)S(1)}, f32[16,64,320]{2,1,0:T(8,128)}, u32[]{:S(2)}) copy-start(f32[16,64,320]{2,1,0:T(8,128)} %copy-done.2) | copy-start | bytes 3932164
  350.2 4.8 %copy-start.7 = (bf16[320,320,1]{1,0,2:T(8,128)(2,1)S(1)}, bf16[320,320,1]{1,0,2:T(8,128)(2,1)}, u32[]{:S(2)}) copy-start(bf16[320,320,1]{1,0,2:T(8,128)(2,1)} %reshape.821) | copy-start | bytes 614404
  355.1 8.2 %copy-start.20 = (f32[320]{0:T(512)S(1)}, f32[320]{0:T(512)}, u32[]{:S(2)}) copy-start(f32[320]{0:T(512)} %param.42) | copy-start | bytes 3844
  363.2 9.2 %copy-start.22 = (bf16[2880,4]{0,1:T(4,128)(2,1)S(1)}, bf16[2880,4]{0,1:T(4,128)(2,1)}, u32[]{:S(2)}) copy-start(bf16[2880,4]{0,1:T(4,128)(2,1)} %param.38) | copy-start | bytes 69124
  363.8 3.9 %collective-permute-start.6 = (bf16[1,1,64,320]{3,2,1,0:T(8,128)(2,1)S(1)}, bf16[1,1,64,320]{3,2,1,0:T(8,128)(2,1)S(1)}, u32[]{:S(2)}, u32[]{:S(2)}) collective-permute-start(bf16[1,1,64,320]{3,2,1,0:T(8,128)(2,1)S(1)} %get-tuple-element.36), channel_id=1, source_target_pairs={{0,1},{2,3},{4,5},{6,7},{8,9},{10,11},{12,13},{14,15},{16,17},{18,... | collective-permute-start | bytes 122888 | tf_op jit(solution)/shard_map/ppermute | solution.py:27
  366.0 6.0 %collective-permute-start.7 = (bf16[1,1,64,320]{3,2,1,0:T(8,128)(2,1)S(1)}, bf16[1,1,64,320]{3,2,1,0:T(8,128)(2,1)S(1)}, u32[]{:S(2)}, u32[]{:S(2)}) collective-permute-start(bf16[1,1,64,320]{3,2,1,0:T(8,128)(2,1)S(1)} %get-tuple-element.37), channel_id=1, source_target_pairs={{1,0},{3,2},{5,4},{7,6},{9,8},{11,10},{13,12},{15,14},{17,16},{19,... | collective-permute-start | bytes 122888 | tf_op jit(solution)/shard_map/ppermute | solution.py:29
  375.7 2.2 copy-start.1
  (4 other events, 5.0 us)
Sparse Core Ops, SparseCore 0:
  9.5 44.8 all-gather.19
  60.2 44.6 all-gather.21
  174.5 22.1 all-gather.15
  254.5 21.6 all-gather.17
where the time goes:
time: 391 us; the launch traced here: 385 us
  blocking collectives  170 us (43%)
  matrix products  103 us (26%)
  other arithmetic  32 us (8%)
  local copies, waits for them, and re-layouts  31.3 us (8%)
  starting transfers between devices  23.9 us (6%)
  between operations  16 us (4%)
  waiting for transfers between devices  8.87 us (2%)
    dot_general x4, matrix products, keys_everywhere(): jnp.einsum('bhqk,bkhd->bhqd', weights.astype(jnp.bfloat16), value_blk, pr...  34.7 us
    dot_general x4, matrix products, keys_everywhere(): jnp.einsum('bqhd,bkhd->bhqk', query_heads, key_blk, preferred_element_typ...  32.6 us
    dot_general x36, matrix products, convolve(): jnp.einsum('bhwc,cd->bhwd', window, kernel[offset * width_in:(offset + 1)...  25.6 us
    reduce_sum x2, other arithmetic, keys_everywhere(): row_sum = row_sum * shrink + jnp.sum(weights, axis=-1)  24.8 us
    all_gather x1, blocking collectives, body(): lax.all_gather(proj_inner, 'batch', axis=1, tiled=True)  22.5 us
    psum x4, blocking collectives, group_norm(): sums_all, squares_all = lax.psum((sums_local, squares_local), 'space')  21.6 us
    unnamed x60, local copies, waits for them, and re-layouts  20.8 us
    all_gather x1, blocking collectives, body(): lax.all_gather(query_weight, 'batch', axis=1, tiled=True)  20 us
  transfers between devices with their start and end apart: 13, of which 3 were waited for; matrix products, arithmetic and copies ran while one was open for 21% of the time, Pallas kernels for 0%

commit v1 on v0

v1 whole, which is shorter than its diff:
```python
import math

import jax
import jax.numpy as jnp
from jax import lax
from jax.experimental import pallas as pl
from jax.experimental.pallas import tpu as pltpu
from jax.sharding import PartitionSpec as P

HEADS = 8
HEAD_SIZE = 40
GROUPS = 32
STEPS = 1000
EPS_GROUP = 1e-06
EPS_BLOCK = 1e-05
EPS_LAYER = 1e-05
VMEM_BYTES = 60 << 20
RING_LIMIT = 16
F32 = jnp.float32
BF16 = jnp.bfloat16


def plan():
    fraction = jnp.arange(STEPS, dtype=F32) / (STEPS - 1)
    beta_root = math.sqrt(0.00085) + fraction * (math.sqrt(0.012) - math.sqrt(0.00085))
    return jnp.cumprod(1.0 - beta_root * beta_root)


def lookup(timesteps):
    matches = jnp.arange(STEPS, dtype=jnp.int32)[None, :] == timesteps[:, None]
    return jnp.sum(jnp.where(matches, plan()[None, :], 0.0), axis=1)


def waveform_of(timesteps, halfway):
    frequency = jnp.exp(-math.log(10000.0) * jnp.arange(halfway, dtype=F32) / halfway)
    angles = timesteps.astype(F32)[:, None] * frequency[None, :]
    return jnp.concatenate([jnp.cos(angles), jnp.sin(angles)], axis=1).astype(BF16)


def batch_ring(count):
    side = count // 4
    ring = 2 * side

    def group(spot):
        spot = spot % ring
        deep, wide = (spot, 0) if spot < side else (ring - 1 - spot, 1)
        return 2 * deep + wide

    onward = []
    for spot in range(ring):
        onward.append((2 * group(spot), 2 * group(spot + 1)))
        onward.append((2 * group(spot) + 1, 2 * group(spot - 1) + 1))
    sibling = [(place, place ^ 1) for place in range(count)]
    half = ring // 2
    spot_of = [0] * (count // 2)
    for spot in range(ring):
        spot_of[group(spot)] = spot
    table = []
    for place in range(count):
        core, spot = place % 2, spot_of[place // 2]
        row = [place, place ^ 1]
        step = -1 if core == 0 else 1
        for far in range(1, half):
            mine = group(spot + step * far)
            row += [2 * mine + core, 2 * mine + (core ^ 1)]
            theirs = group(spot - step * far)
            row += [2 * theirs + (core ^ 1), 2 * theirs + core]
        far_one = group(spot + step * half)
        row += [2 * far_one + core, 2 * far_one + (core ^ 1)]
        table.append(row)
    return onward, sibling, half, table


def gather_shards(shards, beside):
    count = lax.axis_size("batch")
    if count % 4 or count > RING_LIMIT:
        whole = [[lax.all_gather(shard, "batch", axis=0, tiled=True)] for shard in shards]
        return whole, jnp.arange(count, dtype=jnp.int32), beside()
    onward, sibling, half, table = batch_ring(count)
    rows = shards[0].shape[0]
    others = [lax.ppermute(shard, "batch", sibling) for shard in shards]
    moving = [pair_up(shard, other) for shard, other in zip(shards, others)]
    gathered = [[pair] for pair in moving]
    extra = None
    for step in range(1, half):
        moving = [lax.ppermute(pair, "batch", onward) for pair in moving]
        if extra is None:
            extra = beside()
            moving, extra = lax.optimization_barrier((moving, extra))
        for pieces, pair in zip(gathered, moving):
            pieces += [pair, lax.ppermute(pair, "batch", sibling)]
    for pieces, pair in zip(gathered, moving):
        last = lax.ppermute(pair[:rows], "batch", onward)
        pieces += [last, lax.ppermute(last, "batch", sibling)]
    origin = jnp.asarray(table, dtype=jnp.int32)[lax.axis_index("batch")]
    return gathered, origin, extra


def lane_sums(value):
    total = value[:, :128]
    for start in range(128, value.shape[1], 128):
        total = total + value[:, start : start + 128]
    return total


def group_moments(sums, squares, number):
    chan_n = sums.shape[0]
    size = chan_n // GROUPS
    rows = lax.broadcasted_iota(jnp.int32, (chan_n, chan_n), 0) // size
    cols = lax.broadcasted_iota(jnp.int32, (chan_n, chan_n), 1) // size
    member = jnp.where(rows == cols, 1.0, 0.0).astype(F32)
    both = jnp.concatenate([sums, squares], axis=1)
    grouped = jnp.dot(member, both, preferred_element_type=F32, precision=lax.Precision.HIGHEST)
    mean = jnp.sum(grouped[:, :128], axis=1, keepdims=True) / number
    square = jnp.sum(grouped[:, 128:], axis=1, keepdims=True) / number
    return mean, square


def padded(rows):
    return -(-rows // 16) * 16


def assemble(origin_ref, pieces, stage, rows, out_ref):
    total, deep = out_ref.shape[0], stage.shape[0]
    rid = lax.broadcasted_iota(jnp.int32, (total, deep), 0)
    cid = lax.broadcasted_iota(jnp.int32, (total, deep), 1)
    want = jnp.full((total, deep), -1, jnp.int32)
    place = base = 0
    for ref in pieces:
        size = ref.shape[0]
        stage[base : base + size, :] = ref[...]
        if padded(size) > size:
            fill = jnp.zeros((padded(size) - size, stage.shape[1]), stage.dtype)
            stage[base + size : base + padded(size), :] = fill
        for sub in range(size // rows):
            first = base + sub * rows
            inside = (cid >= first) & (cid < first + rows)
            want = jnp.where(inside, origin_ref[place] * rows + cid - first, want)
            place += 1
        base += padded(size)
    pick = jnp.where(rid == want, 1.0, 0.0).astype(BF16)
    width = stage.shape[1]
    for start in range(0, width, 512):
        stop = min(width, start + 512)
        out_ref[:, start:stop] = jnp.dot(
            pick, stage[:, start:stop], preferred_element_type=F32
        ).astype(BF16)


def spread_taps(load, store, chan_n, token_n, breadth, chunk=16):
    def one(index, carry):
        base = pl.multiple_of(index * chunk, chunk)
        value = load(base, chunk)
        lane = lax.broadcasted_iota(jnp.int32, (chunk, token_n), 1)
        column = lane % breadth
        left = jnp.where(column == 0, 0.0, pltpu.roll(value, 1, 1))
        right = jnp.where(column == breadth - 1, 0.0, pltpu.roll(value, token_n - 1, 1))
        for col, variant in enumerate((left, value, right)):
            up = jnp.where(lane < breadth, 0.0, pltpu.roll(variant, breadth, 1))
            down = jnp.where(
                lane >= token_n - breadth, 0.0, pltpu.roll(variant, token_n - breadth, 1)
            )
            for row, shifted in enumerate((up, variant, down)):
                store((3 * row + col) * chan_n + base, chunk, shifted.astype(BF16))
        return carry

    lax.fori_loop(0, chan_n // chunk, one, 0)


def silu(value):
    return value / (1.0 + jnp.exp(-value))


def normal_taps(source_ref, taps_ref, mean_ref, factor_ref, breadth):
    chan_n, token_n = source_ref.shape

    def load(base, chunk):
        value = source_ref[pl.ds(base, chunk), :].astype(F32)
        mean = mean_ref[pl.ds(base, chunk), 0:1]
        factor = factor_ref[pl.ds(base, chunk), 0:1]
        return silu((value - mean) * factor)

    def store(base, chunk, value):
        taps_ref[pl.ds(pl.multiple_of(base, chunk), chunk), :] = value

    spread_taps(load, store, chan_n, token_n, breadth)


def set_moments(sums, squares, number, gain, epsilon, mean_ref, factor_ref):
    mean, square = group_moments(sums, squares, number)
    factor = lax.rsqrt(square - mean * mean + epsilon) * gain
    mean_ref[...] = jnp.broadcast_to(mean, mean_ref.shape)
    factor_ref[...] = jnp.broadcast_to(factor, factor_ref.shape)


def pair_kernel(one_ref, two_ref, out_ref):
    rows = one_ref.shape[0]
    out_ref[:rows] = one_ref[...]
    out_ref[rows:] = two_ref[...]


def pair_up(one, two):
    whole = jax.ShapeDtypeStruct((2 * one.shape[0], one.shape[1]), one.dtype)
    return kernel_call(pair_kernel, whole, [])(one, two)


def pack_kernel(conv_first, time_first, time_second, conv_second, *rest):
    squares, (one_ref, two_ref) = rest[:-2], rest[-2:]
    rows, conv_width = conv_first.shape
    chan_n = time_first.shape[1]
    one_ref[:, :conv_width] = conv_first[...]
    for index in range(time_first.shape[0] // rows):
        base = conv_width + index * chan_n
        one_ref[:, base : base + chan_n] = time_first[index * rows : (index + 1) * rows]
    one_ref[:, conv_width + time_second.shape[1] :] = time_second[...]
    two_ref[:, :conv_width] = conv_second[...]
    for index, square in enumerate(squares):
        base = conv_width + index * chan_n
        two_ref[:, base : base + chan_n] = square[...]


def opening_kernel(breadth, noisy_ref, kernel_ref, start_ref, sums_ref, squares_ref, flat, taps):
    height, lat_n, _ = noisy_ref.shape
    token_n = height * breadth
    flat[...] = jnp.zeros(flat.shape, F32)
    for row in range(height):
        flat[0:lat_n, row * breadth : (row + 1) * breadth] = noisy_ref[row].astype(F32)
    taps[...] = jnp.zeros(taps.shape, F32)
    value = flat[...]
    lane = lax.broadcasted_iota(jnp.int32, value.shape, 1)
    column = lane % breadth
    for offset in range(9):
        row_off, col_off = offset // 3 - 1, offset % 3 - 1
        shift = -(row_off * breadth + col_off) % token_n
        moved = pltpu.roll(value, shift, 1) if shift else value
        good = (column + col_off >= 0) & (column + col_off < breadth)
        good = good & (lane + row_off * breadth >= 0) & (lane + row_off * breadth < token_n)
        moved = jnp.where(good, moved, 0.0)
        taps[offset * lat_n : (offset + 1) * lat_n, :] = moved[0:lat_n]
    block_n = min(512, token_n)
    for start in range(0, token_n, block_n):
        part = jnp.dot(
            kernel_ref[...],
            taps[:, start : start + block_n].astype(BF16),
            preferred_element_type=F32,
        ).astype(BF16)
        start_ref[:, start : start + block_n] = part
        wide = part.astype(F32)
        if start == 0:
            sums_ref[...] = lane_sums(wide)
            squares_ref[...] = lane_sums(wide * wide)
        else:
            sums_ref[...] += lane_sums(wide)
            squares_ref[...] += lane_sums(wide * wide)


def first_kernel(
    counts,
    rows,
    breadth,
    origin_ref,
    start_ref,
    sums_ref,
    squares_ref,
    gains_ref,
    wave_ref,
    bias_ref,
    *rest,
):
    pieces = rest[:counts]
    middle_ref, sums_out, squares_out = rest[counts : counts + 3]
    stage, weights, taps, mean, factor, hidden = rest[counts + 3 :]
    chan_n, token_n = start_ref.shape
    number = token_n * (chan_n // GROUPS)
    assemble(origin_ref, pieces, stage, rows, weights)
    conv_width = 9 * chan_n
    temb_n = hidden.shape[0]
    many = temb_n // chan_n
    for index in range(many):
        first = weights[:, conv_width + index * chan_n : conv_width + (index + 1) * chan_n]
        inner = jnp.dot(first, wave_ref[...], preferred_element_type=F32)
        for place in range(chan_n // rows):
            base = place * many * rows + index * rows
            hidden[base : base + rows, :] = inner[place * rows : (place + 1) * rows]
    second = weights[:, conv_width + temb_n : conv_width + 2 * temb_n]
    lifted = silu(silu(hidden[...] + bias_ref[...].T[:, 0:1])).astype(BF16)
    embedded = jnp.dot(second, lifted, preferred_element_type=F32)
    embedded = embedded[:, 0:1] + gains_ref[:, 5:6]
    set_moments(
        sums_ref[...], squares_ref[...], number, gains_ref[:, 0:1], EPS_BLOCK, mean, factor
    )
    normal_taps(start_ref, taps, mean, factor, breadth)
    block_n = min(512, token_n)
    for start in range(0, token_n, block_n):
        part = jnp.dot(
            weights[:, :conv_width], taps[:, start : start + block_n], preferred_element_type=F32
        )
        part = (part + embedded).astype(BF16)
        middle_ref[:, start : start + block_n] = part
        wide = part.astype(F32)
        if start == 0:
            sums_out[...] = lane_sums(wide)
            squares_out[...] = lane_sums(wide * wide)
        else:
            sums_out[...] += lane_sums(wide)
            squares_out[...] += lane_sums(wide * wide)


def second_kernel(
    counts,
    rows,
    breadth,
    origin_ref,
    space_ref,
    middle_ref,
    sums_ref,
    squares_ref,
    start_ref,
    gains_ref,
    *rest,
):
    pieces = rest[:counts]
    block_out, projected_out, query_out, key_out, value_out, outer_out = rest[counts : counts + 6]
    stage, weights, taps, mean, factor, sums, squares, block, tokens = rest[counts + 6 :]
    chan_n, token_n = middle_ref.shape
    query_n = block_out.shape[1]
    number = token_n * (chan_n // GROUPS)
    assemble(origin_ref, pieces, stage, rows, weights)
    conv_width = 9 * chan_n

    def small(index):
        base = conv_width + index * chan_n
        return weights[:, base : base + chan_n]

    set_moments(
        sums_ref[...], squares_ref[...], number, gains_ref[:, 1:2], EPS_BLOCK, mean, factor
    )
    normal_taps(middle_ref, taps, mean, factor, breadth)
    block_n = min(512, token_n)
    for start in range(0, token_n, block_n):
        part = jnp.dot(
            weights[:, :conv_width], taps[:, start : start + block_n], preferred_element_type=F32
        )
        part = (part + start_ref[:, start : start + block_n].astype(F32)).astype(BF16)
        block[:, start : start + block_n] = part
        wide = part.astype(F32)
        if start == 0:
            sums[...] = lane_sums(wide)
            squares[...] = lane_sums(wide * wide)
        else:
            sums[...] += lane_sums(wide)
            squares[...] += lane_sums(wide * wide)
    set_moments(sums[...], squares[...], number, gains_ref[:, 2:3], EPS_GROUP, mean, factor)
    own = pl.multiple_of(space_ref[0] * query_n, 128)

    def project(source):
        normed = ((source.astype(F32) - mean[:, 0:1]) * factor[:, 0:1]).astype(BF16)
        return jnp.dot(small(0), normed, preferred_element_type=F32)

    for start in range(0, token_n, block_n):
        projected = project(block[:, start : start + block_n])
        average = jnp.mean(projected, axis=0, keepdims=True)
        centred = projected - average
        spread = jnp.mean(centred * centred, axis=0, keepdims=True)
        scaled = centred * lax.rsqrt(spread + EPS_LAYER) * gains_ref[:, 4:5]
        token = scaled.astype(BF16)
        tokens[:, start : start + block_n] = token
        value = jnp.dot(small(3), token, preferred_element_type=F32)
        ones = jnp.ones((8, block_n), F32)
        for head in range(HEADS):
            piece = value[head * HEAD_SIZE : (head + 1) * HEAD_SIZE]
            value_out[head, :, start : start + block_n] = jnp.concatenate(
                [piece, ones], axis=0
            ).astype(BF16)
        upright = scaled.T.astype(BF16)
        half = HEADS // 2 * HEAD_SIZE
        for part in range(2):
            matrix = weights[
                part * half : (part + 1) * half,
                conv_width + 2 * chan_n : conv_width + 3 * chan_n,
            ]
            key_out[part, start : start + block_n, :] = lax.dot_general(
                upright, matrix, (((1,), (1,)), ((), ())), preferred_element_type=F32
            ).astype(BF16)
    block_out[...] = block[:, pl.ds(own, query_n)]
    projected_out[...] = project(block[:, pl.ds(own, query_n)])
    query = jnp.dot(small(1), tokens[:, pl.ds(own, query_n)], preferred_element_type=F32)
    query = query * (math.log2(math.e) / math.sqrt(HEAD_SIZE))
    per_half = HEADS // 2
    for head in range(HEADS):
        spot = head % per_half
        piece = query[head * HEAD_SIZE : (head + 1) * HEAD_SIZE]
        parts = []
        if spot:
            parts.append(jnp.zeros((spot * HEAD_SIZE, query_n), F32))
        parts.append(piece)
        if spot < per_half - 1:
            parts.append(jnp.zeros(((per_half - 1 - spot) * HEAD_SIZE, query_n), F32))
        query_out[head] = jnp.concatenate(parts, axis=0).astype(BF16)
    outer_out[0] = small(4)
    outer_out[1] = small(5)


def exact_parts(value):
    high = value.astype(BF16)
    rest = value - high.astype(F32)
    middle = rest.astype(BF16)
    return [high, middle, (rest - middle.astype(F32)).astype(BF16)]


def attention_kernel(
    breadth,
    space_ref,
    query_ref,
    key_ref,
    value_ref,
    projected_ref,
    block_ref,
    outer_ref,
    block_two_ref,
    sums_ref,
    squares_ref,
    packed_ref,
    scores,
    weights,
    attended,
):
    heads, _, query_n = query_ref.shape
    token_n = key_ref.shape[1]
    width = scores.shape[1]
    per_half = heads // 2
    key_n = min(512, token_n)

    for head in range(heads):

        def one(step, carry):
            base = pl.multiple_of(step * width, 128)
            query = query_ref[head, :, pl.ds(base, width)]
            top = jnp.full((1, width), -jnp.inf, F32)
            for start in range(0, token_n, key_n):
                part = jnp.dot(
                    key_ref[head // per_half, start : start + key_n, :],
                    query,
                    preferred_element_type=F32,
                )
                scores[start : start + key_n, :] = part
                top = jnp.maximum(top, jnp.max(part, axis=0, keepdims=True))
            for start in range(0, token_n, key_n):
                weights[start : start + key_n, :] = jnp.exp2(
                    scores[start : start + key_n, :] - top
                ).astype(BF16)
            mixed = jnp.dot(value_ref[head], weights[...], preferred_element_type=F32)
            result = mixed[:HEAD_SIZE] / mixed[HEAD_SIZE : HEAD_SIZE + 1]
            attended[head * HEAD_SIZE : (head + 1) * HEAD_SIZE, pl.ds(base, width)] = result
            return carry

        lax.fori_loop(0, query_n // width, one, 0)
    mixture = jnp.dot(outer_ref[0], attended[...].astype(BF16), preferred_element_type=F32)
    mixture = (mixture + projected_ref[...]).astype(BF16)
    outer = jnp.dot(outer_ref[1], mixture, preferred_element_type=F32)
    block_two = (block_ref[...].astype(F32) + outer).astype(BF16)
    block_two_ref[...] = block_two
    wide = block_two.astype(F32)
    sums = lane_sums(wide)
    squares = lane_sums(wide * wide)
    sums_ref[...] = sums
    squares_ref[...] = squares
    edge = jnp.where(space_ref[0] == 0, wide[:, query_n - breadth :], wide[:, :breadth])
    columns = [edge.astype(BF16)]
    columns += exact_parts(jnp.sum(sums, axis=1, keepdims=True))
    columns += exact_parts(jnp.sum(squares, axis=1, keepdims=True))
    lane = lax.broadcasted_iota(jnp.int32, packed_ref.shape, 1)
    packed = jnp.zeros(packed_ref.shape, F32)
    for index, part in enumerate(columns[1:]):
        packed = jnp.where(lane == breadth + index, part.astype(F32), packed)
    packed_ref[...] = packed.astype(BF16)
    packed_ref[:, :breadth] = columns[0]


def closing_kernel(
    breadth,
    number,
    space_n,
    space_ref,
    weight_ref,
    block_ref,
    above_ref,
    below_ref,
    sums_ref,
    squares_ref,
    gains_ref,
    kernel_ref,
    noise_ref,
    out_ref,
    active,
):
    chan_n, token_n = block_ref.shape
    lat_n = noise_ref.shape[1]
    sums, squares = sums_ref[...], squares_ref[...]
    if space_n == 2:
        lane = lax.broadcasted_iota(jnp.int32, sums.shape, 1)
        peer = above_ref[...].astype(F32)
        sums = sums + jnp.where((lane >= breadth) & (lane < breadth + 3), peer, 0.0)
        squares = squares + jnp.where((lane >= breadth + 3) & (lane < breadth + 6), peer, 0.0)
    mean, square = group_moments(sums, squares, number)
    factor = lax.rsqrt(square - mean * mean + EPS_BLOCK) * gains_ref[:, 3:4]

    def act(value):
        return silu((value.astype(F32) - mean) * factor)

    first = space_ref[0] == 0
    last = space_ref[0] == space_n - 1
    margin = 2 * breadth
    top = jnp.where(first, 0.0, act(above_ref[:, :breadth]))
    end = jnp.where(last, 0.0, act(below_ref[:, :breadth]))
    blank = jnp.zeros((chan_n, breadth), F32)
    active[:, :margin] = jnp.concatenate([blank, top], axis=1).astype(BF16)
    active[:, margin : margin + token_n] = act(block_ref[...]).astype(BF16)
    active[:, margin + token_n :] = jnp.concatenate([end, blank], axis=1).astype(BF16)
    taps = jnp.dot(kernel_ref[...], active[...], preferred_element_type=F32)
    total_n = token_n + 2 * margin
    lane = lax.broadcasted_iota(jnp.int32, (8, token_n), 1)
    column = lane % breadth
    result = jnp.zeros((8, token_n), F32)
    for offset in range(9):
        row_off, col_off = offset // 3 - 1, offset % 3 - 1
        piece = taps[offset * 8 : (offset + 1) * 8]
        shift = -(row_off * breadth + col_off) % total_n
        moved = pltpu.roll(piece, shift, 1) if shift else piece
        moved = moved[:, margin : margin + token_n]
        good = (column + col_off >= 0) & (column + col_off < breadth)
        result = result + jnp.where(good, moved, 0.0)
    weight = weight_ref[0]
    for row in range(token_n // breadth):
        part = result[0:lat_n, row * breadth : (row + 1) * breadth]
        out_ref[row] = weight * (part - noise_ref[row])


def kernel_call(body, out_shape, scratch, scalars=0):
    smem = pl.BlockSpec(memory_space=pltpu.SMEM)
    vmem = pl.BlockSpec(memory_space=pltpu.VMEM)

    def call(*args):
        return pl.pallas_call(
            body,
            out_shape=out_shape,
            in_specs=[smem] * scalars + [vmem] * (len(args) - scalars),
            scratch_shapes=scratch,
            compiler_params=pltpu.CompilerParams(vmem_limit_bytes=VMEM_BYTES),
        )(*args)

    return call


def body(
    latents,
    noise_draw,
    timesteps,
    inlet_conv,
    time_first,
    time_first_bias,
    time_second,
    time_second_bias,
    conv_first,
    conv_second,
    proj_inner,
    query_weight,
    key_weight,
    value_weight,
    attn_out,
    proj_outer,
    outlet_conv,
    first_gain,
    second_gain,
    third_gain,
    final_gain,
    layer_gain,
):
    shape = jax.ShapeDtypeStruct
    view_n, height, breadth, lat_n = latents.shape
    assert view_n == 1
    rows = conv_first.shape[1]
    chan_n = inlet_conv.shape[1]
    temb_n = time_first_bias.shape[0]
    many = temb_n // chan_n
    space_n = lax.axis_size("space")
    place = lax.axis_index("space")
    token_n = height * space_n * breadth
    query_n = height * breadth

    squares = (proj_inner, query_weight, key_weight, value_weight, attn_out, proj_outer)
    shards = (conv_first, time_first, time_second, conv_second) + squares
    conv_width = conv_first.shape[0]
    width_one = conv_width + 2 * temb_n
    width_two = conv_width + len(squares) * chan_n
    batch_one, batch_two = kernel_call(
        pack_kernel,
        [shape((rows, width_one), BF16), shape((rows, width_two), BF16)],
        [],
    )(*(shard.T for shard in shards))

    moments = [shape((chan_n, 128), F32)] * 2
    taps_n = 9 * lat_n
    taps_pad = -(-taps_n // 16) * 16
    alpha_bar = lookup(timesteps)

    def early():
        alpha_here = alpha_bar[:, None, None, None]
        noisy = jnp.sqrt(alpha_here) * latents + jnp.sqrt(1.0 - alpha_here) * noise_draw
        noisy = noisy.astype(BF16)[0].transpose(0, 2, 1)
        noisy = lax.all_gather(noisy, "space", axis=0, tiled=True)
        inlet = jnp.pad(inlet_conv.T, ((0, 0), (0, taps_pad - taps_n)))
        opened = kernel_call(
            lambda *refs: opening_kernel(breadth, *refs),
            [shape((chan_n, token_n), BF16)] + moments,
            [pltpu.VMEM((8, token_n), F32), pltpu.VMEM((taps_pad, token_n), F32)],
        )(noisy, inlet)
        wave = waveform_of(timesteps, chan_n // 2)
        wave = jnp.broadcast_to(wave.reshape(chan_n, 1), (chan_n, 128))
        gains = (first_gain, second_gain, third_gain, final_gain, layer_gain, time_second_bias)
        gains = jnp.stack(gains, axis=1)
        outlet = outlet_conv.T.reshape(lat_n, 9, chan_n).transpose(1, 0, 2)
        outlet = jnp.pad(outlet, ((0, 0), (0, 8 - lat_n), (0, 0))).reshape(72, chan_n)
        bias = jnp.broadcast_to(time_first_bias[None], (8, temb_n))
        return list(opened) + [wave, gains, outlet, bias]

    (pieces_one, pieces_two), origin, extra = gather_shards((batch_one, batch_two), early)
    start, sums, squares, wave, gains, outlet, bias = extra
    space_id = place.reshape(1).astype(jnp.int32)

    count_one = len(pieces_one)
    deep = sum(padded(piece.shape[0]) for piece in pieces_one)
    args = (origin, start, sums, squares, gains, wave, bias, *pieces_one)
    middle, sums, squares = kernel_call(
        lambda *refs: first_kernel(count_one, rows, breadth, *refs),
        [shape((chan_n, token_n), BF16)] + moments,
        [
            pltpu.VMEM((deep, width_one), BF16),
            pltpu.VMEM((chan_n, width_one), BF16),
            pltpu.VMEM((9 * chan_n, token_n), BF16),
            pltpu.VMEM((chan_n, 128), F32),
            pltpu.VMEM((chan_n, 128), F32),
            pltpu.VMEM((temb_n, 128), F32),
        ],
        1,
    )(*args)

    count_two = len(pieces_two)
    half = HEADS // 2 * HEAD_SIZE
    args = (origin, space_id, middle, sums, squares, start, gains, *pieces_two)
    block, projected, query, key, value, outer = kernel_call(
        lambda *refs: second_kernel(count_two, rows, breadth, *refs),
        [
            shape((chan_n, query_n), BF16),
            shape((chan_n, query_n), F32),
            shape((HEADS, half, query_n), BF16),
            shape((2, token_n, half), BF16),
            shape((HEADS, HEAD_SIZE + 8, token_n), BF16),
            shape((2, chan_n, chan_n), BF16),
        ],
        [
            pltpu.VMEM((deep, width_two), BF16),
            pltpu.VMEM((chan_n, width_two), BF16),
            pltpu.VMEM((9 * chan_n, token_n), BF16),
            pltpu.VMEM((chan_n, 128), F32),
            pltpu.VMEM((chan_n, 128), F32),
            pltpu.VMEM((chan_n, 128), F32),
            pltpu.VMEM((chan_n, 128), F32),
            pltpu.VMEM((chan_n, token_n), BF16),
            pltpu.VMEM((chan_n, token_n), BF16),
        ],
        2,
    )(*args)

    block_w = min(256, query_n)
    block_two, sums, squares, packed = kernel_call(
        lambda *refs: attention_kernel(breadth, *refs),
        [shape((chan_n, query_n), BF16)] + moments + [shape((chan_n, 128), BF16)],
        [
            pltpu.VMEM((token_n, block_w), F32),
            pltpu.VMEM((token_n, block_w), BF16),
            pltpu.VMEM((chan_n, query_n), F32),
        ],
        1,
    )(space_id, query, key, value, projected, block, outer)

    if space_n == 2:
        above = below = lax.ppermute(packed, "space", [(0, 1), (1, 0)])
    else:
        sums, squares = lax.psum((sums, squares), "space")
        ahead = [(i, i + 1) for i in range(space_n - 1)]
        above = lax.ppermute(block_two[:, query_n - breadth :], "space", ahead)
        below = lax.ppermute(block_two[:, :breadth], "space", [(j, i) for i, j in ahead])
    number = token_n * (chan_n // GROUPS)
    args = (
        space_id,
        1.0 - alpha_bar,
        block_two,
        above,
        below,
        sums,
        squares,
        gains,
        outlet,
        noise_draw[0].transpose(0, 2, 1),
    )
    out = kernel_call(
        lambda *refs: closing_kernel(breadth, number, space_n, *refs),
        shape((height, lat_n, breadth), F32),
        [pltpu.VMEM((chan_n, query_n + 4 * breadth), BF16)],
        2,
    )(*args)
    return out.transpose(0, 2, 1)[None]


def solution(mesh):
    split = P(None, "batch")
    view = P("batch", "space", None, None)
    in_specs = (view, view, P("batch"), P(), split, P(), split, P())
    in_specs = in_specs + (split,) * 8 + (P(),) * 6
    return jax.shard_map(body, mesh=mesh, in_specs=in_specs, out_specs=view, check_vma=False)
```

time: 391 us -> 158 us (0.40); the launches traced: 385 us -> 158 us
  blocking collectives: 170 us -> 4.48 us
  matrix products: 103 us -> 0 us
  Pallas kernels: 0 us -> 103 us
  other arithmetic: 32 us -> 1.2 us
  local copies, waits for them, and re-layouts: 31.3 us -> 8.88 us
  between operations: 16 us -> 2.36 us
  waiting for transfers between devices: 8.87 us -> 20 us
  starting transfers between devices: 23.9 us -> 17.9 us
    all_gather x7 -> x1, blocking collectives: 136 us -> 4.48 us  [early(): noisy = lax.all_gather(noisy, 'space', axis=0, tiled=True)]
    pallas_call x0 -> x8, Pallas kernels: none -> 103 us  [call(): pl.pallas_call(body, out_shape=out_shape, in_specs=[smem] * scalars + [vm...]
    dot_general x52 -> x0, matrix products: 103 us -> none  [the longest x4 34.7 us: keys_everywhere(): jnp.einsum('bhqk,bkhd->bhqd', weights.astype(jnp.bfloat16), value_blk, pr...]
    reduce_sum x12 -> x1, other arithmetic: 26.5 us -> 0.67 us  [lookup(): return jnp.sum(jnp.where(matches, plan()[None, :], 0.0), axis=1)]
    psum x4 -> x0, blocking collectives: 21.6 us -> none  [group_norm(): sums_all, squares_all = lax.psum((sums_local, squares_local), 'space')]
    unnamed x60 -> x50, local copies, waits for them, and re-layouts: 20.8 us -> 3.81 us
    ppermute x8 -> x19, waiting for transfers between devices: 7.37 us -> 20 us  [the longest x6 13 us: gather_shards(): moving = [lax.ppermute(pair, 'batch', onward) for pair in moving]]
    unnamed x1 -> x0, blocking collectives: 12.3 us -> none
  transfers between devices with their start and end apart: 13 -> 19, of which waited for: 3 -> 7; matrix products, arithmetic and copies ran while one was open for 21% -> 3% of each run, Pallas kernels for 0% -> 16%
where the time goes in v1:
time: 158 us
  Pallas kernels  103 us (65%)
  waiting for transfers between devices  20 us (13%)
  starting transfers between devices  17.9 us (11%)
  local copies, waits for them, and re-layouts  8.88 us (6%)
  blocking collectives  4.48 us (3%)
  between operations  2.36 us (1%)
    pallas_call x8, Pallas kernels, call(): pl.pallas_call(body, out_shape=out_shape, in_specs=[smem] * scalars + [vm...  103 us
    ppermute x6, waiting for transfers between devices, gather_shards(): moving = [lax.ppermute(pair, 'batch', onward) for pair in moving]  13 us
    ppermute x6, starting transfers between devices, gather_shards(): moving = [lax.ppermute(pair, 'batch', onward) for pair in moving]  10.8 us
    all_gather x1, blocking collectives, early(): noisy = lax.all_gather(noisy, 'space', axis=0, tiled=True)  4.48 us
    ppermute x2, waiting for transfers between devices, gather_shards(): last = lax.ppermute(pair[:rows], 'batch', onward)  3.91 us
    unnamed x50, local copies, waits for them, and re-layouts  3.81 us
    ppermute x2, starting transfers between devices, gather_shards(): last = lax.ppermute(pair[:rows], 'batch', onward)  3.42 us
  transfers between devices with their start and end apart: 19, of which 7 were waited for; matrix products, arithmetic and copies ran while one was open for 3% of the time, Pallas kernels for 16%

profile of v1, /device:TPU:0, one launch (start us, length us, event | category | flops | bytes accessed | tf_op | source)
XLA Modules:
  0.0 158.1 jit_solution(12197984301197727617)
XLA Ops:
  0.1 2.0 %shard_map.217 = (bf16[20,5440]{1,0:T(8,128)(2,1)}, bf16[20,4800]{1,0:T(8,128)(2,1)}) custom-call(bf16[20,2880]{1,0:T(8,128)(2,1)} %bitcast.38, bf16[80,320]{1,0:T(8,128)(2,1)} %bitcast.41, bf16[20,1280]{1,0:T(8,128)(2,1)} %bitcast.42, bf16[20,2880]{1,0:T(8,128)(2,1)} %bitcast.39, bf16[20,320]{1,0:T(8,128)(2,1)} %bitcast.44, bf16[20,320]{1,0:T(8,128)(2,1)} %bitcast.45, ...), custom_call_target="tpu_custom_call" | custom-call | tf_op jit(solution)/shard_map/pallas_call | solution.py:544
  5.9 0.7 copy-done.12
  6.6 1.8 %shard_map.219.refs_7_ = bf16[40,4800]{1,0:T(8,128)(2,1)} custom-call(bf16[20,4800]{1,0:T(8,128)(2,1)} %get-tuple-element.33.one_ref, bf16[20,4800]{1,0:T(8,128)(2,1)} %copy-done.12), custom_call_target="tpu_custom_call" | custom-call | tf_op jit(solution)/shard_map/pallas_call | solution.py:544
  8.4 3.0 %collective-permute-start.3 = (bf16[40,4800]{1,0:T(8,128)(2,1)}, bf16[40,4800]{1,0:T(8,128)(2,1)S(1)}, u32[]{:S(2)}, u32[]{:S(2)}) collective-permute-start(bf16[40,4800]{1,0:T(8,128)(2,1)} %shard_map.219.refs_7_), channel_id=1, source_target_pairs={{0,8},{2,6},{8,16},{10,2},{16,24},{18,10},{24,28},{26,18},{28,20},... | collective-permute-start | bytes 1152008 | tf_op jit(solution)/shard_map/ppermute | solution.py:86
  11.5 0.7 copy-done.11
  12.2 1.8 %shard_map.218.refs_7_ = bf16[40,5440]{1,0:T(8,128)(2,1)} custom-call(bf16[20,5440]{1,0:T(8,128)(2,1)} %get-tuple-element.32.one_ref, bf16[20,5440]{1,0:T(8,128)(2,1)} %copy-done.11), custom_call_target="tpu_custom_call" | custom-call | tf_op jit(solution)/shard_map/pallas_call | solution.py:544
  14.1 1.6 collective-permute-start.1
  16.7 4.5 %all_gather.3.refs_0_ = bf16[32,4,64]{2,1,0:T(4,128)(2,1)} all-gather(bf16[16,4,64]{2,1,0:T(4,128)(2,1)S(1)} %fusion), channel_id=1, replica_groups=mesh['batch'=16,'space'=2] {'space'}, dimensions={0}, use_global_device_ids=true | all-gather | bytes 24576 | tf_op jit(solution)/shard_map/all_gather | solution.py:611
  21.2 2.8 %shard_map.220 = (bf16[320,2048]{1,0:T(8,128)(2,1)}, f32[320,128]{1,0:T(8,128)}, f32[320,128]{1,0:T(8,128)}) custom-call(bf16[32,4,64]{2,1,0:T(4,128)(2,1)} %all_gather.3.refs_0_, bf16[320,48]{1,0:T(8,128)(2,1)} %pad.12.refs_1_), custom_call_target="tpu_custom_call" | custom-call | tf_op jit(solution)/shard_map/pallas_call | solution.py:544
  25.5 0.7 broadcast_in_dim.11.refs_5_
  26.2 1.6 collective-permute-start.5
  27.8 1.5 collective-permute-start.12
  29.3 5.2 %collective-permute-done.5.refs_10_ = bf16[40,5440]{1,0:T(8,128)(2,1)S(1)} collective-permute-done((bf16[40,5440]{1,0:T(8,128)(2,1)S(1)}, bf16[40,5440]{1,0:T(8,128)(2,1)S(1)}, u32[]{:S(2)}, u32[]{:S(2)}) %collective-permute-start.5) | collective-permute-done | bytes 435232 | tf_op jit(solution)/shard_map/ppermute | solution.py:86
  34.5 1.6 collective-permute-start.7
  36.1 2.7 %collective-permute-done.12.refs_10_ = bf16[40,4800]{1,0:T(8,128)(2,1)} collective-permute-done((bf16[40,4800]{1,0:T(8,128)(2,1)S(1)}, bf16[40,4800]{1,0:T(8,128)(2,1)}, u32[]{:S(2)}, u32[]{:S(2)}) %collective-permute-start.12) | collective-permute-done | bytes 384032 | tf_op jit(solution)/shard_map/ppermute | solution.py:86
  38.8 1.6 collective-permute-start.14
  40.9 2.5 %collective-permute-done.7.refs_12_ = bf16[40,5440]{1,0:T(8,128)(2,1)S(1)} collective-permute-done((bf16[40,5440]{1,0:T(8,128)(2,1)S(1)}, bf16[40,5440]{1,0:T(8,128)(2,1)S(1)}, u32[]{:S(2)}, u32[]{:S(2)}) %collective-permute-start.7) | collective-permute-done | bytes 435232 | tf_op jit(solution)/shard_map/ppermute | solution.py:86
  43.4 1.6 %collective-permute-start.9 = (bf16[20,5440]{1,0:T(8,128)(2,1)S(1)}, bf16[20,5440]{1,0:T(8,128)(2,1)S(1)}, u32[]{:S(2)}, u32[]{:S(2)}) collective-permute-start(bf16[20,5440]{1,0:T(8,128)(2,1)S(1)} %slice.22), channel_id=1, source_target_pairs={{0,8},{2,6},{8,16},{10,2},{16,24},{18,10},{24,28},{26,18},{28,20},... | collective-permute-start | bytes 652808 | tf_op jit(solution)/shard_map/ppermute | solution.py:93
  45.0 2.5 %collective-permute-done.14.refs_12_ = bf16[40,4800]{1,0:T(8,128)(2,1)S(1)} collective-permute-done((bf16[40,4800]{1,0:T(8,128)(2,1)}, bf16[40,4800]{1,0:T(8,128)(2,1)S(1)}, u32[]{:S(2)}, u32[]{:S(2)}) %collective-permute-start.14) | collective-permute-done | bytes 384032 | tf_op jit(solution)/shard_map/ppermute | solution.py:86
  47.6 1.8 %collective-permute-start.16 = (bf16[20,4800]{1,0:T(8,128)(2,1)S(1)}, bf16[20,4800]{1,0:T(8,128)(2,1)}, u32[]{:S(2)}, u32[]{:S(2)}) collective-permute-start(bf16[20,4800]{1,0:T(8,128)(2,1)S(1)} %slice.23), channel_id=1, source_target_pairs={{0,8},{2,6},{8,16},{10,2},{16,24},{18,10},{24,28},{26,18},{28,20},... | collective-permute-start | bytes 576008 | tf_op jit(solution)/shard_map/ppermute | solution.py:93
  49.4 1.0 collective-permute-done.9.refs_14_
  51.1 2.9 %collective-permute-done.16.refs_14_ = bf16[20,4800]{1,0:T(8,128)(2,1)} collective-permute-done((bf16[20,4800]{1,0:T(8,128)(2,1)S(1)}, bf16[20,4800]{1,0:T(8,128)(2,1)}, u32[]{:S(2)}, u32[]{:S(2)}) %collective-permute-start.16) | collective-permute-done | bytes 192032 | tf_op jit(solution)/shard_map/ppermute | solution.py:93
  54.0 0.7 copy-done.10
  55.2 1.2 dynamic-slice_bitcast_fusion.refs_0_
  56.4 0.8 copy.36.refs_4_.refs_6_.refs_7_
  57.3 0.8 copy-done.6
  58.0 19.1 %shard_map.221 = (bf16[320,2048]{1,0:T(8,128)(2,1)}, f32[320,128]{1,0:T(8,128)}, f32[320,128]{1,0:T(8,128)}) custom-call(s32[16]{0:T(128)} %dynamic-slice_bitcast_fusion.refs_0_, bf16[320,2048]{1,0:T(8,128)(2,1)} %get-tuple-element.37.refs_1_.refs_5_, f32[320,128]{1,0:T(8,128)} %get-tuple-element.38.refs_2_, f32[320,128]{1,0:T(8,128)} %get-tuple-element.39.refs_3_, ...), custom_call_target="tpu_custom_call" | custom-call | tf_op jit(solution)/shard_map/pallas_call | solution.py:544
  77.2 25.9 %shard_map.222 = (bf16[320,1024]{1,0:T(8,128)(2,1)}, f32[320,1024]{1,0:T(8,128)}, bf16[8,160,1024]{2,1,0:T(8,128)(2,1)}, bf16[2,2048,160]{2,1,0:T(8,128)(2,1)}, ...) custom-call(s32[16]{0:T(128)} %dynamic-slice_bitcast_fusion.refs_0_, s32[1]{0:T(128)} %bitcast.refs_1_.refs_0_, ...), custom_call_target="tpu_custom_call" | custom-call | tf_op jit(solution)/shard_map/pallas_call | solution.py:544
  103.0 45.8 %shard_map.223 = (bf16[320,1024]{1,0:T(8,128)(2,1)}, f32[320,128]{1,0:T(8,128)}, f32[320,128]{1,0:T(8,128)}, bf16[320,128]{1,0:T(8,128)(2,1)}) custom-call(s32[1]{0:T(128)} %bitcast.refs_1_.refs_0_, bf16[8,160,1024]{2,1,0:T(8,128)(2,1)} %get-tuple-element.48.refs_1_, bf16[2,2048,160]{2,1,0:T(8,128)(2,1)} %get-tuple-element.49.refs_2_, ...), custom_call_target="tpu_custom_call" | custom-call | tf_op jit(solution)/shard_map/pallas_call | solution.py:544
  148.8 1.5 collective-permute-start.18
  150.3 3.1 %collective-permute-done.18.refs_3_.refs_4_ = bf16[320,128]{1,0:T(8,128)(2,1)S(1)} collective-permute-done((bf16[320,128]{1,0:T(8,128)(2,1)}, bf16[320,128]{1,0:T(8,128)(2,1)S(1)}, u32[]{:S(2)}, u32[]{:S(2)}) %collective-permute-start.18) | collective-permute-done | bytes 81952 | tf_op jit(solution)/shard_map/ppermute | solution.py:688
  154.1 4.0 %shard_map.224 = f32[16,4,64]{2,1,0:T(4,128)} custom-call(s32[1]{0:T(128)} %bitcast.refs_1_.refs_0_, f32[1]{0:T(128)} %bitcast.4.refs_1_, bf16[320,1024]{1,0:T(8,128)(2,1)} %get-tuple-element.54.refs_2_, bf16[320,128]{1,0:T(8,128)(2,1)} %copy-done.8, bf16[320,128]{1,0:T(8,128)(2,1)} %copy-done.8, f32[320,128]{1,0:T(8,128)} %get-tuple-element.56.refs_5_, ...), custom_call_target="tpu_custom_call" | custom-call | tf_op jit(solution)/shard_map/pallas_call | solution.py:544
  (92 shorter events, 6.6 us)
Async XLA Ops:
  0.0 15.7 %copy-start.18 = (f32[320]{0:T(512)S(1)}, f32[320]{0:T(512)}, u32[]{:S(2)}) copy-start(f32[320]{0:T(512)} %param.30) | copy-start | bytes 3844
  0.0 15.7 %copy-start.19 = (f32[320]{0:T(512)S(1)}, f32[320]{0:T(512)}, u32[]{:S(2)}) copy-start(f32[320]{0:T(512)} %param.40) | copy-start | bytes 3844
  0.0 15.7 %copy-start.20 = (f32[320]{0:T(512)S(1)}, f32[320]{0:T(512)}, u32[]{:S(2)}) copy-start(f32[320]{0:T(512)} %param.41) | copy-start | bytes 3844
  0.0 15.7 %copy-start.21 = (f32[320]{0:T(512)S(1)}, f32[320]{0:T(512)}, u32[]{:S(2)}) copy-start(f32[320]{0:T(512)} %param.42) | copy-start | bytes 3844
  0.0 15.7 %copy-start.22 = (f32[320]{0:T(512)S(1)}, f32[320]{0:T(512)}, u32[]{:S(2)}) copy-start(f32[320]{0:T(512)} %param.43) | copy-start | bytes 3844
  0.0 15.7 %copy-start.23 = (f32[320]{0:T(512)S(1)}, f32[320]{0:T(512)}, u32[]{:S(2)}) copy-start(f32[320]{0:T(512)} %param.44) | copy-start | bytes 3844
  0.0 15.7 %copy-start.16 = (bf16[2880,4]{0,1:T(4,128)(2,1)S(1)}, bf16[2880,4]{0,1:T(4,128)(2,1)}, u32[]{:S(2)}) copy-start(bf16[2880,4]{0,1:T(4,128)(2,1)} %param.39) | copy-start | bytes 69124
  0.1 15.9 %copy-start.15 = (bf16[36,320]{1,0:T(8,128)(2,1)S(1)}, bf16[36,320]{1,0:T(8,128)(2,1)}, u32[]{:S(2)}) copy-start(bf16[36,320]{1,0:T(8,128)(2,1)} %param.26) | copy-start | bytes 69124
  0.1 24.8 %copy-start.17 = (f32[1280]{0:T(1024)S(1)}, f32[1280]{0:T(1024)}, u32[]{:S(2)}) copy-start(f32[1280]{0:T(1024)} %param.28) | copy-start | bytes 15364
  2.1 3.8 %collective-permute-start.2 = (bf16[20,4800]{1,0:T(8,128)(2,1)}, bf16[20,4800]{1,0:T(8,128)(2,1)S(1)}, u32[]{:S(2)}, u32[]{:S(2)}) collective-permute-start(bf16[20,4800]{1,0:T(8,128)(2,1)} %get-tuple-element.33.one_ref), channel_id=1, source_target_pairs={{0,2},{2,0},{4,6},{6,4},{8,10},{10,8},{12,14},{14,12},{16,18},{18,... | collective-permute-start | bytes 576008 | tf_op jit(solution)/shard_map/ppermute | solution.py:81
  2.6 8.9 %collective-permute-start = (bf16[20,5440]{1,0:T(8,128)(2,1)}, bf16[20,5440]{1,0:T(8,128)(2,1)S(1)}, u32[]{:S(2)}, u32[]{:S(2)}) collective-permute-start(bf16[20,5440]{1,0:T(8,128)(2,1)} %get-tuple-element.32.one_ref), channel_id=1, source_target_pairs={{0,2},{2,0},{4,6},{6,4},{8,10},{10,8},{12,14},{14,12},{16,18},{18,... | collective-permute-start | bytes 652808 | tf_op jit(solution)/shard_map/ppermute | solution.py:81
  8.4 16.4 %collective-permute-start.3 = (bf16[40,4800]{1,0:T(8,128)(2,1)}, bf16[40,4800]{1,0:T(8,128)(2,1)S(1)}, u32[]{:S(2)}, u32[]{:S(2)}) collective-permute-start(bf16[40,4800]{1,0:T(8,128)(2,1)} %shard_map.219.refs_7_), channel_id=1, source_target_pairs={{0,8},{2,6},{8,16},{10,2},{16,24},{18,10},{24,28},{26,18},{28,20},... | collective-permute-start | bytes 1152008 | tf_op jit(solution)/shard_map/ppermute | solution.py:86
  14.1 10.8 %collective-permute-start.1 = (bf16[40,5440]{1,0:T(8,128)(2,1)}, bf16[40,5440]{1,0:T(8,128)(2,1)S(1)}, u32[]{:S(2)}, u32[]{:S(2)}) collective-permute-start(bf16[40,5440]{1,0:T(8,128)(2,1)} %shard_map.218.refs_7_), channel_id=1, source_target_pairs={{0,8},{2,6},{8,16},{10,2},{16,24},{18,10},{24,28},{26,18},{28,20},... | collective-permute-start | bytes 1305608 | tf_op jit(solution)/shard_map/ppermute | solution.py:86
  24.8 52.4 %copy-start.7 = (bf16[40,4800]{1,0:T(8,128)(2,1)}, bf16[40,4800]{1,0:T(8,128)(2,1)S(1)}, u32[]{:S(2)}) copy-start(bf16[40,4800]{1,0:T(8,128)(2,1)S(1)} %collective-permute-done.3.refs_8_) | copy-start | bytes 1152004
  24.8 32.4 %copy-start.2 = (bf16[40,5440]{1,0:T(8,128)(2,1)}, bf16[40,5440]{1,0:T(8,128)(2,1)S(1)}, u32[]{:S(2)}) copy-start(bf16[40,5440]{1,0:T(8,128)(2,1)S(1)} %collective-permute-done.1.refs_8_) | copy-start | bytes 1305604
  26.2 8.3 %collective-permute-start.5 = (bf16[40,5440]{1,0:T(8,128)(2,1)S(1)}, bf16[40,5440]{1,0:T(8,128)(2,1)S(1)}, u32[]{:S(2)}, u32[]{:S(2)}) collective-permute-start(bf16[40,5440]{1,0:T(8,128)(2,1)S(1)} %collective-permute-done.1.refs_8_), channel_id=1, source_target_pairs={{0,8},{2,6},{8,16},{10,2},{16,24},{18,10},{24,28},{26,18},{28,20},... | collective-permute-start | bytes 1305608 | tf_op jit(solution)/shard_map/ppermute | solution.py:86
  27.8 11.0 %collective-permute-start.12 = (bf16[40,4800]{1,0:T(8,128)(2,1)S(1)}, bf16[40,4800]{1,0:T(8,128)(2,1)}, u32[]{:S(2)}, u32[]{:S(2)}) collective-permute-start(bf16[40,4800]{1,0:T(8,128)(2,1)S(1)} %collective-permute-done.3.refs_8_), channel_id=1, source_target_pairs={{0,8},{2,6},{8,16},{10,2},{16,24},{18,10},{24,28},{26,18},{28,20},... | collective-permute-start | bytes 1152008 | tf_op jit(solution)/shard_map/ppermute | solution.py:86
  34.5 22.7 %copy-start.3 = (bf16[40,5440]{1,0:T(8,128)(2,1)}, bf16[40,5440]{1,0:T(8,128)(2,1)S(1)}, u32[]{:S(2)}) copy-start(bf16[40,5440]{1,0:T(8,128)(2,1)S(1)} %collective-permute-done.5.refs_10_) | copy-start | bytes 1305604
  34.5 8.9 %collective-permute-start.7 = (bf16[40,5440]{1,0:T(8,128)(2,1)S(1)}, bf16[40,5440]{1,0:T(8,128)(2,1)S(1)}, u32[]{:S(2)}, u32[]{:S(2)}) collective-permute-start(bf16[40,5440]{1,0:T(8,128)(2,1)S(1)} %collective-permute-done.5.refs_10_), channel_id=1, source_target_pairs={{0,8},{2,6},{8,16},{10,2},{16,24},{18,10},{24,28},{26,18},{28,20},... | collective-permute-start | bytes 1305608 | tf_op jit(solution)/shard_map/ppermute | solution.py:86
  38.8 8.8 %collective-permute-start.14 = (bf16[40,4800]{1,0:T(8,128)(2,1)}, bf16[40,4800]{1,0:T(8,128)(2,1)S(1)}, u32[]{:S(2)}, u32[]{:S(2)}) collective-permute-start(bf16[40,4800]{1,0:T(8,128)(2,1)} %collective-permute-done.12.refs_10_), channel_id=1, source_target_pairs={{0,8},{2,6},{8,16},{10,2},{16,24},{18,10},{24,28},{26,18},{28,20},... | collective-permute-start | bytes 1152008 | tf_op jit(solution)/shard_map/ppermute | solution.py:86
  40.4 10.1 %collective-permute-start.4 = (bf16[40,5440]{1,0:T(8,128)(2,1)S(1)}, bf16[40,5440]{1,0:T(8,128)(2,1)S(1)}, u32[]{:S(2)}, u32[]{:S(2)}) collective-permute-start(bf16[40,5440]{1,0:T(8,128)(2,1)S(1)} %collective-permute-done.1.refs_8_), channel_id=1, source_target_pairs={{0,2},{2,0},{4,6},{6,4},{8,10},{10,8},{12,14},{14,12},{16,18},{18,... | collective-permute-start | bytes 1305608 | tf_op jit(solution)/shard_map/ppermute | solution.py:91
  40.4 10.6 %collective-permute-start.6 = (bf16[40,5440]{1,0:T(8,128)(2,1)S(1)}, bf16[40,5440]{1,0:T(8,128)(2,1)S(1)}, u32[]{:S(2)}, u32[]{:S(2)}) collective-permute-start(bf16[40,5440]{1,0:T(8,128)(2,1)S(1)} %collective-permute-done.5.refs_10_), channel_id=1, source_target_pairs={{0,2},{2,0},{4,6},{6,4},{8,10},{10,8},{12,14},{14,12},{16,18},{18,... | collective-permute-start | bytes 1305608 | tf_op jit(solution)/shard_map/ppermute | solution.py:91
  43.4 7.0 %collective-permute-start.9 = (bf16[20,5440]{1,0:T(8,128)(2,1)S(1)}, bf16[20,5440]{1,0:T(8,128)(2,1)S(1)}, u32[]{:S(2)}, u32[]{:S(2)}) collective-permute-start(bf16[20,5440]{1,0:T(8,128)(2,1)S(1)} %slice.22), channel_id=1, source_target_pairs={{0,8},{2,6},{8,16},{10,2},{16,24},{18,10},{24,28},{26,18},{28,20},... | collective-permute-start | bytes 652808 | tf_op jit(solution)/shard_map/ppermute | solution.py:93
  47.6 29.6 %copy-start.1 = (bf16[40,4800]{1,0:T(8,128)(2,1)}, bf16[40,4800]{1,0:T(8,128)(2,1)S(1)}, u32[]{:S(2)}) copy-start(bf16[40,4800]{1,0:T(8,128)(2,1)S(1)} %collective-permute-done.14.refs_12_) | copy-start | bytes 1152004
  47.6 6.4 %collective-permute-start.16 = (bf16[20,4800]{1,0:T(8,128)(2,1)S(1)}, bf16[20,4800]{1,0:T(8,128)(2,1)}, u32[]{:S(2)}, u32[]{:S(2)}) collective-permute-start(bf16[20,4800]{1,0:T(8,128)(2,1)S(1)} %slice.23), channel_id=1, source_target_pairs={{0,8},{2,6},{8,16},{10,2},{16,24},{18,10},{24,28},{26,18},{28,20},... | collective-permute-start | bytes 576008 | tf_op jit(solution)/shard_map/ppermute | solution.py:93
  49.4 7.8 %collective-permute-start.8 = (bf16[40,5440]{1,0:T(8,128)(2,1)S(1)}, bf16[40,5440]{1,0:T(8,128)(2,1)S(1)}, u32[]{:S(2)}, u32[]{:S(2)}) collective-permute-start(bf16[40,5440]{1,0:T(8,128)(2,1)S(1)} %collective-permute-done.7.refs_12_), channel_id=1, source_target_pairs={{0,2},{2,0},{4,6},{6,4},{8,10},{10,8},{12,14},{14,12},{16,18},{18,... | collective-permute-start | bytes 1305608 | tf_op jit(solution)/shard_map/ppermute | solution.py:91
  50.4 3.6 %collective-permute-start.10 = (bf16[20,5440]{1,0:T(8,128)(2,1)S(1)}, bf16[20,5440]{1,0:T(8,128)(2,1)S(1)}, u32[]{:S(2)}, u32[]{:S(2)}) collective-permute-start(bf16[20,5440]{1,0:T(8,128)(2,1)S(1)} %collective-permute-done.9.refs_14_), channel_id=1, source_target_pairs={{0,2},{2,0},{4,6},{6,4},{8,10},{10,8},{12,14},{14,12},{16,18},{18,... | collective-permute-start | bytes 652808 | tf_op jit(solution)/shard_map/ppermute | solution.py:94
  50.4 26.7 %collective-permute-start.11 = (bf16[40,4800]{1,0:T(8,128)(2,1)S(1)}, bf16[40,4800]{1,0:T(8,128)(2,1)}, u32[]{:S(2)}, u32[]{:S(2)}) collective-permute-start(bf16[40,4800]{1,0:T(8,128)(2,1)S(1)} %collective-permute-done.3.refs_8_), channel_id=1, source_target_pairs={{0,2},{2,0},{4,6},{6,4},{8,10},{10,8},{12,14},{14,12},{16,18},{18,... | collective-permute-start | bytes 1152008 | tf_op jit(solution)/shard_map/ppermute | solution.py:91
  50.9 26.2 %collective-permute-start.13 = (bf16[40,4800]{1,0:T(8,128)(2,1)}, bf16[40,4800]{1,0:T(8,128)(2,1)}, u32[]{:S(2)}, u32[]{:S(2)}) collective-permute-start(bf16[40,4800]{1,0:T(8,128)(2,1)} %collective-permute-done.12.refs_10_), channel_id=1, source_target_pairs={{0,2},{2,0},{4,6},{6,4},{8,10},{10,8},{12,14},{14,12},{16,18},{18,... | collective-permute-start | bytes 1152008 | tf_op jit(solution)/shard_map/ppermute | solution.py:91
  54.0 23.1 %collective-permute-start.15 = (bf16[40,4800]{1,0:T(8,128)(2,1)S(1)}, bf16[40,4800]{1,0:T(8,128)(2,1)}, u32[]{:S(2)}, u32[]{:S(2)}) collective-permute-start(bf16[40,4800]{1,0:T(8,128)(2,1)S(1)} %collective-permute-done.14.refs_12_), channel_id=1, source_target_pairs={{0,2},{2,0},{4,6},{6,4},{8,10},{10,8},{12,14},{14,12},{16,18},{18,... | collective-permute-start | bytes 1152008 | tf_op jit(solution)/shard_map/ppermute | solution.py:91
  54.7 22.5 %collective-permute-start.17 = (bf16[20,4800]{1,0:T(8,128)(2,1)}, bf16[20,4800]{1,0:T(8,128)(2,1)}, u32[]{:S(2)}, u32[]{:S(2)}) collective-permute-start(bf16[20,4800]{1,0:T(8,128)(2,1)} %collective-permute-done.16.refs_14_), channel_id=1, source_target_pairs={{0,2},{2,0},{4,6},{6,4},{8,10},{10,8},{12,14},{14,12},{16,18},{18,... | collective-permute-start | bytes 576008 | tf_op jit(solution)/shard_map/ppermute | solution.py:94
  148.8 4.7 %collective-permute-start.18 = (bf16[320,128]{1,0:T(8,128)(2,1)}, bf16[320,128]{1,0:T(8,128)(2,1)S(1)}, u32[]{:S(2)}, u32[]{:S(2)}) collective-permute-start(bf16[320,128]{1,0:T(8,128)(2,1)} %get-tuple-element.55), channel_id=1, source_target_pairs={{0,1},{1,0},{2,3},{3,2},{4,5},{5,4},{6,7},{7,6},{8,9},{9,8},{10,11... | collective-permute-start | bytes 245768 | tf_op jit(solution)/shard_map/ppermute | solution.py:688
  (11 other events, 62.5 us)

commit v2 on v1

--- a/solution.py
+++ b/solution.py
@@ -81,18 +81,18 @@
     others = [lax.ppermute(shard, "batch", sibling) for shard in shards]
     moving = [pair_up(shard, other) for shard, other in zip(shards, others)]
     gathered = [[pair] for pair in moving]
+    table = jnp.asarray(table, dtype=jnp.int32)
     extra = None
     for step in range(1, half):
         moving = [lax.ppermute(pair, "batch", onward) for pair in moving]
         if extra is None:
-            extra = beside()
-            moving, extra = lax.optimization_barrier((moving, extra))
+            origin = table[lax.axis_index("batch")]
+            moving, origin, extra = lax.optimization_barrier((moving, origin, beside()))
         for pieces, pair in zip(gathered, moving):
             pieces += [pair, lax.ppermute(pair, "batch", sibling)]
     for pieces, pair in zip(gathered, moving):
         last = lax.ppermute(pair[:rows], "batch", onward)
         pieces += [last, lax.ppermute(last, "batch", sibling)]
-    origin = jnp.asarray(table, dtype=jnp.int32)[lax.axis_index("batch")]
     return gathered, origin, extra
 
 
@@ -123,8 +123,8 @@
 def assemble(origin_ref, pieces, stage, rows, out_ref):
     total, deep = out_ref.shape[0], stage.shape[0]
     rid = lax.broadcasted_iota(jnp.int32, (total, deep), 0)
-    cid = lax.broadcasted_iota(jnp.int32, (total, deep), 1)
-    want = jnp.full((total, deep), -1, jnp.int32)
+    cid = lax.broadcasted_iota(jnp.int32, (1, deep), 1)
+    want = jnp.full((1, deep), -1, jnp.int32)
     place = base = 0
     for ref in pieces:
         size = ref.shape[0]
@@ -147,43 +147,56 @@
         ).astype(BF16)
 
 
-def spread_taps(load, store, chan_n, token_n, breadth, chunk=16):
+def spread_taps(load, level_ref, offset_ref, breadth, chunk=16):
+    chan_n, token_n = level_ref.shape[0] // 3, level_ref.shape[1]
+
     def one(index, carry):
         base = pl.multiple_of(index * chunk, chunk)
         value = load(base, chunk)
-        lane = lax.broadcasted_iota(jnp.int32, (chunk, token_n), 1)
-        column = lane % breadth
+        column = lax.broadcasted_iota(jnp.int32, (chunk, token_n), 1) % breadth
         left = jnp.where(column == 0, 0.0, pltpu.roll(value, 1, 1))
         right = jnp.where(column == breadth - 1, 0.0, pltpu.roll(value, token_n - 1, 1))
+        margin = lax.broadcasted_iota(jnp.int32, (chunk, 2 * breadth), 1) < breadth
         for col, variant in enumerate((left, value, right)):
-            up = jnp.where(lane < breadth, 0.0, pltpu.roll(variant, breadth, 1))
-            down = jnp.where(
-                lane >= token_n - breadth, 0.0, pltpu.roll(variant, token_n - breadth, 1)
-            )
-            for row, shifted in enumerate((up, variant, down)):
-                store((3 * row + col) * chan_n + base, chunk, shifted.astype(BF16))
+            place = pl.ds(pl.multiple_of(col * chan_n + base, chunk), chunk)
+            level_ref[place, :] = variant.astype(BF16)
+            later = pltpu.roll(variant, breadth, 1)
+            head = later[:, : 2 * breadth]
+            offset_ref[place, : 2 * breadth] = jnp.where(margin, 0.0, head).astype(BF16)
+            offset_ref[place, 2 * breadth : token_n] = later[:, 2 * breadth :].astype(BF16)
+            offset_ref[place, token_n:] = jnp.where(margin, head, 0.0).astype(BF16)
         return carry
 
     lax.fori_loop(0, chan_n // chunk, one, 0)
+
+
+def convolve(weights, level_ref, offset_ref, breadth, start, block_n):
+    deep = level_ref.shape[0]
+    total = None
+    for row in range(3):
+        source = level_ref if row == 1 else offset_ref
+        first = start + (2 * breadth if row == 2 else 0)
+        part = jnp.dot(
+            weights[:, row * deep : (row + 1) * deep],
+            source[:, first : first + block_n],
+            preferred_element_type=F32,
+        )
+        total = part if total is None else total + part
+    return total
 
 
 def silu(value):
     return value / (1.0 + jnp.exp(-value))
 
 
-def normal_taps(source_ref, taps_ref, mean_ref, factor_ref, breadth):
-    chan_n, token_n = source_ref.shape
-
+def normal_taps(source_ref, level_ref, offset_ref, mean_ref, factor_ref, breadth):
     def load(base, chunk):
         value = source_ref[pl.ds(base, chunk), :].astype(F32)
         mean = mean_ref[pl.ds(base, chunk), 0:1]
         factor = factor_ref[pl.ds(base, chunk), 0:1]
         return silu((value - mean) * factor)
 
-    def store(base, chunk, value):
-        taps_ref[pl.ds(pl.multiple_of(base, chunk), chunk), :] = value
-
-    spread_taps(load, store, chan_n, token_n, breadth)
+    spread_taps(load, level_ref, offset_ref, breadth)
 
 
 def set_moments(sums, squares, number, gain, epsilon, mean_ref, factor_ref):
@@ -269,7 +282,7 @@
 ):
     pieces = rest[:counts]
     middle_ref, sums_out, squares_out = rest[counts : counts + 3]
-    stage, weights, taps, mean, factor, hidden = rest[counts + 3 :]
+    stage, weights, level, offset, mean, factor, hidden = rest[counts + 3 :]
     chan_n, token_n = start_ref.shape
     number = token_n * (chan_n // GROUPS)
     assemble(origin_ref, pieces, stage, rows, weights)
@@ -289,12 +302,10 @@
     set_moments(
         sums_ref[...], squares_ref[...], number, gains_ref[:, 0:1], EPS_BLOCK, mean, factor
     )
-    normal_taps(start_ref, taps, mean, factor, breadth)
+    normal_taps(start_ref, level, offset, mean, factor, breadth)
     block_n = min(512, token_n)
     for start in range(0, token_n, block_n):
-        part = jnp.dot(
-            weights[:, :conv_width], taps[:, start : start + block_n], preferred_element_type=F32
-        )
+        part = convolve(weights, level, offset, breadth, start, block_n)
         part = (part + embedded).astype(BF16)
         middle_ref[:, start : start + block_n] = part
         wide = part.astype(F32)
@@ -320,10 +331,13 @@
     *rest,
 ):
     pieces = rest[:counts]
-    block_out, projected_out, query_out, key_out, value_out, outer_out = rest[counts : counts + 6]
-    stage, weights, taps, mean, factor, sums, squares, block, tokens = rest[counts + 6 :]
+    outputs = rest[counts : counts + 4]
+    stage, weights, level, offset, mean, factor, sums, squares, block, tokens = rest[
+        counts + 4 : counts + 14
+    ]
+    query_out, key_out, value_out = rest[counts + 14 : counts + 17]
     chan_n, token_n = middle_ref.shape
-    query_n = block_out.shape[1]
+    query_n = query_out.shape[2]
     number = token_n * (chan_n // GROUPS)
     assemble(origin_ref, pieces, stage, rows, weights)
     conv_width = 9 * chan_n
@@ -335,12 +349,10 @@
     set_moments(
         sums_ref[...], squares_ref[...], number, gains_ref[:, 1:2], EPS_BLOCK, mean, factor
     )
-    normal_taps(middle_ref, taps, mean, factor, breadth)
+    normal_taps(middle_ref, level, offset, mean, factor, breadth)
     block_n = min(512, token_n)
     for start in range(0, token_n, block_n):
-        part = jnp.dot(
-            weights[:, :conv_width], taps[:, start : start + block_n], preferred_element_type=F32
-        )
+        part = convolve(weights, level, offset, breadth, start, block_n)
         part = (part + start_ref[:, start : start + block_n].astype(F32)).astype(BF16)
         block[:, start : start + block_n] = part
         wide = part.astype(F32)
@@ -372,7 +384,7 @@
             value_out[head, :, start : start + block_n] = jnp.concatenate(
                 [piece, ones], axis=0
             ).astype(BF16)
-        upright = scaled.T.astype(BF16)
+        upright = token.T
         half = HEADS // 2 * HEAD_SIZE
         for part in range(2):
             matrix = weights[
@@ -382,8 +394,6 @@
             key_out[part, start : start + block_n, :] = lax.dot_general(
                 upright, matrix, (((1,), (1,)), ((), ())), preferred_element_type=F32
             ).astype(BF16)
-    block_out[...] = block[:, pl.ds(own, query_n)]
-    projected_out[...] = project(block[:, pl.ds(own, query_n)])
     query = jnp.dot(small(1), tokens[:, pl.ds(own, query_n)], preferred_element_type=F32)
     query = query * (math.log2(math.e) / math.sqrt(HEAD_SIZE))
     per_half = HEADS // 2
@@ -397,8 +407,13 @@
         if spot < per_half - 1:
             parts.append(jnp.zeros(((per_half - 1 - spot) * HEAD_SIZE, query_n), F32))
         query_out[head] = jnp.concatenate(parts, axis=0).astype(BF16)
-    outer_out[0] = small(4)
-    outer_out[1] = small(5)
+    attend(query_out, key_out, value_out, *rest[counts + 17 :])
+    attended = rest[counts + 17]
+    mine = block[:, pl.ds(own, query_n)]
+    mixture = jnp.dot(small(4), attended[...].astype(BF16), preferred_element_type=F32)
+    mixture = (mixture + project(mine)).astype(BF16)
+    outer = jnp.dot(small(5), mixture, preferred_element_type=F32)
+    report((mine.astype(F32) + outer).astype(BF16), breadth, space_ref[0] == 0, *outputs)
 
 
 def exact_parts(value):
@@ -408,73 +423,71 @@
     return [high, middle, (rest - middle.astype(F32)).astype(BF16)]
 
 
-def attention_kernel(
-    breadth,
-    space_ref,
-    query_ref,
-    key_ref,
-    value_ref,
-    projected_ref,
-    block_ref,
-    outer_ref,
-    block_two_ref,
-    sums_ref,
-    squares_ref,
-    packed_ref,
-    scores,
-    weights,
-    attended,
-):
+def attend(query_ref, key_ref, value_ref, attended, *slots):
     heads, _, query_n = query_ref.shape
     token_n = key_ref.shape[1]
-    width = scores.shape[1]
-    per_half = heads // 2
-    key_n = min(512, token_n)
-
-    for head in range(heads):
-
-        def one(step, carry):
-            base = pl.multiple_of(step * width, 128)
-            query = query_ref[head, :, pl.ds(base, width)]
-            top = jnp.full((1, width), -jnp.inf, F32)
-            for start in range(0, token_n, key_n):
+    width = slots[0].shape[1]
+    blocks = query_n // width
+    items = heads * blocks
+    key_n = min(256, token_n)
+
+    def spot(item):
+        return item // blocks, pl.multiple_of((item % blocks) * width, 128)
+
+    def step(item, scores, tops, ahead, scores_ahead, tops_ahead):
+        head_ahead, base_ahead = spot(ahead)
+        query = query_ref[head_ahead, :, pl.ds(base_ahead, width)]
+        running = mixed = None
+        if item is not None:
+            head, base = spot(item)
+            top = jnp.max(tops[...], axis=0, keepdims=True)
+        for start in range(0, token_n, key_n):
+            keys = key_ref[head_ahead // (heads // 2), start : start + key_n, :]
+            part = jnp.dot(keys, query, preferred_element_type=F32)
+            scores_ahead[start : start + key_n, :] = part
+            part = jnp.max(part.reshape(key_n // 8, 8, width), axis=0)
+            running = part if running is None else jnp.maximum(running, part)
+            if item is not None:
+                weight = jnp.exp2(scores[start : start + key_n, :] - top).astype(BF16)
                 part = jnp.dot(
-                    key_ref[head // per_half, start : start + key_n, :],
-                    query,
-                    preferred_element_type=F32,
+                    value_ref[head, :, start : start + key_n], weight, preferred_element_type=F32
                 )
-                scores[start : start + key_n, :] = part
-                top = jnp.maximum(top, jnp.max(part, axis=0, keepdims=True))
-            for start in range(0, token_n, key_n):
-                weights[start : start + key_n, :] = jnp.exp2(
-                    scores[start : start + key_n, :] - top
-                ).astype(BF16)
-            mixed = jnp.dot(value_ref[head], weights[...], preferred_element_type=F32)
-            result = mixed[:HEAD_SIZE] / mixed[HEAD_SIZE : HEAD_SIZE + 1]
-            attended[head * HEAD_SIZE : (head + 1) * HEAD_SIZE, pl.ds(base, width)] = result
-            return carry
-
-        lax.fori_loop(0, query_n // width, one, 0)
-    mixture = jnp.dot(outer_ref[0], attended[...].astype(BF16), preferred_element_type=F32)
-    mixture = (mixture + projected_ref[...]).astype(BF16)
-    outer = jnp.dot(outer_ref[1], mixture, preferred_element_type=F32)
-    block_two = (block_ref[...].astype(F32) + outer).astype(BF16)
+                mixed = part if mixed is None else mixed + part
+        tops_ahead[...] = running
+        if item is not None:
+            row = pl.multiple_of(head * HEAD_SIZE, 8)
+            attended[pl.ds(row, HEAD_SIZE), pl.ds(base, width)] = (
+                mixed[:HEAD_SIZE] / mixed[HEAD_SIZE : HEAD_SIZE + 1]
+            )
+
+    even, odd = slots[0:2], slots[2:4]
+    step(None, None, None, 0, *even)
+
+    def two(index, carry):
+        step(2 * index, *even, 2 * index + 1, *odd)
+        step(2 * index + 1, *odd, jnp.minimum(2 * index + 2, items - 1), *even)
+        return carry
+
+    lax.fori_loop(0, items // 2, two, 0)
+
+
+def report(block_two, breadth, first, block_two_ref, sums_ref, squares_ref, packed_ref):
+    query_n = block_two.shape[1]
     block_two_ref[...] = block_two
     wide = block_two.astype(F32)
     sums = lane_sums(wide)
     squares = lane_sums(wide * wide)
     sums_ref[...] = sums
     squares_ref[...] = squares
-    edge = jnp.where(space_ref[0] == 0, wide[:, query_n - breadth :], wide[:, :breadth])
-    columns = [edge.astype(BF16)]
-    columns += exact_parts(jnp.sum(sums, axis=1, keepdims=True))
+    edge = jnp.where(first, wide[:, query_n - breadth :], wide[:, :breadth])
+    columns = exact_parts(jnp.sum(sums, axis=1, keepdims=True))
     columns += exact_parts(jnp.sum(squares, axis=1, keepdims=True))
     lane = lax.broadcasted_iota(jnp.int32, packed_ref.shape, 1)
     packed = jnp.zeros(packed_ref.shape, F32)
-    for index, part in enumerate(columns[1:]):
+    for index, part in enumerate(columns):
         packed = jnp.where(lane == breadth + index, part.astype(F32), packed)
     packed_ref[...] = packed.astype(BF16)
-    packed_ref[:, :breadth] = columns[0]
+    packed_ref[:, :breadth] = edge.astype(BF16)
 
 
 def closing_kernel(
@@ -637,7 +650,8 @@
         [
             pltpu.VMEM((deep, width_one), BF16),
             pltpu.VMEM((chan_n, width_one), BF16),
-            pltpu.VMEM((9 * chan_n, token_n), BF16),
+            pltpu.VMEM((3 * chan_n, token_n), BF16),
+            pltpu.VMEM((3 * chan_n, token_n + 2 * breadth), BF16),
             pltpu.VMEM((chan_n, 128), F32),
             pltpu.VMEM((chan_n, 128), F32),
             pltpu.VMEM((temb_n, 128), F32),
@@ -648,41 +662,29 @@
     count_two = len(pieces_two)
     half = HEADS // 2 * HEAD_SIZE
     args = (origin, space_id, middle, sums, squares, start, gains, *pieces_two)
-    block, projected, query, key, value, outer = kernel_call(
+    width = min(512, query_n)
+    block_two, sums, squares, packed = kernel_call(
         lambda *refs: second_kernel(count_two, rows, breadth, *refs),
-        [
-            shape((chan_n, query_n), BF16),
-            shape((chan_n, query_n), F32),
-            shape((HEADS, half, query_n), BF16),
-            shape((2, token_n, half), BF16),
-            shape((HEADS, HEAD_SIZE + 8, token_n), BF16),
-            shape((2, chan_n, chan_n), BF16),
-        ],
+        [shape((chan_n, query_n), BF16)] + moments + [shape((chan_n, 128), BF16)],
         [
             pltpu.VMEM((deep, width_two), BF16),
             pltpu.VMEM((chan_n, width_two), BF16),
-            pltpu.VMEM((9 * chan_n, token_n), BF16),
+            pltpu.VMEM((3 * chan_n, token_n), BF16),
+            pltpu.VMEM((3 * chan_n, token_n + 2 * breadth), BF16),
             pltpu.VMEM((chan_n, 128), F32),
             pltpu.VMEM((chan_n, 128), F32),
             pltpu.VMEM((chan_n, 128), F32),
             pltpu.VMEM((chan_n, 128), F32),
             pltpu.VMEM((chan_n, token_n), BF16),
             pltpu.VMEM((chan_n, token_n), BF16),
-        ],
+            pltpu.VMEM((HEADS, half, query_n), BF16),
+            pltpu.VMEM((2, token_n, half), BF16),
+            pltpu.VMEM((HEADS, HEAD_SIZE + 8, token_n), BF16),
+            pltpu.VMEM((chan_n, query_n), F32),
+        ]
+        + [pltpu.VMEM((token_n, width), F32), pltpu.VMEM((8, width), F32)] * 2,
         2,
     )(*args)
-
-    block_w = min(256, query_n)
-    block_two, sums, squares, packed = kernel_call(
-        lambda *refs: attention_kernel(breadth, *refs),
-        [shape((chan_n, query_n), BF16)] + moments + [shape((chan_n, 128), BF16)],
-        [
-            pltpu.VMEM((token_n, block_w), F32),
-            pltpu.VMEM((token_n, block_w), BF16),
-            pltpu.VMEM((chan_n, query_n), F32),
-        ],
-        1,
-    )(space_id, query, key, value, projected, block, outer)
 
     if space_n == 2:
         above = below = lax.ppermute(packed, "space", [(0, 1), (1, 0)])

time: 158 us -> 132 us (0.84)
  Pallas kernels: 103 us -> 75.8 us
    pallas_call x8 -> x7, Pallas kernels: 103 us -> 75.8 us  [call(): pl.pallas_call(body, out_shape=out_shape, in_specs=[smem] * scalars + [vm...]
    unnamed x50 -> x46, local copies, waits for them, and re-layouts: 3.81 us -> 3.81 us
  transfers between devices with their start and end apart: 19 -> 19, of which waited for: 7 -> 7; matrix products, arithmetic and copies ran while one was open for 3% -> 4% of each run, Pallas kernels for 16% -> 19%
where the time goes in v2:
time: 132 us
  Pallas kernels  75.8 us (57%)
  waiting for transfers between devices  20 us (15%)
  starting transfers between devices  17.9 us (14%)
  local copies, waits for them, and re-layouts  8.99 us (7%)
  blocking collectives  4.5 us (3%)
  between operations  2.32 us (2%)
  other arithmetic  1.97 us (1%)
    pallas_call x7, Pallas kernels, call(): pl.pallas_call(body, out_shape=out_shape, in_specs=[smem] * scalars + [vm...  75.8 us
    ppermute x6, waiting for transfers between devices, gather_shards(): moving = [lax.ppermute(pair, 'batch', onward) for pair in moving]  12.9 us
    ppermute x6, starting transfers between devices, gather_shards(): moving = [lax.ppermute(pair, 'batch', onward) for pair in moving]  10.9 us
    all_gather x1, blocking collectives, early(): noisy = lax.all_gather(noisy, 'space', axis=0, tiled=True)  4.5 us
    ppermute x2, waiting for transfers between devices, gather_shards(): last = lax.ppermute(pair[:rows], 'batch', onward)  3.87 us
    unnamed x46, local copies, waits for them, and re-layouts  3.81 us
    ppermute x2, starting transfers between devices, gather_shards(): last = lax.ppermute(pair[:rows], 'batch', onward)  3.44 us
    ppermute x1, waiting for transfers between devices, body(): above = below = lax.ppermute(packed, 'space', [(0, 1), (1, 0)])  3.12 us
  transfers between devices with their start and end apart: 19, of which 7 were waited for; matrix products, arithmetic and copies ran while one was open for 4% of the time, Pallas kernels for 19%

profile of v2, /device:TPU:0, one launch (start us, length us, event | category | flops | bytes accessed | tf_op | source)
XLA Modules:
  0.0 131.5 jit_solution(12232564955942934818)
XLA Ops:
  0.0 2.0 %shard_map.217 = (bf16[20,5440]{1,0:T(8,128)(2,1)}, bf16[20,4800]{1,0:T(8,128)(2,1)}) custom-call(bf16[20,2880]{1,0:T(8,128)(2,1)} %bitcast.38, bf16[80,320]{1,0:T(8,128)(2,1)} %bitcast.41, bf16[20,1280]{1,0:T(8,128)(2,1)} %bitcast.42, bf16[20,2880]{1,0:T(8,128)(2,1)} %bitcast.39, bf16[20,320]{1,0:T(8,128)(2,1)} %bitcast.44, bf16[20,320]{1,0:T(8,128)(2,1)} %bitcast.45, ...), custom_call_target="tpu_custom_call" | custom-call | tf_op jit(solution)/shard_map/pallas_call | solution.py:557
  5.8 0.8 fusion
  6.7 0.7 copy-done.12
  7.3 1.8 %shard_map.219.refs_7_ = bf16[40,4800]{1,0:T(8,128)(2,1)} custom-call(bf16[20,4800]{1,0:T(8,128)(2,1)} %get-tuple-element.28.one_ref, bf16[20,4800]{1,0:T(8,128)(2,1)} %copy-done.12), custom_call_target="tpu_custom_call" | custom-call | tf_op jit(solution)/shard_map/pallas_call | solution.py:557
  9.2 3.0 %collective-permute-start.3 = (bf16[40,4800]{1,0:T(8,128)(2,1)}, bf16[40,4800]{1,0:T(8,128)(2,1)S(1)}, u32[]{:S(2)}, u32[]{:S(2)}) collective-permute-start(bf16[40,4800]{1,0:T(8,128)(2,1)} %shard_map.219.refs_7_), channel_id=1, source_target_pairs={{0,8},{2,6},{8,16},{10,2},{16,24},{18,10},{24,28},{26,18},{28,20},... | collective-permute-start | bytes 1152008 | tf_op jit(solution)/shard_map/ppermute | solution.py:87
  12.2 0.7 copy-done.11
  12.9 1.8 %shard_map.218.refs_7_ = bf16[40,5440]{1,0:T(8,128)(2,1)} custom-call(bf16[20,5440]{1,0:T(8,128)(2,1)} %get-tuple-element.27.one_ref, bf16[20,5440]{1,0:T(8,128)(2,1)} %copy-done.11), custom_call_target="tpu_custom_call" | custom-call | tf_op jit(solution)/shard_map/pallas_call | solution.py:557
  14.8 1.6 %collective-permute-start.1 = (bf16[40,5440]{1,0:T(8,128)(2,1)}, bf16[40,5440]{1,0:T(8,128)(2,1)S(1)}, u32[]{:S(2)}, u32[]{:S(2)}) collective-permute-start(bf16[40,5440]{1,0:T(8,128)(2,1)} %shard_map.218.refs_7_), channel_id=1, source_target_pairs={{0,8},{2,6},{8,16},{10,2},{16,24},{18,10},{24,28},{26,18},{28,20},... | collective-permute-start | bytes 1305608 | tf_op jit(solution)/shard_map/ppermute | solution.py:87
  16.4 1.2 dynamic-slice_bitcast_fusion.refs_0_
  18.6 4.5 %all_gather.3.refs_0_ = bf16[32,4,64]{2,1,0:T(4,128)(2,1)} all-gather(bf16[16,4,64]{2,1,0:T(4,128)(2,1)S(1)} %fusion), channel_id=1, replica_groups=mesh['batch'=16,'space'=2] {'space'}, dimensions={0}, use_global_device_ids=true | all-gather | bytes 24576 | tf_op jit(solution)/shard_map/all_gather | solution.py:624
  23.1 2.9 %shard_map.220 = (bf16[320,2048]{1,0:T(8,128)(2,1)}, f32[320,128]{1,0:T(8,128)}, f32[320,128]{1,0:T(8,128)}) custom-call(bf16[32,4,64]{2,1,0:T(4,128)(2,1)} %all_gather.3.refs_0_, bf16[320,48]{1,0:T(8,128)(2,1)} %pad.12.refs_1_), custom_call_target="tpu_custom_call" | custom-call | tf_op jit(solution)/shard_map/pallas_call | solution.py:557
  26.8 0.9 broadcast_in_dim.11.refs_5_
  28.3 1.6 %collective-permute-start.5 = (bf16[40,5440]{1,0:T(8,128)(2,1)S(1)}, bf16[40,5440]{1,0:T(8,128)(2,1)S(1)}, u32[]{:S(2)}, u32[]{:S(2)}) collective-permute-start(bf16[40,5440]{1,0:T(8,128)(2,1)S(1)} %collective-permute-done.1.refs_8_), channel_id=1, source_target_pairs={{0,8},{2,6},{8,16},{10,2},{16,24},{18,10},{24,28},{26,18},{28,20},... | collective-permute-start | bytes 1305608 | tf_op jit(solution)/shard_map/ppermute | solution.py:87
  29.9 1.5 %collective-permute-start.12 = (bf16[40,4800]{1,0:T(8,128)(2,1)S(1)}, bf16[40,4800]{1,0:T(8,128)(2,1)}, u32[]{:S(2)}, u32[]{:S(2)}) collective-permute-start(bf16[40,4800]{1,0:T(8,128)(2,1)S(1)} %collective-permute-done.3.refs_8_), channel_id=1, source_target_pairs={{0,8},{2,6},{8,16},{10,2},{16,24},{18,10},{24,28},{26,18},{28,20},... | collective-permute-start | bytes 1152008 | tf_op jit(solution)/shard_map/ppermute | solution.py:87
  31.4 5.2 %collective-permute-done.5.refs_10_ = bf16[40,5440]{1,0:T(8,128)(2,1)S(1)} collective-permute-done((bf16[40,5440]{1,0:T(8,128)(2,1)S(1)}, bf16[40,5440]{1,0:T(8,128)(2,1)S(1)}, u32[]{:S(2)}, u32[]{:S(2)}) %collective-permute-start.5) | collective-permute-done | bytes 435232 | tf_op jit(solution)/shard_map/ppermute | solution.py:87
  36.6 1.6 %collective-permute-start.7 = (bf16[40,5440]{1,0:T(8,128)(2,1)S(1)}, bf16[40,5440]{1,0:T(8,128)(2,1)S(1)}, u32[]{:S(2)}, u32[]{:S(2)}) collective-permute-start(bf16[40,5440]{1,0:T(8,128)(2,1)S(1)} %collective-permute-done.5.refs_10_), channel_id=1, source_target_pairs={{0,8},{2,6},{8,16},{10,2},{16,24},{18,10},{24,28},{26,18},{28,20},... | collective-permute-start | bytes 1305608 | tf_op jit(solution)/shard_map/ppermute | solution.py:87
  38.2 2.7 %collective-permute-done.12.refs_10_ = bf16[40,4800]{1,0:T(8,128)(2,1)} collective-permute-done((bf16[40,4800]{1,0:T(8,128)(2,1)S(1)}, bf16[40,4800]{1,0:T(8,128)(2,1)}, u32[]{:S(2)}, u32[]{:S(2)}) %collective-permute-start.12) | collective-permute-done | bytes 384032 | tf_op jit(solution)/shard_map/ppermute | solution.py:87
  40.8 1.6 %collective-permute-start.14 = (bf16[40,4800]{1,0:T(8,128)(2,1)}, bf16[40,4800]{1,0:T(8,128)(2,1)S(1)}, u32[]{:S(2)}, u32[]{:S(2)}) collective-permute-start(bf16[40,4800]{1,0:T(8,128)(2,1)} %collective-permute-done.12.refs_10_), channel_id=1, source_target_pairs={{0,8},{2,6},{8,16},{10,2},{16,24},{18,10},{24,28},{26,18},{28,20},... | collective-permute-start | bytes 1152008 | tf_op jit(solution)/shard_map/ppermute | solution.py:87
  42.9 2.5 %collective-permute-done.7.refs_12_ = bf16[40,5440]{1,0:T(8,128)(2,1)S(1)} collective-permute-done((bf16[40,5440]{1,0:T(8,128)(2,1)S(1)}, bf16[40,5440]{1,0:T(8,128)(2,1)S(1)}, u32[]{:S(2)}, u32[]{:S(2)}) %collective-permute-start.7) | collective-permute-done | bytes 435232 | tf_op jit(solution)/shard_map/ppermute | solution.py:87
  45.5 1.6 %collective-permute-start.9 = (bf16[20,5440]{1,0:T(8,128)(2,1)S(1)}, bf16[20,5440]{1,0:T(8,128)(2,1)S(1)}, u32[]{:S(2)}, u32[]{:S(2)}) collective-permute-start(bf16[20,5440]{1,0:T(8,128)(2,1)S(1)} %slice.22), channel_id=1, source_target_pairs={{0,8},{2,6},{8,16},{10,2},{16,24},{18,10},{24,28},{26,18},{28,20},... | collective-permute-start | bytes 652808 | tf_op jit(solution)/shard_map/ppermute | solution.py:94
  47.1 2.5 %collective-permute-done.14.refs_12_ = bf16[40,4800]{1,0:T(8,128)(2,1)S(1)} collective-permute-done((bf16[40,4800]{1,0:T(8,128)(2,1)}, bf16[40,4800]{1,0:T(8,128)(2,1)S(1)}, u32[]{:S(2)}, u32[]{:S(2)}) %collective-permute-start.14) | collective-permute-done | bytes 384032 | tf_op jit(solution)/shard_map/ppermute | solution.py:87
  49.6 1.8 %collective-permute-start.16 = (bf16[20,4800]{1,0:T(8,128)(2,1)S(1)}, bf16[20,4800]{1,0:T(8,128)(2,1)}, u32[]{:S(2)}, u32[]{:S(2)}) collective-permute-start(bf16[20,4800]{1,0:T(8,128)(2,1)S(1)} %slice.23), channel_id=1, source_target_pairs={{0,8},{2,6},{8,16},{10,2},{16,24},{18,10},{24,28},{26,18},{28,20},... | collective-permute-start | bytes 576008 | tf_op jit(solution)/shard_map/ppermute | solution.py:94
  51.5 1.0 collective-permute-done.9.refs_14_
  53.2 2.9 %collective-permute-done.16.refs_14_ = bf16[20,4800]{1,0:T(8,128)(2,1)} collective-permute-done((bf16[20,4800]{1,0:T(8,128)(2,1)S(1)}, bf16[20,4800]{1,0:T(8,128)(2,1)}, u32[]{:S(2)}, u32[]{:S(2)}) %collective-permute-start.16) | collective-permute-done | bytes 192032 | tf_op jit(solution)/shard_map/ppermute | solution.py:94
  56.1 0.7 copy-done.10
  57.3 0.8 copy.36.refs_4_.refs_6_.refs_7_
  58.1 0.8 copy-done.6
  58.9 18.8 %shard_map.221 = (bf16[320,2048]{1,0:T(8,128)(2,1)}, f32[320,128]{1,0:T(8,128)}, f32[320,128]{1,0:T(8,128)}) custom-call(s32[16]{0:T(128)} %dynamic-slice_bitcast_fusion.refs_0_, bf16[320,2048]{1,0:T(8,128)(2,1)} %get-tuple-element.33.refs_1_.refs_5_, f32[320,128]{1,0:T(8,128)} %get-tuple-element.34.refs_2_, f32[320,128]{1,0:T(8,128)} %get-tuple-element.35.refs_3_, ...), custom_call_target="tpu_custom_call" | custom-call | tf_op jit(solution)/shard_map/pallas_call | solution.py:557
  77.8 44.4 %shard_map.222 = (bf16[320,1024]{1,0:T(8,128)(2,1)}, f32[320,128]{1,0:T(8,128)}, f32[320,128]{1,0:T(8,128)}, bf16[320,128]{1,0:T(8,128)(2,1)}) custom-call(s32[16]{0:T(128)} %dynamic-slice_bitcast_fusion.refs_0_, s32[1]{0:T(128)} %bitcast.refs_1_.refs_0_, bf16[320,2048]{1,0:T(8,128)(2,1)} %get-tuple-element.40.refs_2_, ...), custom_call_target="tpu_custom_call" | custom-call | tf_op jit(solution)/shard_map/pallas_call | solution.py:557
  122.2 1.5 %collective-permute-start.18 = (bf16[320,128]{1,0:T(8,128)(2,1)}, bf16[320,128]{1,0:T(8,128)(2,1)S(1)}, u32[]{:S(2)}, u32[]{:S(2)}) collective-permute-start(bf16[320,128]{1,0:T(8,128)(2,1)} %get-tuple-element.45), channel_id=1, source_target_pairs={{0,1},{1,0},{2,3},{3,2},{4,5},{5,4},{6,7},{7,6},{8,9},{9,8},{10,11... | collective-permute-start | bytes 245768 | tf_op jit(solution)/shard_map/ppermute | solution.py:690
  123.7 3.1 %collective-permute-done.18.refs_3_.refs_4_ = bf16[320,128]{1,0:T(8,128)(2,1)S(1)} collective-permute-done((bf16[320,128]{1,0:T(8,128)(2,1)}, bf16[320,128]{1,0:T(8,128)(2,1)S(1)}, u32[]{:S(2)}, u32[]{:S(2)}) %collective-permute-start.18) | collective-permute-done | bytes 81952 | tf_op jit(solution)/shard_map/ppermute | solution.py:690
  127.5 4.0 %shard_map.223 = f32[16,4,64]{2,1,0:T(4,128)} custom-call(s32[1]{0:T(128)} %bitcast.refs_1_.refs_0_, f32[1]{0:T(128)} %bitcast.4.refs_1_, bf16[320,1024]{1,0:T(8,128)(2,1)} %get-tuple-element.44.refs_2_, bf16[320,128]{1,0:T(8,128)(2,1)} %copy-done.8, bf16[320,128]{1,0:T(8,128)(2,1)} %copy-done.8, f32[320,128]{1,0:T(8,128)} %get-tuple-element.46.refs_5_, ...), custom_call_target="tpu_custom_call" | custom-call | tf_op jit(solution)/shard_map/pallas_call | solution.py:557
  (87 shorter events, 6.6 us)
Async XLA Ops:
  0.0 17.6 %copy-start.13 = (bf16[36,320]{1,0:T(8,128)(2,1)S(1)}, bf16[36,320]{1,0:T(8,128)(2,1)}, u32[]{:S(2)}) copy-start(bf16[36,320]{1,0:T(8,128)(2,1)} %param.26) | copy-start | bytes 69124
  0.0 17.7 %copy-start.14 = (bf16[2880,4]{0,1:T(4,128)(2,1)S(1)}, bf16[2880,4]{0,1:T(4,128)(2,1)}, u32[]{:S(2)}) copy-start(bf16[2880,4]{0,1:T(4,128)(2,1)} %param.39) | copy-start | bytes 69124
  0.0 17.8 %copy-start.16 = (f32[320]{0:T(512)S(1)}, f32[320]{0:T(512)}, u32[]{:S(2)}) copy-start(f32[320]{0:T(512)} %param.40) | copy-start | bytes 3844
  0.0 17.9 %copy-start.17 = (f32[320]{0:T(512)S(1)}, f32[320]{0:T(512)}, u32[]{:S(2)}) copy-start(f32[320]{0:T(512)} %param.41) | copy-start | bytes 3844
  0.0 17.9 %copy-start.18 = (f32[320]{0:T(512)S(1)}, f32[320]{0:T(512)}, u32[]{:S(2)}) copy-start(f32[320]{0:T(512)} %param.42) | copy-start | bytes 3844
  0.0 17.9 %copy-start.19 = (f32[320]{0:T(512)S(1)}, f32[320]{0:T(512)}, u32[]{:S(2)}) copy-start(f32[320]{0:T(512)} %param.43) | copy-start | bytes 3844
  0.0 17.9 %copy-start.20 = (f32[320]{0:T(512)S(1)}, f32[320]{0:T(512)}, u32[]{:S(2)}) copy-start(f32[320]{0:T(512)} %param.44) | copy-start | bytes 3844
  0.0 17.9 %copy-start.21 = (f32[320]{0:T(512)S(1)}, f32[320]{0:T(512)}, u32[]{:S(2)}) copy-start(f32[320]{0:T(512)} %param.30) | copy-start | bytes 3844
  2.0 4.6 %collective-permute-start.2 = (bf16[20,4800]{1,0:T(8,128)(2,1)}, bf16[20,4800]{1,0:T(8,128)(2,1)S(1)}, u32[]{:S(2)}, u32[]{:S(2)}) collective-permute-start(bf16[20,4800]{1,0:T(8,128)(2,1)} %get-tuple-element.28.one_ref), channel_id=1, source_target_pairs={{0,2},{2,0},{4,6},{6,4},{8,10},{10,8},{12,14},{14,12},{16,18},{18,... | collective-permute-start | bytes 576008 | tf_op jit(solution)/shard_map/ppermute | solution.py:81
  2.5 9.7 %collective-permute-start = (bf16[20,5440]{1,0:T(8,128)(2,1)}, bf16[20,5440]{1,0:T(8,128)(2,1)S(1)}, u32[]{:S(2)}, u32[]{:S(2)}) collective-permute-start(bf16[20,5440]{1,0:T(8,128)(2,1)} %get-tuple-element.27.one_ref), channel_id=1, source_target_pairs={{0,2},{2,0},{4,6},{6,4},{8,10},{10,8},{12,14},{14,12},{16,18},{18,... | collective-permute-start | bytes 652808 | tf_op jit(solution)/shard_map/ppermute | solution.py:81
  6.6 21.0 %copy-start.15 = (f32[1280]{0:T(1024)S(1)}, f32[1280]{0:T(1024)}, u32[]{:S(2)}) copy-start(f32[1280]{0:T(1024)} %param.28) | copy-start | bytes 15364
  9.2 17.6 %collective-permute-start.3 = (bf16[40,4800]{1,0:T(8,128)(2,1)}, bf16[40,4800]{1,0:T(8,128)(2,1)S(1)}, u32[]{:S(2)}, u32[]{:S(2)}) collective-permute-start(bf16[40,4800]{1,0:T(8,128)(2,1)} %shard_map.219.refs_7_), channel_id=1, source_target_pairs={{0,8},{2,6},{8,16},{10,2},{16,24},{18,10},{24,28},{26,18},{28,20},... | collective-permute-start | bytes 1152008 | tf_op jit(solution)/shard_map/ppermute | solution.py:87
  14.8 12.0 %collective-permute-start.1 = (bf16[40,5440]{1,0:T(8,128)(2,1)}, bf16[40,5440]{1,0:T(8,128)(2,1)S(1)}, u32[]{:S(2)}, u32[]{:S(2)}) collective-permute-start(bf16[40,5440]{1,0:T(8,128)(2,1)} %shard_map.218.refs_7_), channel_id=1, source_target_pairs={{0,8},{2,6},{8,16},{10,2},{16,24},{18,10},{24,28},{26,18},{28,20},... | collective-permute-start | bytes 1305608 | tf_op jit(solution)/shard_map/ppermute | solution.py:87
  26.8 51.0 %copy-start.7 = (bf16[40,4800]{1,0:T(8,128)(2,1)}, bf16[40,4800]{1,0:T(8,128)(2,1)S(1)}, u32[]{:S(2)}) copy-start(bf16[40,4800]{1,0:T(8,128)(2,1)S(1)} %collective-permute-done.3.refs_8_) | copy-start | bytes 1152004
  26.8 31.3 %copy-start.2 = (bf16[40,5440]{1,0:T(8,128)(2,1)}, bf16[40,5440]{1,0:T(8,128)(2,1)S(1)}, u32[]{:S(2)}) copy-start(bf16[40,5440]{1,0:T(8,128)(2,1)S(1)} %collective-permute-done.1.refs_8_) | copy-start | bytes 1305604
  28.3 8.3 %collective-permute-start.5 = (bf16[40,5440]{1,0:T(8,128)(2,1)S(1)}, bf16[40,5440]{1,0:T(8,128)(2,1)S(1)}, u32[]{:S(2)}, u32[]{:S(2)}) collective-permute-start(bf16[40,5440]{1,0:T(8,128)(2,1)S(1)} %collective-permute-done.1.refs_8_), channel_id=1, source_target_pairs={{0,8},{2,6},{8,16},{10,2},{16,24},{18,10},{24,28},{26,18},{28,20},... | collective-permute-start | bytes 1305608 | tf_op jit(solution)/shard_map/ppermute | solution.py:87
  29.9 11.0 %collective-permute-start.12 = (bf16[40,4800]{1,0:T(8,128)(2,1)S(1)}, bf16[40,4800]{1,0:T(8,128)(2,1)}, u32[]{:S(2)}, u32[]{:S(2)}) collective-permute-start(bf16[40,4800]{1,0:T(8,128)(2,1)S(1)} %collective-permute-done.3.refs_8_), channel_id=1, source_target_pairs={{0,8},{2,6},{8,16},{10,2},{16,24},{18,10},{24,28},{26,18},{28,20},... | collective-permute-start | bytes 1152008 | tf_op jit(solution)/shard_map/ppermute | solution.py:87
  36.6 21.5 %copy-start.3 = (bf16[40,5440]{1,0:T(8,128)(2,1)}, bf16[40,5440]{1,0:T(8,128)(2,1)S(1)}, u32[]{:S(2)}) copy-start(bf16[40,5440]{1,0:T(8,128)(2,1)S(1)} %collective-permute-done.5.refs_10_) | copy-start | bytes 1305604
  36.6 8.9 %collective-permute-start.7 = (bf16[40,5440]{1,0:T(8,128)(2,1)S(1)}, bf16[40,5440]{1,0:T(8,128)(2,1)S(1)}, u32[]{:S(2)}, u32[]{:S(2)}) collective-permute-start(bf16[40,5440]{1,0:T(8,128)(2,1)S(1)} %collective-permute-done.5.refs_10_), channel_id=1, source_target_pairs={{0,8},{2,6},{8,16},{10,2},{16,24},{18,10},{24,28},{26,18},{28,20},... | collective-permute-start | bytes 1305608 | tf_op jit(solution)/shard_map/ppermute | solution.py:87
  40.8 8.8 %collective-permute-start.14 = (bf16[40,4800]{1,0:T(8,128)(2,1)}, bf16[40,4800]{1,0:T(8,128)(2,1)S(1)}, u32[]{:S(2)}, u32[]{:S(2)}) collective-permute-start(bf16[40,4800]{1,0:T(8,128)(2,1)} %collective-permute-done.12.refs_10_), channel_id=1, source_target_pairs={{0,8},{2,6},{8,16},{10,2},{16,24},{18,10},{24,28},{26,18},{28,20},... | collective-permute-start | bytes 1152008 | tf_op jit(solution)/shard_map/ppermute | solution.py:87
  42.4 10.0 %collective-permute-start.4 = (bf16[40,5440]{1,0:T(8,128)(2,1)S(1)}, bf16[40,5440]{1,0:T(8,128)(2,1)S(1)}, u32[]{:S(2)}, u32[]{:S(2)}) collective-permute-start(bf16[40,5440]{1,0:T(8,128)(2,1)S(1)} %collective-permute-done.1.refs_8_), channel_id=1, source_target_pairs={{0,2},{2,0},{4,6},{6,4},{8,10},{10,8},{12,14},{14,12},{16,18},{18,... | collective-permute-start | bytes 1305608 | tf_op jit(solution)/shard_map/ppermute | solution.py:92
  42.4 10.6 %collective-permute-start.6 = (bf16[40,5440]{1,0:T(8,128)(2,1)S(1)}, bf16[40,5440]{1,0:T(8,128)(2,1)S(1)}, u32[]{:S(2)}, u32[]{:S(2)}) collective-permute-start(bf16[40,5440]{1,0:T(8,128)(2,1)S(1)} %collective-permute-done.5.refs_10_), channel_id=1, source_target_pairs={{0,2},{2,0},{4,6},{6,4},{8,10},{10,8},{12,14},{14,12},{16,18},{18,... | collective-permute-start | bytes 1305608 | tf_op jit(solution)/shard_map/ppermute | solution.py:92
  45.5 7.0 %collective-permute-start.9 = (bf16[20,5440]{1,0:T(8,128)(2,1)S(1)}, bf16[20,5440]{1,0:T(8,128)(2,1)S(1)}, u32[]{:S(2)}, u32[]{:S(2)}) collective-permute-start(bf16[20,5440]{1,0:T(8,128)(2,1)S(1)} %slice.22), channel_id=1, source_target_pairs={{0,8},{2,6},{8,16},{10,2},{16,24},{18,10},{24,28},{26,18},{28,20},... | collective-permute-start | bytes 652808 | tf_op jit(solution)/shard_map/ppermute | solution.py:94
  49.6 28.1 %copy-start.1 = (bf16[40,4800]{1,0:T(8,128)(2,1)}, bf16[40,4800]{1,0:T(8,128)(2,1)S(1)}, u32[]{:S(2)}) copy-start(bf16[40,4800]{1,0:T(8,128)(2,1)S(1)} %collective-permute-done.14.refs_12_) | copy-start | bytes 1152004
  49.6 6.4 %collective-permute-start.16 = (bf16[20,4800]{1,0:T(8,128)(2,1)S(1)}, bf16[20,4800]{1,0:T(8,128)(2,1)}, u32[]{:S(2)}, u32[]{:S(2)}) collective-permute-start(bf16[20,4800]{1,0:T(8,128)(2,1)S(1)} %slice.23), channel_id=1, source_target_pairs={{0,8},{2,6},{8,16},{10,2},{16,24},{18,10},{24,28},{26,18},{28,20},... | collective-permute-start | bytes 576008 | tf_op jit(solution)/shard_map/ppermute | solution.py:94
  51.5 6.6 %collective-permute-start.8 = (bf16[40,5440]{1,0:T(8,128)(2,1)S(1)}, bf16[40,5440]{1,0:T(8,128)(2,1)S(1)}, u32[]{:S(2)}, u32[]{:S(2)}) collective-permute-start(bf16[40,5440]{1,0:T(8,128)(2,1)S(1)} %collective-permute-done.7.refs_12_), channel_id=1, source_target_pairs={{0,2},{2,0},{4,6},{6,4},{8,10},{10,8},{12,14},{14,12},{16,18},{18,... | collective-permute-start | bytes 1305608 | tf_op jit(solution)/shard_map/ppermute | solution.py:92
  52.5 3.6 %collective-permute-start.10 = (bf16[20,5440]{1,0:T(8,128)(2,1)S(1)}, bf16[20,5440]{1,0:T(8,128)(2,1)S(1)}, u32[]{:S(2)}, u32[]{:S(2)}) collective-permute-start(bf16[20,5440]{1,0:T(8,128)(2,1)S(1)} %collective-permute-done.9.refs_14_), channel_id=1, source_target_pairs={{0,2},{2,0},{4,6},{6,4},{8,10},{10,8},{12,14},{14,12},{16,18},{18,... | collective-permute-start | bytes 652808 | tf_op jit(solution)/shard_map/ppermute | solution.py:95
  52.5 25.2 %collective-permute-start.11 = (bf16[40,4800]{1,0:T(8,128)(2,1)S(1)}, bf16[40,4800]{1,0:T(8,128)(2,1)}, u32[]{:S(2)}, u32[]{:S(2)}) collective-permute-start(bf16[40,4800]{1,0:T(8,128)(2,1)S(1)} %collective-permute-done.3.refs_8_), channel_id=1, source_target_pairs={{0,2},{2,0},{4,6},{6,4},{8,10},{10,8},{12,14},{14,12},{16,18},{18,... | collective-permute-start | bytes 1152008 | tf_op jit(solution)/shard_map/ppermute | solution.py:92
  53.0 24.7 %collective-permute-start.13 = (bf16[40,4800]{1,0:T(8,128)(2,1)}, bf16[40,4800]{1,0:T(8,128)(2,1)}, u32[]{:S(2)}, u32[]{:S(2)}) collective-permute-start(bf16[40,4800]{1,0:T(8,128)(2,1)} %collective-permute-done.12.refs_10_), channel_id=1, source_target_pairs={{0,2},{2,0},{4,6},{6,4},{8,10},{10,8},{12,14},{14,12},{16,18},{18,... | collective-permute-start | bytes 1152008 | tf_op jit(solution)/shard_map/ppermute | solution.py:92
  56.1 21.7 %collective-permute-start.15 = (bf16[40,4800]{1,0:T(8,128)(2,1)S(1)}, bf16[40,4800]{1,0:T(8,128)(2,1)}, u32[]{:S(2)}, u32[]{:S(2)}) collective-permute-start(bf16[40,4800]{1,0:T(8,128)(2,1)S(1)} %collective-permute-done.14.refs_12_), channel_id=1, source_target_pairs={{0,2},{2,0},{4,6},{6,4},{8,10},{10,8},{12,14},{14,12},{16,18},{18,... | collective-permute-start | bytes 1152008 | tf_op jit(solution)/shard_map/ppermute | solution.py:92
  56.8 21.0 %collective-permute-start.17 = (bf16[20,4800]{1,0:T(8,128)(2,1)}, bf16[20,4800]{1,0:T(8,128)(2,1)}, u32[]{:S(2)}, u32[]{:S(2)}) collective-permute-start(bf16[20,4800]{1,0:T(8,128)(2,1)} %collective-permute-done.16.refs_14_), channel_id=1, source_target_pairs={{0,2},{2,0},{4,6},{6,4},{8,10},{10,8},{12,14},{14,12},{16,18},{18,... | collective-permute-start | bytes 576008 | tf_op jit(solution)/shard_map/ppermute | solution.py:95
  122.2 4.7 %collective-permute-start.18 = (bf16[320,128]{1,0:T(8,128)(2,1)}, bf16[320,128]{1,0:T(8,128)(2,1)S(1)}, u32[]{:S(2)}, u32[]{:S(2)}) collective-permute-start(bf16[320,128]{1,0:T(8,128)(2,1)} %get-tuple-element.45), channel_id=1, source_target_pairs={{0,1},{1,0},{2,3},{3,2},{4,5},{5,4},{6,7},{7,6},{8,9},{9,8},{10,11... | collective-permute-start | bytes 245768 | tf_op jit(solution)/shard_map/ppermute | solution.py:690
  (9 other events, 27.7 us)

commit v3 on v2

--- a/solution.py
+++ b/solution.py
@@ -6,6 +6,7 @@
 from jax.experimental import pallas as pl
 from jax.experimental.pallas import tpu as pltpu
 from jax.sharding import PartitionSpec as P
+
 
 HEADS = 8
 HEAD_SIZE = 40
@@ -16,6 +17,7 @@
 EPS_LAYER = 1e-05
 VMEM_BYTES = 60 << 20
 RING_LIMIT = 16
+UNROLL = 2
 F32 = jnp.float32
 BF16 = jnp.bfloat16
 
@@ -71,29 +73,38 @@
     return onward, sibling, half, table
 
 
-def gather_shards(shards, beside):
+def gather_shards(urgent, patient, token, beside):
     count = lax.axis_size("batch")
     if count % 4 or count > RING_LIMIT:
-        whole = [[lax.all_gather(shard, "batch", axis=0, tiled=True)] for shard in shards]
-        return whole, jnp.arange(count, dtype=jnp.int32), beside()
+        whole = [[lax.all_gather(part, "batch", axis=0, tiled=True)] for part in (urgent, patient)]
+        return whole, jnp.arange(count, dtype=jnp.int32), [work(token) for work in beside]
     onward, sibling, half, table = batch_ring(count)
-    rows = shards[0].shape[0]
-    others = [lax.ppermute(shard, "batch", sibling) for shard in shards]
-    moving = [pair_up(shard, other) for shard, other in zip(shards, others)]
-    gathered = [[pair] for pair in moving]
-    table = jnp.asarray(table, dtype=jnp.int32)
-    extra = None
+    rows = urgent.shape[0]
+    others = [lax.ppermute(part, "batch", sibling) for part in (urgent, patient)]
+    first, second, token = pair_up(token, (urgent, patient), others)
+    origin = jnp.asarray(table, dtype=jnp.int32)[lax.axis_index("batch")]
+
+    moving = first
+    pieces_one = [moving]
+    for _ in range(1, half):
+        moving = lax.ppermute(moving, "batch", onward)
+        pieces_one += [moving, lax.ppermute(moving, "batch", sibling)]
+    last = lax.ppermute(moving[:rows], "batch", onward)
+    pieces_one += [last, lax.ppermute(last, "batch", sibling)]
+
+    moving = second
+    pieces_two = [moving]
+    extra = []
     for step in range(1, half):
-        moving = [lax.ppermute(pair, "batch", onward) for pair in moving]
-        if extra is None:
-            origin = table[lax.axis_index("batch")]
-            moving, origin, extra = lax.optimization_barrier((moving, origin, beside()))
-        for pieces, pair in zip(gathered, moving):
-            pieces += [pair, lax.ppermute(pair, "batch", sibling)]
-    for pieces, pair in zip(gathered, moving):
-        last = lax.ppermute(pair[:rows], "batch", onward)
-        pieces += [last, lax.ppermute(last, "batch", sibling)]
-    return gathered, origin, extra
+        if step <= len(beside):
+            now = (beside[step - 1](token), origin)
+            moving, (now, origin) = lax.optimization_barrier((moving, now))
+            extra.append(now)
+        moving = lax.ppermute(moving, "batch", onward)
+        pieces_two += [moving, lax.ppermute(moving, "batch", sibling)]
+    extra += [work(token) for work in beside[half - 1 :]]
+    pieces_two.append(lax.ppermute(moving, "batch", onward))
+    return (pieces_one, pieces_two), origin, extra
 
 
 def lane_sums(value):
@@ -103,17 +114,39 @@
     return total
 
 
-def group_moments(sums, squares, number):
-    chan_n = sums.shape[0]
+def exact_parts(value):
+    high = value.astype(BF16).astype(F32)
+    rest = value - high
+    middle = rest.astype(BF16).astype(F32)
+    return [high, middle, rest - middle]
+
+
+def moment_columns(sums, squares, base):
+    parts = exact_parts(jnp.sum(sums, axis=1, keepdims=True))
+    parts += exact_parts(jnp.sum(squares, axis=1, keepdims=True))
+    lane = lax.broadcasted_iota(jnp.int32, sums.shape, 1)
+    columns = jnp.zeros(sums.shape, F32)
+    for index, part in enumerate(parts):
+        columns = jnp.where(lane == base + index, part, columns)
+    return columns
+
+
+def group_moments(columns, bases, number):
+    chan_n = columns.shape[0]
     size = chan_n // GROUPS
-    rows = lax.broadcasted_iota(jnp.int32, (chan_n, chan_n), 0) // size
-    cols = lax.broadcasted_iota(jnp.int32, (chan_n, chan_n), 1) // size
-    member = jnp.where(rows == cols, 1.0, 0.0).astype(F32)
-    both = jnp.concatenate([sums, squares], axis=1)
-    grouped = jnp.dot(member, both, preferred_element_type=F32, precision=lax.Precision.HIGHEST)
-    mean = jnp.sum(grouped[:, :128], axis=1, keepdims=True) / number
-    square = jnp.sum(grouped[:, 128:], axis=1, keepdims=True) / number
-    return mean, square
+    rows = lax.broadcasted_iota(jnp.int32, (chan_n, 1), 0) // size
+    cols = lax.broadcasted_iota(jnp.int32, (1, chan_n), 1) // size
+    member = jnp.where(rows == cols, 1.0, 0.0).astype(BF16)
+    grouped = jnp.dot(member, columns.astype(BF16), preferred_element_type=F32)
+    lane = lax.broadcasted_iota(jnp.int32, columns.shape, 1)
+    totals = []
+    for shift in (0, 3):
+        keep = lane < 0
+        for base in bases:
+            keep = keep | ((lane >= base + shift) & (lane < base + shift + 3))
+        kept = jnp.where(keep, grouped, 0.0)
+        totals.append(jnp.sum(kept, axis=1, keepdims=True) / number)
+    return totals
 
 
 def padded(rows):
@@ -167,7 +200,7 @@
             offset_ref[place, token_n:] = jnp.where(margin, head, 0.0).astype(BF16)
         return carry
 
-    lax.fori_loop(0, chan_n // chunk, one, 0)
+    lax.fori_loop(0, chan_n // chunk, one, 0, unroll=UNROLL)
 
 
 def convolve(weights, level_ref, offset_ref, breadth, start, block_n):
@@ -186,7 +219,8 @@
 
 
 def silu(value):
-    return value / (1.0 + jnp.exp(-value))
+    half = 0.5 * value
+    return half + half * jnp.tanh(half)
 
 
 def normal_taps(source_ref, level_ref, offset_ref, mean_ref, factor_ref, breadth):
@@ -200,21 +234,34 @@
 
 
 def set_moments(sums, squares, number, gain, epsilon, mean_ref, factor_ref):
-    mean, square = group_moments(sums, squares, number)
+    mean, square = group_moments(moment_columns(sums, squares, 0), (0,), number)
     factor = lax.rsqrt(square - mean * mean + epsilon) * gain
     mean_ref[...] = jnp.broadcast_to(mean, mean_ref.shape)
     factor_ref[...] = jnp.broadcast_to(factor, factor_ref.shape)
 
 
-def pair_kernel(one_ref, two_ref, out_ref):
-    rows = one_ref.shape[0]
-    out_ref[:rows] = one_ref[...]
-    out_ref[rows:] = two_ref[...]
-
-
-def pair_up(one, two):
-    whole = jax.ShapeDtypeStruct((2 * one.shape[0], one.shape[1]), one.dtype)
-    return kernel_call(pair_kernel, whole, [])(one, two)
+def pair_kernel(token_ref, *refs):
+    token_out, refs = refs[-1], refs[:-1]
+    token_out[0] = token_ref[0]
+    count = len(refs) // 3
+    for index in range(count):
+        one_ref, two_ref, out_ref = refs[index::count]
+        rows = one_ref.shape[0]
+        out_ref[:rows] = one_ref[...]
+        out_ref[rows:] = two_ref[...]
+
+
+def pair_up(token, ones, twos):
+    wholes = [jax.ShapeDtypeStruct((2 * one.shape[0], one.shape[1]), one.dtype) for one in ones]
+    smem = pl.BlockSpec(memory_space=pltpu.SMEM)
+    vmem = pl.BlockSpec(memory_space=pltpu.VMEM)
+    return pl.pallas_call(
+        pair_kernel,
+        out_shape=wholes + [jax.ShapeDtypeStruct(token.shape, token.dtype)],
+        in_specs=[smem] + [vmem] * (2 * len(ones)),
+        out_specs=[vmem] * len(ones) + [smem],
+        compiler_params=pltpu.CompilerParams(vmem_limit_bytes=VMEM_BYTES),
+    )(token, *ones, *twos)
 
 
 def pack_kernel(conv_first, time_first, time_second, conv_second, *rest):
@@ -284,6 +331,7 @@
     middle_ref, sums_out, squares_out = rest[counts : counts + 3]
     stage, weights, level, offset, mean, factor, hidden = rest[counts + 3 :]
     chan_n, token_n = start_ref.shape
+    gains = gains_ref[...].T
     number = token_n * (chan_n // GROUPS)
     assemble(origin_ref, pieces, stage, rows, weights)
     conv_width = 9 * chan_n
@@ -298,9 +346,9 @@
     second = weights[:, conv_width + temb_n : conv_width + 2 * temb_n]
     lifted = silu(silu(hidden[...] + bias_ref[...].T[:, 0:1])).astype(BF16)
     embedded = jnp.dot(second, lifted, preferred_element_type=F32)
-    embedded = embedded[:, 0:1] + gains_ref[:, 5:6]
+    embedded = embedded[:, 0:1] + gains[:, 5:6]
     set_moments(
-        sums_ref[...], squares_ref[...], number, gains_ref[:, 0:1], EPS_BLOCK, mean, factor
+        sums_ref[...], squares_ref[...], number, gains[:, 0:1], EPS_BLOCK, mean, factor
     )
     normal_taps(start_ref, level, offset, mean, factor, breadth)
     block_n = min(512, token_n)
@@ -337,6 +385,7 @@
     ]
     query_out, key_out, value_out = rest[counts + 14 : counts + 17]
     chan_n, token_n = middle_ref.shape
+    gains = gains_ref[...].T
     query_n = query_out.shape[2]
     number = token_n * (chan_n // GROUPS)
     assemble(origin_ref, pieces, stage, rows, weights)
@@ -347,7 +396,7 @@
         return weights[:, base : base + chan_n]
 
     set_moments(
-        sums_ref[...], squares_ref[...], number, gains_ref[:, 1:2], EPS_BLOCK, mean, factor
+        sums_ref[...], squares_ref[...], number, gains[:, 1:2], EPS_BLOCK, mean, factor
     )
     normal_taps(middle_ref, level, offset, mean, factor, breadth)
     block_n = min(512, token_n)
@@ -362,7 +411,7 @@
         else:
             sums[...] += lane_sums(wide)
             squares[...] += lane_sums(wide * wide)
-    set_moments(sums[...], squares[...], number, gains_ref[:, 2:3], EPS_GROUP, mean, factor)
+    set_moments(sums[...], squares[...], number, gains[:, 2:3], EPS_GROUP, mean, factor)
     own = pl.multiple_of(space_ref[0] * query_n, 128)
 
     def project(source):
@@ -374,7 +423,7 @@
         average = jnp.mean(projected, axis=0, keepdims=True)
         centred = projected - average
         spread = jnp.mean(centred * centred, axis=0, keepdims=True)
-        scaled = centred * lax.rsqrt(spread + EPS_LAYER) * gains_ref[:, 4:5]
+        scaled = centred * lax.rsqrt(spread + EPS_LAYER) * gains[:, 4:5]
         token = scaled.astype(BF16)
         tokens[:, start : start + block_n] = token
         value = jnp.dot(small(3), token, preferred_element_type=F32)
@@ -416,13 +465,6 @@
     report((mine.astype(F32) + outer).astype(BF16), breadth, space_ref[0] == 0, *outputs)
 
 
-def exact_parts(value):
-    high = value.astype(BF16)
-    rest = value - high.astype(F32)
-    middle = rest.astype(BF16)
-    return [high, middle, (rest - middle.astype(F32)).astype(BF16)]
-
-
 def attend(query_ref, key_ref, value_ref, attended, *slots):
     heads, _, query_n = query_ref.shape
     token_n = key_ref.shape[1]
@@ -480,13 +522,7 @@
     sums_ref[...] = sums
     squares_ref[...] = squares
     edge = jnp.where(first, wide[:, query_n - breadth :], wide[:, :breadth])
-    columns = exact_parts(jnp.sum(sums, axis=1, keepdims=True))
-    columns += exact_parts(jnp.sum(squares, axis=1, keepdims=True))
-    lane = lax.broadcasted_iota(jnp.int32, packed_ref.shape, 1)
-    packed = jnp.zeros(packed_ref.shape, F32)
-    for index, part in enumerate(columns):
-        packed = jnp.where(lane == breadth + index, part.astype(F32), packed)
-    packed_ref[...] = packed.astype(BF16)
+    packed_ref[...] = moment_columns(sums, squares, breadth).astype(BF16)
     packed_ref[:, :breadth] = edge.astype(BF16)
 
 
@@ -508,15 +544,16 @@
     active,
 ):
     chan_n, token_n = block_ref.shape
+    gains = gains_ref[...].T
     lat_n = noise_ref.shape[1]
-    sums, squares = sums_ref[...], squares_ref[...]
+    columns = moment_columns(sums_ref[...], squares_ref[...], 0)
+    bases = (0,)
     if space_n == 2:
-        lane = lax.broadcasted_iota(jnp.int32, sums.shape, 1)
-        peer = above_ref[...].astype(F32)
-        sums = sums + jnp.where((lane >= breadth) & (lane < breadth + 3), peer, 0.0)
-        squares = squares + jnp.where((lane >= breadth + 3) & (lane < breadth + 6), peer, 0.0)
-    mean, square = group_moments(sums, squares, number)
-    factor = lax.rsqrt(square - mean * mean + EPS_BLOCK) * gains_ref[:, 3:4]
+        lane = lax.broadcasted_iota(jnp.int32, columns.shape, 1)
+        columns = jnp.where(lane >= breadth, above_ref[...].astype(F32), columns)
+        bases = (0, breadth)
+    mean, square = group_moments(columns, bases, number)
+    factor = lax.rsqrt(square - mean * mean + EPS_BLOCK) * gains[:, 3:4]
 
     def act(value):
         return silu((value.astype(F32) - mean) * factor)
@@ -549,9 +586,10 @@
         out_ref[row] = weight * (part - noise_ref[row])
 
 
-def kernel_call(body, out_shape, scratch, scalars=0):
+def kernel_call(body, out_shape, scratch, scalars=0, flops=0):
     smem = pl.BlockSpec(memory_space=pltpu.SMEM)
     vmem = pl.BlockSpec(memory_space=pltpu.VMEM)
+    cost = pl.CostEstimate(flops=flops, transcendentals=0, bytes_accessed=0) if flops else None
 
     def call(*args):
         return pl.pallas_call(
@@ -560,6 +598,7 @@
             in_specs=[smem] * scalars + [vmem] * (len(args) - scalars),
             scratch_shapes=scratch,
             compiler_params=pltpu.CompilerParams(vmem_limit_bytes=VMEM_BYTES),
+            cost_estimate=cost,
         )(*args)
 
     return call
@@ -595,7 +634,6 @@
     rows = conv_first.shape[1]
     chan_n = inlet_conv.shape[1]
     temb_n = time_first_bias.shape[0]
-    many = temb_n // chan_n
     space_n = lax.axis_size("space")
     place = lax.axis_index("space")
     token_n = height * space_n * breadth
@@ -615,34 +653,45 @@
     moments = [shape((chan_n, 128), F32)] * 2
     taps_n = 9 * lat_n
     taps_pad = -(-taps_n // 16) * 16
-    alpha_bar = lookup(timesteps)
-
-    def early():
+
+    def early(steps):
+        alpha_bar = lookup(steps)
         alpha_here = alpha_bar[:, None, None, None]
         noisy = jnp.sqrt(alpha_here) * latents + jnp.sqrt(1.0 - alpha_here) * noise_draw
         noisy = noisy.astype(BF16)[0].transpose(0, 2, 1)
-        noisy = lax.all_gather(noisy, "space", axis=0, tiled=True)
+        if space_n == 2:
+            other = lax.ppermute(noisy, "space", [(0, 1), (1, 0)])
+            noisy = jnp.stack([noisy, other])
+            noisy = jnp.where(place == 0, noisy, noisy[::-1]).reshape(2 * height, lat_n, breadth)
+        else:
+            noisy = lax.all_gather(noisy, "space", axis=0, tiled=True)
         inlet = jnp.pad(inlet_conv.T, ((0, 0), (0, taps_pad - taps_n)))
         opened = kernel_call(
             lambda *refs: opening_kernel(breadth, *refs),
             [shape((chan_n, token_n), BF16)] + moments,
             [pltpu.VMEM((8, token_n), F32), pltpu.VMEM((taps_pad, token_n), F32)],
         )(noisy, inlet)
-        wave = waveform_of(timesteps, chan_n // 2)
+        return opened, alpha_bar
+
+    def later(steps):
+        wave = waveform_of(steps, chan_n // 2)
         wave = jnp.broadcast_to(wave.reshape(chan_n, 1), (chan_n, 128))
         gains = (first_gain, second_gain, third_gain, final_gain, layer_gain, time_second_bias)
-        gains = jnp.stack(gains, axis=1)
+        gains = jnp.stack(gains + (layer_gain,) * 2)
         outlet = outlet_conv.T.reshape(lat_n, 9, chan_n).transpose(1, 0, 2)
         outlet = jnp.pad(outlet, ((0, 0), (0, 8 - lat_n), (0, 0))).reshape(72, chan_n)
         bias = jnp.broadcast_to(time_first_bias[None], (8, temb_n))
-        return list(opened) + [wave, gains, outlet, bias]
-
-    (pieces_one, pieces_two), origin, extra = gather_shards((batch_one, batch_two), early)
-    start, sums, squares, wave, gains, outlet, bias = extra
+        return wave, gains, outlet, bias
+
+    (pieces_one, pieces_two), origin, extra = gather_shards(
+        batch_one, batch_two, timesteps, (early, later)
+    )
+    ((start, sums, squares), alpha_bar), (wave, gains, outlet, bias) = extra
     space_id = place.reshape(1).astype(jnp.int32)
 
     count_one = len(pieces_one)
     deep = sum(padded(piece.shape[0]) for piece in pieces_one)
+    deep_two = sum(padded(piece.shape[0]) for piece in pieces_two)
     args = (origin, start, sums, squares, gains, wave, bias, *pieces_one)
     middle, sums, squares = kernel_call(
         lambda *refs: first_kernel(count_one, rows, breadth, *refs),
@@ -657,6 +706,7 @@
             pltpu.VMEM((temb_n, 128), F32),
         ],
         1,
+        2 * token_n * conv_width * chan_n,
     )(*args)
 
     count_two = len(pieces_two)
@@ -667,7 +717,7 @@
         lambda *refs: second_kernel(count_two, rows, breadth, *refs),
         [shape((chan_n, query_n), BF16)] + moments + [shape((chan_n, 128), BF16)],
         [
-            pltpu.VMEM((deep, width_two), BF16),
+            pltpu.VMEM((deep_two, width_two), BF16),
             pltpu.VMEM((chan_n, width_two), BF16),
             pltpu.VMEM((3 * chan_n, token_n), BF16),
             pltpu.VMEM((3 * chan_n, token_n + 2 * breadth), BF16),
@@ -720,4 +770,5 @@
     view = P("batch", "space", None, None)
     in_specs = (view, view, P("batch"), P(), split, P(), split, P())
     in_specs = in_specs + (split,) * 8 + (P(),) * 6
+
     return jax.shard_map(body, mesh=mesh, in_specs=in_specs, out_specs=view, check_vma=False)

time: 132 us -> 120 us (0.909)
  Pallas kernels: 75.8 us -> 65.5 us
  blocking collectives: 4.5 us -> 0 us
  starting transfers between devices: 17.9 us -> 19.5 us
    pallas_call x7 -> x5, Pallas kernels: 75.8 us -> 63.3 us  [call(): pl.pallas_call(body, out_shape=out_shape, in_specs=[smem] * scalars + [vm...]
    all_gather x1 -> x0, blocking collectives: 4.5 us -> none  [early(): noisy = lax.all_gather(noisy, 'space', axis=0, tiled=True)]
    pallas_call x0 -> x1, Pallas kernels: none -> 2.2 us  [pair_up(): pl.pallas_call(pair_kernel, out_shape=wholes + [jax.ShapeDtypeStruct(toke...]
    ppermute x18, starting transfers between devices: 16.4 us -> 18 us  [the longest x6 11.6 us: gather_shards(): moving = lax.ppermute(moving, 'batch', onward)]
    unnamed x46 -> x52, local copies, waits for them, and re-layouts: 3.81 us -> 4.07 us
  transfers between devices with their start and end apart: 19 -> 19, of which waited for: 7 -> 8; matrix products, arithmetic and copies ran while one was open for 4% -> 6% of each run, Pallas kernels for 19% -> 15%
where the time goes in v3:
time: 120 us
  Pallas kernels  65.5 us (55%)
  waiting for transfers between devices  19.7 us (16%)
  starting transfers between devices  19.5 us (16%)
  local copies, waits for them, and re-layouts  8.99 us (7%)
  between operations  3.62 us (3%)
  other arithmetic  2.48 us (2%)
    pallas_call x5, Pallas kernels, call(): pl.pallas_call(body, out_shape=out_shape, in_specs=[smem] * scalars + [vm...  63.3 us
    ppermute x6, waiting for transfers between devices, gather_shards(): moving = lax.ppermute(moving, 'batch', onward)  13.4 us
    ppermute x6, starting transfers between devices, gather_shards(): moving = lax.ppermute(moving, 'batch', onward)  11.6 us
    unnamed x52, local copies, waits for them, and re-layouts  4.07 us
    ppermute x1, waiting for transfers between devices, body(): above = below = lax.ppermute(packed, 'space', [(0, 1), (1, 0)])  2.87 us
  transfers between devices with their start and end apart: 19, of which 8 were waited for; matrix products, arithmetic and copies ran while one was open for 6% of the time, Pallas kernels for 15%

profile of v3, /device:TPU:0, one launch (start us, length us, event | category | flops | bytes accessed | tf_op | source)
XLA Modules:
  0.0 119.8 jit_solution(12333205289972862307)
XLA Ops:
  0.1 2.0 %shard_map.217 = (bf16[20,5440]{1,0:T(8,128)(2,1)}, bf16[20,4800]{1,0:T(8,128)(2,1)}) custom-call(bf16[20,2880]{1,0:T(8,128)(2,1)} %bitcast.43, bf16[80,320]{1,0:T(8,128)(2,1)} %bitcast.46, bf16[20,1280]{1,0:T(8,128)(2,1)} %bitcast.47, bf16[20,2880]{1,0:T(8,128)(2,1)} %bitcast.44, bf16[20,320]{1,0:T(8,128)(2,1)} %bitcast.49, bf16[20,320]{1,0:T(8,128)(2,1)} %bitcast.50, ...), custom_call_target="tpu_custom_call" | custom-call | tf_op jit(solution)/shard_map/pallas_call | solution.py:595
  3.8 0.9 copy.26
  4.7 1.3 %dynamic-slice_bitcast_fusion.refs_0_ = s32[16]{0:T(128)} fusion(s32[16,16]{1,0:T(8,128)} %constant.40.clone, s32[]{:T(128)S(6)} %select_n.19), kind=kLoop, calls=%fused_computation.14 | loop fusion | bytes 132 | tf_op jit(solution)/shard_map/squeeze | solution.py:85
  6.7 0.7 copy-done.10
  7.3 0.7 copy-done.9
  8.0 2.2 %shard_map.218 = (bf16[40,5440]{1,0:T(8,128)(2,1)}, bf16[40,4800]{1,0:T(8,128)(2,1)}, s32[1]{0:T(128)}) custom-call(s32[1]{0:T(128)S(6)} %copy.29.token_ref, bf16[20,5440]{1,0:T(8,128)(2,1)} %get-tuple-element.32.refs_0_, bf16[20,4800]{1,0:T(8,128)(2,1)} %get-tuple-element.33.refs_1_, bf16[20,5440]{1,0:T(8,128)(2,1)} %copy-done.9, bf16[20,4800]{1,0:T(8,128)(2,1)} %copy-done.10), custom_call_target="tpu_custom_call" | custom-call | tf_op jit(solution)/shard_map/pallas_call | solution.py:258
  10.2 1.3 %select_reduce_fusion = f32[]{:T(128)} fusion(f32[1024]{0:T(1024)S(1)} %multiply_bitcast_fusion, s32[]{:T(128)} %bitcast.11), kind=kLoop, calls=%fused_computation.5 | loop fusion | flops 2999 | bytes 4008 | tf_op jit(solution)/shard_map/reduce_sum | solution.py:33
  12.9 3.1 %collective-permute-start.4 = (bf16[40,5440]{1,0:T(8,128)(2,1)}, bf16[40,5440]{1,0:T(8,128)(2,1)S(1)}, u32[]{:S(2)}, u32[]{:S(2)}) collective-permute-start(bf16[40,5440]{1,0:T(8,128)(2,1)} %get-tuple-element.49.refs_7_), channel_id=1, source_target_pairs={{0,8},{2,6},{8,16},{10,2},{16,24},{18,10},{24,28},{26,18},{28,20},... | collective-permute-start | bytes 1305608 | tf_op jit(solution)/shard_map/ppermute | solution.py:90
  16.0 1.6 %collective-permute-start.2 = (bf16[16,4,64]{2,1,0:T(4,128)(2,1)S(1)}, bf16[16,4,64]{2,1,0:T(4,128)(2,1)S(1)}, u32[]{:S(2)}, u32[]{:S(2)}) collective-permute-start(bf16[16,4,64]{2,1,0:T(4,128)(2,1)S(1)} %fusion.1), channel_id=1, source_target_pairs={{0,1},{1,0},{2,3},{3,2},{4,5},{5,4},{6,7},{7,6},{8,9},{9,8},{10,11... | collective-permute-start | bytes 24584 | tf_op jit(solution)/shard_map/ppermute | solution.py:663
  17.6 2.2 %collective-permute-done.2 = bf16[16,4,64]{2,1,0:T(4,128)(2,1)S(1)} collective-permute-done((bf16[16,4,64]{2,1,0:T(4,128)(2,1)S(1)}, bf16[16,4,64]{2,1,0:T(4,128)(2,1)S(1)}, u32[]{:S(2)}, u32[]{:S(2)}) %collective-permute-start.2) | collective-permute-done | bytes 8224 | tf_op jit(solution)/shard_map/ppermute | solution.py:663
  19.8 2.5 %collective-permute-done.4.refs_8_ = bf16[40,5440]{1,0:T(8,128)(2,1)S(1)} collective-permute-done((bf16[40,5440]{1,0:T(8,128)(2,1)}, bf16[40,5440]{1,0:T(8,128)(2,1)S(1)}, u32[]{:S(2)}, u32[]{:S(2)}) %collective-permute-start.4) | collective-permute-done | bytes 435232 | tf_op jit(solution)/shard_map/ppermute | solution.py:90
  22.4 2.1 %collective-permute-start.6 = (bf16[40,5440]{1,0:T(8,128)(2,1)S(1)}, bf16[40,5440]{1,0:T(8,128)(2,1)S(1)}, u32[]{:S(2)}, u32[]{:S(2)}) collective-permute-start(bf16[40,5440]{1,0:T(8,128)(2,1)S(1)} %collective-permute-done.4.refs_8_), channel_id=1, source_target_pairs={{0,8},{2,6},{8,16},{10,2},{16,24},{18,10},{24,28},{26,18},{28,20},... | collective-permute-start | bytes 1305608 | tf_op jit(solution)/shard_map/ppermute | solution.py:90
  25.1 2.9 %shard_map.219 = (bf16[320,2048]{1,0:T(8,128)(2,1)}, f32[320,128]{1,0:T(8,128)}, f32[320,128]{1,0:T(8,128)}) custom-call(bf16[32,4,64]{2,1,0:T(4,128)(2,1)} %bitcast.45, bf16[320,48]{1,0:T(8,128)(2,1)} %pad.12.refs_1_), custom_call_target="tpu_custom_call" | custom-call | tf_op jit(solution)/shard_map/pallas_call | solution.py:595
  28.0 1.6 %collective-permute-start.3 = (bf16[40,4800]{1,0:T(8,128)(2,1)}, bf16[40,4800]{1,0:T(8,128)(2,1)S(1)}, u32[]{:S(2)}, u32[]{:S(2)}) collective-permute-start(bf16[40,4800]{1,0:T(8,128)(2,1)} %get-tuple-element.40.refs_7_), channel_id=1, source_target_pairs={{0,8},{2,6},{8,16},{10,2},{16,24},{18,10},{24,28},{26,18},{28,20},... | collective-permute-start | bytes 1152008 | tf_op jit(solution)/shard_map/ppermute | solution.py:103
  31.8 1.6 %collective-permute-start.8 = (bf16[40,5440]{1,0:T(8,128)(2,1)S(1)}, bf16[40,5440]{1,0:T(8,128)(2,1)S(1)}, u32[]{:S(2)}, u32[]{:S(2)}) collective-permute-start(bf16[40,5440]{1,0:T(8,128)(2,1)S(1)} %collective-permute-done.6.refs_10_), channel_id=1, source_target_pairs={{0,8},{2,6},{8,16},{10,2},{16,24},{18,10},{24,28},{26,18},{28,20},... | collective-permute-start | bytes 1305608 | tf_op jit(solution)/shard_map/ppermute | solution.py:90
  33.5 2.5 %collective-permute-done.3.refs_8_ = bf16[40,4800]{1,0:T(8,128)(2,1)S(1)} collective-permute-done((bf16[40,4800]{1,0:T(8,128)(2,1)}, bf16[40,4800]{1,0:T(8,128)(2,1)S(1)}, u32[]{:S(2)}, u32[]{:S(2)}) %collective-permute-start.3) | collective-permute-done | bytes 384032 | tf_op jit(solution)/shard_map/ppermute | solution.py:103
  36.0 0.7 broadcast_in_dim.12.refs_6_
  36.6 0.7 broadcast_in_dim.11.refs_5_
  37.4 1.6 %collective-permute-start.13 = (bf16[40,4800]{1,0:T(8,128)(2,1)S(1)}, bf16[40,4800]{1,0:T(8,128)(2,1)S(1)}, u32[]{:S(2)}, u32[]{:S(2)}) collective-permute-start(bf16[40,4800]{1,0:T(8,128)(2,1)S(1)} %collective-permute-done.3.refs_8_), channel_id=1, source_target_pairs={{0,8},{2,6},{8,16},{10,2},{16,24},{18,10},{24,28},{26,18},{28,20},... | collective-permute-start | bytes 1152008 | tf_op jit(solution)/shard_map/ppermute | solution.py:103
  39.5 1.2 %collective-permute-done.8.refs_12_ = bf16[40,5440]{1,0:T(8,128)(2,1)S(1)} collective-permute-done((bf16[40,5440]{1,0:T(8,128)(2,1)S(1)}, bf16[40,5440]{1,0:T(8,128)(2,1)S(1)}, u32[]{:S(2)}, u32[]{:S(2)}) %collective-permute-start.8) | collective-permute-done | bytes 435232 | tf_op jit(solution)/shard_map/ppermute | solution.py:90
  40.7 1.6 %collective-permute-start.10 = (bf16[20,5440]{1,0:T(8,128)(2,1)S(1)}, bf16[20,5440]{1,0:T(8,128)(2,1)S(1)}, u32[]{:S(2)}, u32[]{:S(2)}) collective-permute-start(bf16[20,5440]{1,0:T(8,128)(2,1)S(1)} %slice.18), channel_id=1, source_target_pairs={{0,8},{2,6},{8,16},{10,2},{16,24},{18,10},{24,28},{26,18},{28,20},... | collective-permute-start | bytes 652808 | tf_op jit(solution)/shard_map/ppermute | solution.py:92
  42.3 2.8 %collective-permute-done.13.refs_10_ = bf16[40,4800]{1,0:T(8,128)(2,1)S(1)} collective-permute-done((bf16[40,4800]{1,0:T(8,128)(2,1)S(1)}, bf16[40,4800]{1,0:T(8,128)(2,1)S(1)}, u32[]{:S(2)}, u32[]{:S(2)}) %collective-permute-start.13) | collective-permute-done | bytes 384032 | tf_op jit(solution)/shard_map/ppermute | solution.py:103
  45.1 1.6 %collective-permute-start.15 = (bf16[40,4800]{1,0:T(8,128)(2,1)S(1)}, bf16[40,4800]{1,0:T(8,128)(2,1)S(1)}, u32[]{:S(2)}, u32[]{:S(2)}) collective-permute-start(bf16[40,4800]{1,0:T(8,128)(2,1)S(1)} %collective-permute-done.13.refs_10_), channel_id=1, source_target_pairs={{0,8},{2,6},{8,16},{10,2},{16,24},{18,10},{24,28},{26,18},{28,20},... | collective-permute-start | bytes 1152008 | tf_op jit(solution)/shard_map/ppermute | solution.py:103
  46.7 1.3 %collective-permute-done.10.refs_14_ = bf16[20,5440]{1,0:T(8,128)(2,1)S(1)} collective-permute-done((bf16[20,5440]{1,0:T(8,128)(2,1)S(1)}, bf16[20,5440]{1,0:T(8,128)(2,1)S(1)}, u32[]{:S(2)}, u32[]{:S(2)}) %collective-permute-start.10) | collective-permute-done | bytes 217632 | tf_op jit(solution)/shard_map/ppermute | solution.py:92
  48.5 4.4 %collective-permute-done.15.refs_12_ = bf16[40,4800]{1,0:T(8,128)(2,1)S(1)} collective-permute-done((bf16[40,4800]{1,0:T(8,128)(2,1)S(1)}, bf16[40,4800]{1,0:T(8,128)(2,1)S(1)}, u32[]{:S(2)}, u32[]{:S(2)}) %collective-permute-start.15) | collective-permute-done | bytes 384032 | tf_op jit(solution)/shard_map/ppermute | solution.py:103
  52.9 1.6 %collective-permute-start.17 = (bf16[40,4800]{1,0:T(8,128)(2,1)S(1)}, bf16[40,4800]{1,0:T(8,128)(2,1)S(1)}, u32[]{:S(2)}, u32[]{:S(2)}) collective-permute-start(bf16[40,4800]{1,0:T(8,128)(2,1)S(1)} %collective-permute-done.15.refs_12_), channel_id=1, source_target_pairs={{0,8},{2,6},{8,16},{10,2},{16,24},{18,10},{24,28},{26,18},{28,20},... | collective-permute-start | bytes 1152008 | tf_op jit(solution)/shard_map/ppermute | solution.py:106
  54.6 14.9 %shard_map.220 = (bf16[320,2048]{1,0:T(8,128)(2,1)}, f32[320,128]{1,0:T(8,128)}, f32[320,128]{1,0:T(8,128)}) custom-call(s32[16]{0:T(128)} %dynamic-slice_bitcast_fusion.refs_0_, bf16[320,2048]{1,0:T(8,128)(2,1)} %get-tuple-element.43.refs_1_.refs_5_, f32[320,128]{1,0:T(8,128)} %get-tuple-element.44.refs_2_, f32[320,128]{1,0:T(8,128)} %get-tuple-element.45.refs_3_, ...), custom_call_target="tpu_custom_call" | custom-call | flops 3774873600 | tf_op jit(solution)/shard_map/pallas_call | solution.py:595
  69.6 0.7 copy-done.3
  70.7 40.1 %shard_map.221 = (bf16[320,1024]{1,0:T(8,128)(2,1)}, f32[320,128]{1,0:T(8,128)}, f32[320,128]{1,0:T(8,128)}, bf16[320,128]{1,0:T(8,128)(2,1)}) custom-call(s32[16]{0:T(128)} %dynamic-slice_bitcast_fusion.refs_0_, s32[1]{0:T(128)} %bitcast.refs_1_.refs_0_, bf16[320,2048]{1,0:T(8,128)(2,1)} %get-tuple-element.50.refs_2_, ...), custom_call_target="tpu_custom_call" | custom-call | tf_op jit(solution)/shard_map/pallas_call | solution.py:595
  110.7 1.5 %collective-permute-start.18 = (bf16[320,128]{1,0:T(8,128)(2,1)}, bf16[320,128]{1,0:T(8,128)(2,1)S(1)}, u32[]{:S(2)}, u32[]{:S(2)}) collective-permute-start(bf16[320,128]{1,0:T(8,128)(2,1)} %get-tuple-element.55), channel_id=1, source_target_pairs={{0,1},{1,0},{2,3},{3,2},{4,5},{5,4},{6,7},{7,6},{8,9},{9,8},{10,11... | collective-permute-start | bytes 245768 | tf_op jit(solution)/shard_map/ppermute | solution.py:740
  112.9 2.9 %collective-permute-done.18.refs_3_.refs_4_ = bf16[320,128]{1,0:T(8,128)(2,1)S(1)} collective-permute-done((bf16[320,128]{1,0:T(8,128)(2,1)}, bf16[320,128]{1,0:T(8,128)(2,1)S(1)}, u32[]{:S(2)}, u32[]{:S(2)}) %collective-permute-start.18) | collective-permute-done | bytes 81952 | tf_op jit(solution)/shard_map/ppermute | solution.py:740
  116.4 3.4 %shard_map.222 = f32[16,4,64]{2,1,0:T(4,128)} custom-call(s32[1]{0:T(128)} %bitcast.refs_1_.refs_0_, f32[1]{0:T(128)S(6)} %sub.16.refs_1_, bf16[320,1024]{1,0:T(8,128)(2,1)} %get-tuple-element.54.refs_2_, bf16[320,128]{1,0:T(8,128)(2,1)} %copy-done.7, bf16[320,128]{1,0:T(8,128)(2,1)} %copy-done.7, f32[320,128]{1,0:T(8,128)} %get-tuple-element.56.refs_5_, ...), custom_call_target="tpu_custom_call" | custom-call | tf_op jit(solution)/shard_map/pallas_call | solution.py:595
  (92 shorter events, 6.2 us)
Async XLA Ops:
  0.0 29.6 %copy-start.15 = (f32[320]{0:T(512)S(1)}, f32[320]{0:T(512)}, u32[]{:S(2)}) copy-start(f32[320]{0:T(512)} %param.30) | copy-start | bytes 3844
  0.0 29.6 %copy-start.16 = (f32[320]{0:T(512)S(1)}, f32[320]{0:T(512)}, u32[]{:S(2)}) copy-start(f32[320]{0:T(512)} %param.40) | copy-start | bytes 3844
  0.0 29.6 %copy-start.17 = (f32[320]{0:T(512)S(1)}, f32[320]{0:T(512)}, u32[]{:S(2)}) copy-start(f32[320]{0:T(512)} %param.41) | copy-start | bytes 3844
  0.0 29.6 %copy-start.18 = (f32[320]{0:T(512)S(1)}, f32[320]{0:T(512)}, u32[]{:S(2)}) copy-start(f32[320]{0:T(512)} %param.42) | copy-start | bytes 3844
  0.0 29.6 %copy-start.19 = (f32[320]{0:T(512)S(1)}, f32[320]{0:T(512)}, u32[]{:S(2)}) copy-start(f32[320]{0:T(512)} %param.43) | copy-start | bytes 3844
  0.0 29.6 %copy-start.20 = (f32[320]{0:T(512)S(1)}, f32[320]{0:T(512)}, u32[]{:S(2)}) copy-start(f32[320]{0:T(512)} %param.44) | copy-start | bytes 3844
  0.0 29.7 %copy-start.13 = (bf16[2880,4]{0,1:T(4,128)(2,1)S(1)}, bf16[2880,4]{0,1:T(4,128)(2,1)}, u32[]{:S(2)}) copy-start(bf16[2880,4]{0,1:T(4,128)(2,1)} %param.39) | copy-start | bytes 69124
  0.1 35.9 %copy-start.14 = (f32[1280]{0:T(1024)S(1)}, f32[1280]{0:T(1024)}, u32[]{:S(2)}) copy-start(f32[1280]{0:T(1024)} %param.28) | copy-start | bytes 15364
  2.1 4.6 %collective-permute-start.1 = (bf16[20,4800]{1,0:T(8,128)(2,1)}, bf16[20,4800]{1,0:T(8,128)(2,1)S(1)}, u32[]{:S(2)}, u32[]{:S(2)}) collective-permute-start(bf16[20,4800]{1,0:T(8,128)(2,1)} %get-tuple-element.33.refs_1_), channel_id=1, source_target_pairs={{0,2},{2,0},{4,6},{6,4},{8,10},{10,8},{12,14},{14,12},{16,18},{18,... | collective-permute-start | bytes 576008 | tf_op jit(solution)/shard_map/ppermute | solution.py:83
  2.6 4.1 %collective-permute-start = (bf16[20,5440]{1,0:T(8,128)(2,1)}, bf16[20,5440]{1,0:T(8,128)(2,1)S(1)}, u32[]{:S(2)}, u32[]{:S(2)}) collective-permute-start(bf16[20,5440]{1,0:T(8,128)(2,1)} %get-tuple-element.32.refs_0_), channel_id=1, source_target_pairs={{0,2},{2,0},{4,6},{6,4},{8,10},{10,8},{12,14},{14,12},{16,18},{18,... | collective-permute-start | bytes 652808 | tf_op jit(solution)/shard_map/ppermute | solution.py:83
  12.9 9.5 %collective-permute-start.4 = (bf16[40,5440]{1,0:T(8,128)(2,1)}, bf16[40,5440]{1,0:T(8,128)(2,1)S(1)}, u32[]{:S(2)}, u32[]{:S(2)}) collective-permute-start(bf16[40,5440]{1,0:T(8,128)(2,1)} %get-tuple-element.49.refs_7_), channel_id=1, source_target_pairs={{0,8},{2,6},{8,16},{10,2},{16,24},{18,10},{24,28},{26,18},{28,20},... | collective-permute-start | bytes 1305608 | tf_op jit(solution)/shard_map/ppermute | solution.py:90
  16.0 3.8 %collective-permute-start.2 = (bf16[16,4,64]{2,1,0:T(4,128)(2,1)S(1)}, bf16[16,4,64]{2,1,0:T(4,128)(2,1)S(1)}, u32[]{:S(2)}, u32[]{:S(2)}) collective-permute-start(bf16[16,4,64]{2,1,0:T(4,128)(2,1)S(1)} %fusion.1), channel_id=1, source_target_pairs={{0,1},{1,0},{2,3},{3,2},{4,5},{5,4},{6,7},{7,6},{8,9},{9,8},{10,11... | collective-permute-start | bytes 24584 | tf_op jit(solution)/shard_map/ppermute | solution.py:663
  22.4 32.2 %copy-start.21 = (bf16[40,5440]{1,0:T(8,128)(2,1)}, bf16[40,5440]{1,0:T(8,128)(2,1)S(1)}, u32[]{:S(2)}) copy-start(bf16[40,5440]{1,0:T(8,128)(2,1)S(1)} %collective-permute-done.4.refs_8_) | copy-start | bytes 1305604
  22.4 9.4 %collective-permute-start.6 = (bf16[40,5440]{1,0:T(8,128)(2,1)S(1)}, bf16[40,5440]{1,0:T(8,128)(2,1)S(1)}, u32[]{:S(2)}, u32[]{:S(2)}) collective-permute-start(bf16[40,5440]{1,0:T(8,128)(2,1)S(1)} %collective-permute-done.4.refs_8_), channel_id=1, source_target_pairs={{0,8},{2,6},{8,16},{10,2},{16,24},{18,10},{24,28},{26,18},{28,20},... | collective-permute-start | bytes 1305608 | tf_op jit(solution)/shard_map/ppermute | solution.py:90
  28.0 7.9 %collective-permute-start.3 = (bf16[40,4800]{1,0:T(8,128)(2,1)}, bf16[40,4800]{1,0:T(8,128)(2,1)S(1)}, u32[]{:S(2)}, u32[]{:S(2)}) collective-permute-start(bf16[40,4800]{1,0:T(8,128)(2,1)} %get-tuple-element.40.refs_7_), channel_id=1, source_target_pairs={{0,8},{2,6},{8,16},{10,2},{16,24},{18,10},{24,28},{26,18},{28,20},... | collective-permute-start | bytes 1152008 | tf_op jit(solution)/shard_map/ppermute | solution.py:103
  31.8 21.1 %copy-start.22 = (bf16[40,5440]{1,0:T(8,128)(2,1)}, bf16[40,5440]{1,0:T(8,128)(2,1)S(1)}, u32[]{:S(2)}) copy-start(bf16[40,5440]{1,0:T(8,128)(2,1)S(1)} %collective-permute-done.6.refs_10_) | copy-start | bytes 1305604
  31.8 8.9 %collective-permute-start.8 = (bf16[40,5440]{1,0:T(8,128)(2,1)S(1)}, bf16[40,5440]{1,0:T(8,128)(2,1)S(1)}, u32[]{:S(2)}, u32[]{:S(2)}) collective-permute-start(bf16[40,5440]{1,0:T(8,128)(2,1)S(1)} %collective-permute-done.6.refs_10_), channel_id=1, source_target_pairs={{0,8},{2,6},{8,16},{10,2},{16,24},{18,10},{24,28},{26,18},{28,20},... | collective-permute-start | bytes 1305608 | tf_op jit(solution)/shard_map/ppermute | solution.py:90
  36.0 33.5 %copy-start = (bf16[40,4800]{1,0:T(8,128)(2,1)}, bf16[40,4800]{1,0:T(8,128)(2,1)S(1)}, u32[]{:S(2)}) copy-start(bf16[40,4800]{1,0:T(8,128)(2,1)S(1)} %collective-permute-done.3.refs_8_) | copy-start | bytes 1152004
  37.4 7.7 %collective-permute-start.13 = (bf16[40,4800]{1,0:T(8,128)(2,1)S(1)}, bf16[40,4800]{1,0:T(8,128)(2,1)S(1)}, u32[]{:S(2)}, u32[]{:S(2)}) collective-permute-start(bf16[40,4800]{1,0:T(8,128)(2,1)S(1)} %collective-permute-done.3.refs_8_), channel_id=1, source_target_pairs={{0,8},{2,6},{8,16},{10,2},{16,24},{18,10},{24,28},{26,18},{28,20},... | collective-permute-start | bytes 1152008 | tf_op jit(solution)/shard_map/ppermute | solution.py:103
  39.0 9.0 %collective-permute-start.5 = (bf16[40,5440]{1,0:T(8,128)(2,1)S(1)}, bf16[40,5440]{1,0:T(8,128)(2,1)}, u32[]{:S(2)}, u32[]{:S(2)}) collective-permute-start(bf16[40,5440]{1,0:T(8,128)(2,1)S(1)} %collective-permute-done.4.refs_8_), channel_id=1, source_target_pairs={{0,2},{2,0},{4,6},{6,4},{8,10},{10,8},{12,14},{14,12},{16,18},{18,... | collective-permute-start | bytes 1305608 | tf_op jit(solution)/shard_map/ppermute | solution.py:91
  39.0 13.9 %collective-permute-start.7 = (bf16[40,5440]{1,0:T(8,128)(2,1)S(1)}, bf16[40,5440]{1,0:T(8,128)(2,1)S(1)}, u32[]{:S(2)}, u32[]{:S(2)}) collective-permute-start(bf16[40,5440]{1,0:T(8,128)(2,1)S(1)} %collective-permute-done.6.refs_10_), channel_id=1, source_target_pairs={{0,2},{2,0},{4,6},{6,4},{8,10},{10,8},{12,14},{14,12},{16,18},{18,... | collective-permute-start | bytes 1305608 | tf_op jit(solution)/shard_map/ppermute | solution.py:91
  40.7 7.2 %collective-permute-start.10 = (bf16[20,5440]{1,0:T(8,128)(2,1)S(1)}, bf16[20,5440]{1,0:T(8,128)(2,1)S(1)}, u32[]{:S(2)}, u32[]{:S(2)}) collective-permute-start(bf16[20,5440]{1,0:T(8,128)(2,1)S(1)} %slice.18), channel_id=1, source_target_pairs={{0,8},{2,6},{8,16},{10,2},{16,24},{18,10},{24,28},{26,18},{28,20},... | collective-permute-start | bytes 652808 | tf_op jit(solution)/shard_map/ppermute | solution.py:92
  42.3 12.2 %collective-permute-start.9 = (bf16[40,5440]{1,0:T(8,128)(2,1)S(1)}, bf16[40,5440]{1,0:T(8,128)(2,1)}, u32[]{:S(2)}, u32[]{:S(2)}) collective-permute-start(bf16[40,5440]{1,0:T(8,128)(2,1)S(1)} %collective-permute-done.8.refs_12_), channel_id=1, source_target_pairs={{0,2},{2,0},{4,6},{6,4},{8,10},{10,8},{12,14},{14,12},{16,18},{18,... | collective-permute-start | bytes 1305608 | tf_op jit(solution)/shard_map/ppermute | solution.py:91
  45.1 24.4 %copy-start.1 = (bf16[40,4800]{1,0:T(8,128)(2,1)}, bf16[40,4800]{1,0:T(8,128)(2,1)S(1)}, u32[]{:S(2)}) copy-start(bf16[40,4800]{1,0:T(8,128)(2,1)S(1)} %collective-permute-done.13.refs_10_) | copy-start | bytes 1152004
  45.1 7.7 %collective-permute-start.15 = (bf16[40,4800]{1,0:T(8,128)(2,1)S(1)}, bf16[40,4800]{1,0:T(8,128)(2,1)S(1)}, u32[]{:S(2)}, u32[]{:S(2)}) collective-permute-start(bf16[40,4800]{1,0:T(8,128)(2,1)S(1)} %collective-permute-done.13.refs_10_), channel_id=1, source_target_pairs={{0,8},{2,6},{8,16},{10,2},{16,24},{18,10},{24,28},{26,18},{28,20},... | collective-permute-start | bytes 1152008 | tf_op jit(solution)/shard_map/ppermute | solution.py:103
  48.0 6.6 %collective-permute-start.11 = (bf16[20,5440]{1,0:T(8,128)(2,1)S(1)}, bf16[20,5440]{1,0:T(8,128)(2,1)}, u32[]{:S(2)}, u32[]{:S(2)}) collective-permute-start(bf16[20,5440]{1,0:T(8,128)(2,1)S(1)} %collective-permute-done.10.refs_14_), channel_id=1, source_target_pairs={{0,2},{2,0},{4,6},{6,4},{8,10},{10,8},{12,14},{14,12},{16,18},{18,... | collective-permute-start | bytes 652808 | tf_op jit(solution)/shard_map/ppermute | solution.py:93
  48.0 21.5 %collective-permute-start.12 = (bf16[40,4800]{1,0:T(8,128)(2,1)S(1)}, bf16[40,4800]{1,0:T(8,128)(2,1)S(1)}, u32[]{:S(2)}, u32[]{:S(2)}) collective-permute-start(bf16[40,4800]{1,0:T(8,128)(2,1)S(1)} %collective-permute-done.3.refs_8_), channel_id=1, source_target_pairs={{0,2},{2,0},{4,6},{6,4},{8,10},{10,8},{12,14},{14,12},{16,18},{18,... | collective-permute-start | bytes 1152008 | tf_op jit(solution)/shard_map/ppermute | solution.py:104
  52.9 16.6 %copy-start.2 = (bf16[40,4800]{1,0:T(8,128)(2,1)}, bf16[40,4800]{1,0:T(8,128)(2,1)S(1)}, u32[]{:S(2)}) copy-start(bf16[40,4800]{1,0:T(8,128)(2,1)S(1)} %collective-permute-done.15.refs_12_) | copy-start | bytes 1152004
  52.9 16.7 %collective-permute-start.14 = (bf16[40,4800]{1,0:T(8,128)(2,1)S(1)}, bf16[40,4800]{1,0:T(8,128)(2,1)S(1)}, u32[]{:S(2)}, u32[]{:S(2)}) collective-permute-start(bf16[40,4800]{1,0:T(8,128)(2,1)S(1)} %collective-permute-done.13.refs_10_), channel_id=1, source_target_pairs={{0,2},{2,0},{4,6},{6,4},{8,10},{10,8},{12,14},{14,12},{16,18},{18,... | collective-permute-start | bytes 1152008 | tf_op jit(solution)/shard_map/ppermute | solution.py:104
  52.9 16.7 %collective-permute-start.17 = (bf16[40,4800]{1,0:T(8,128)(2,1)S(1)}, bf16[40,4800]{1,0:T(8,128)(2,1)S(1)}, u32[]{:S(2)}, u32[]{:S(2)}) collective-permute-start(bf16[40,4800]{1,0:T(8,128)(2,1)S(1)} %collective-permute-done.15.refs_12_), channel_id=1, source_target_pairs={{0,8},{2,6},{8,16},{10,2},{16,24},{18,10},{24,28},{26,18},{28,20},... | collective-permute-start | bytes 1152008 | tf_op jit(solution)/shard_map/ppermute | solution.py:106
  54.5 15.0 %collective-permute-start.16 = (bf16[40,4800]{1,0:T(8,128)(2,1)S(1)}, bf16[40,4800]{1,0:T(8,128)(2,1)S(1)}, u32[]{:S(2)}, u32[]{:S(2)}) collective-permute-start(bf16[40,4800]{1,0:T(8,128)(2,1)S(1)} %collective-permute-done.15.refs_12_), channel_id=1, source_target_pairs={{0,2},{2,0},{4,6},{6,4},{8,10},{10,8},{12,14},{14,12},{16,18},{18,... | collective-permute-start | bytes 1152008 | tf_op jit(solution)/shard_map/ppermute | solution.py:104
  110.7 5.0 %collective-permute-start.18 = (bf16[320,128]{1,0:T(8,128)(2,1)}, bf16[320,128]{1,0:T(8,128)(2,1)S(1)}, u32[]{:S(2)}, u32[]{:S(2)}) collective-permute-start(bf16[320,128]{1,0:T(8,128)(2,1)} %get-tuple-element.55), channel_id=1, source_target_pairs={{0,1},{1,0},{2,3},{3,2},{4,5},{5,4},{6,7},{7,6},{8,9},{9,8},{10,11... | collective-permute-start | bytes 245768 | tf_op jit(solution)/shard_map/ppermute | solution.py:740
  (12 other events, 59.8 us)

commit v4 on v3

--- a/solution.py
+++ b/solution.py
@@ -96,13 +96,12 @@
     pieces_two = [moving]
     extra = []
     for step in range(1, half):
-        if step <= len(beside):
-            now = (beside[step - 1](token), origin)
-            moving, (now, origin) = lax.optimization_barrier((moving, now))
+        if 1 < step <= len(beside) + 1:
+            moving, now = lax.optimization_barrier((moving, beside[step - 2](token)))
             extra.append(now)
         moving = lax.ppermute(moving, "batch", onward)
         pieces_two += [moving, lax.ppermute(moving, "batch", sibling)]
-    extra += [work(token) for work in beside[half - 1 :]]
+    extra += [work(token) for work in beside[max(half - 2, 0) :]]
     pieces_two.append(lax.ppermute(moving, "batch", onward))
     return (pieces_one, pieces_two), origin, extra
 

time: 120 us -> 118 us (0.983)
  waiting for transfers between devices: 19.7 us -> 17 us
    unnamed x52 -> x50, local copies, waits for them, and re-layouts: 4.07 us -> 4.07 us
  transfers between devices with their start and end apart: 19 -> 19, of which waited for: 8 -> 7; matrix products, arithmetic and copies ran while one was open for 6% -> 7% of each run, Pallas kernels for 15% -> 15%
where the time goes in v4:
time: 118 us
  Pallas kernels  65.5 us (56%)
  starting transfers between devices  20.1 us (17%)
  waiting for transfers between devices  17 us (14%)
  local copies, waits for them, and re-layouts  8.9 us (8%)
  between operations  3.82 us (3%)
  other arithmetic  2.57 us (2%)
    pallas_call x5, Pallas kernels, call(): pl.pallas_call(body, out_shape=out_shape, in_specs=[smem] * scalars + [vm...  63.3 us
    ppermute x6, waiting for transfers between devices, gather_shards(): moving = lax.ppermute(moving, 'batch', onward)  12.2 us
    ppermute x6, starting transfers between devices, gather_shards(): moving = lax.ppermute(moving, 'batch', onward)  11.7 us
    unnamed x50, local copies, waits for them, and re-layouts  4.07 us
    ppermute x1, waiting for transfers between devices, body(): above = below = lax.ppermute(packed, 'space', [(0, 1), (1, 0)])  2.44 us
  transfers between devices with their start and end apart: 19, of which 7 were waited for; matrix products, arithmetic and copies ran while one was open for 7% of the time, Pallas kernels for 15%

profile of v4, /device:TPU:0, one launch (start us, length us, event | category | flops | bytes accessed | tf_op | source)
XLA Modules:
  0.0 117.8 jit_solution(12039409541040739660)
XLA Ops:
  0.1 2.0 %shard_map.217 = (bf16[20,5440]{1,0:T(8,128)(2,1)}, bf16[20,4800]{1,0:T(8,128)(2,1)}) custom-call(bf16[20,2880]{1,0:T(8,128)(2,1)} %bitcast.43, bf16[80,320]{1,0:T(8,128)(2,1)} %bitcast.46, bf16[20,1280]{1,0:T(8,128)(2,1)} %bitcast.47, bf16[20,2880]{1,0:T(8,128)(2,1)} %bitcast.44, bf16[20,320]{1,0:T(8,128)(2,1)} %bitcast.49, bf16[20,320]{1,0:T(8,128)(2,1)} %bitcast.50, ...), custom_call_target="tpu_custom_call" | custom-call | tf_op jit(solution)/shard_map/pallas_call | solution.py:594
  3.7 0.9 copy.26
  4.6 0.7 pad.12.refs_1_
  5.2 0.7 copy-done.10
  5.9 0.7 copy-done.9
  6.6 2.2 %shard_map.218 = (bf16[40,5440]{1,0:T(8,128)(2,1)}, bf16[40,4800]{1,0:T(8,128)(2,1)}, s32[1]{0:T(128)}) custom-call(s32[1]{0:T(128)S(6)} %copy.29.token_ref, bf16[20,5440]{1,0:T(8,128)(2,1)} %get-tuple-element.30.refs_0_, bf16[20,4800]{1,0:T(8,128)(2,1)} %get-tuple-element.31.refs_1_, bf16[20,5440]{1,0:T(8,128)(2,1)} %copy-done.9, bf16[20,4800]{1,0:T(8,128)(2,1)} %copy-done.10), custom_call_target="tpu_custom_call" | custom-call | tf_op jit(solution)/shard_map/pallas_call | solution.py:257
  8.8 3.1 %collective-permute-start.5 = (bf16[40,5440]{1,0:T(8,128)(2,1)}, bf16[40,5440]{1,0:T(8,128)(2,1)S(1)}, u32[]{:S(2)}, u32[]{:S(2)}) collective-permute-start(bf16[40,5440]{1,0:T(8,128)(2,1)} %get-tuple-element.45.refs_7_), channel_id=1, source_target_pairs={{0,8},{2,6},{8,16},{10,2},{16,24},{18,10},{24,28},{26,18},{28,20},... | collective-permute-start | bytes 1305608 | tf_op jit(solution)/shard_map/ppermute | solution.py:90
  12.1 1.4 %select_reduce_fusion = f32[]{:T(128)} fusion(f32[1024]{0:T(1024)S(1)} %multiply_bitcast_fusion, s32[]{:T(128)} %bitcast.11), kind=kLoop, calls=%fused_computation.5 | loop fusion | flops 2999 | bytes 4008 | tf_op jit(solution)/shard_map/reduce_sum | solution.py:33
  14.9 1.6 %collective-permute-start.2 = (bf16[40,4800]{1,0:T(8,128)(2,1)}, bf16[40,4800]{1,0:T(8,128)(2,1)S(1)}, u32[]{:S(2)}, u32[]{:S(2)}) collective-permute-start(bf16[40,4800]{1,0:T(8,128)(2,1)} %get-tuple-element.32.refs_7_), channel_id=1, source_target_pairs={{0,8},{2,6},{8,16},{10,2},{16,24},{18,10},{24,28},{26,18},{28,20},... | collective-permute-start | bytes 1152008 | tf_op jit(solution)/shard_map/ppermute | solution.py:102
  16.6 1.7 %collective-permute-done.5.refs_8_ = bf16[40,5440]{1,0:T(8,128)(2,1)S(1)} collective-permute-done((bf16[40,5440]{1,0:T(8,128)(2,1)}, bf16[40,5440]{1,0:T(8,128)(2,1)S(1)}, u32[]{:S(2)}, u32[]{:S(2)}) %collective-permute-start.5) | collective-permute-done | bytes 435232 | tf_op jit(solution)/shard_map/ppermute | solution.py:90
  18.3 2.1 %collective-permute-start.7 = (bf16[40,5440]{1,0:T(8,128)(2,1)S(1)}, bf16[40,5440]{1,0:T(8,128)(2,1)S(1)}, u32[]{:S(2)}, u32[]{:S(2)}) collective-permute-start(bf16[40,5440]{1,0:T(8,128)(2,1)S(1)} %collective-permute-done.5.refs_8_), channel_id=1, source_target_pairs={{0,8},{2,6},{8,16},{10,2},{16,24},{18,10},{24,28},{26,18},{28,20},... | collective-permute-start | bytes 1305608 | tf_op jit(solution)/shard_map/ppermute | solution.py:90
  20.4 1.6 %collective-permute-start.3 = (bf16[16,4,64]{2,1,0:T(4,128)(2,1)S(1)}, bf16[16,4,64]{2,1,0:T(4,128)(2,1)S(1)}, u32[]{:S(2)}, u32[]{:S(2)}) collective-permute-start(bf16[16,4,64]{2,1,0:T(4,128)(2,1)S(1)} %fusion.1), channel_id=1, source_target_pairs={{0,1},{1,0},{2,3},{3,2},{4,5},{5,4},{6,7},{7,6},{8,9},{9,8},{10,11... | collective-permute-start | bytes 24584 | tf_op jit(solution)/shard_map/ppermute | solution.py:662
  22.0 2.2 %collective-permute-done.3 = bf16[16,4,64]{2,1,0:T(4,128)(2,1)S(1)} collective-permute-done((bf16[16,4,64]{2,1,0:T(4,128)(2,1)S(1)}, bf16[16,4,64]{2,1,0:T(4,128)(2,1)S(1)}, u32[]{:S(2)}, u32[]{:S(2)}) %collective-permute-start.3) | collective-permute-done | bytes 8224 | tf_op jit(solution)/shard_map/ppermute | solution.py:662
  24.3 3.3 %collective-permute-done.7.refs_10_ = bf16[40,5440]{1,0:T(8,128)(2,1)S(1)} collective-permute-done((bf16[40,5440]{1,0:T(8,128)(2,1)S(1)}, bf16[40,5440]{1,0:T(8,128)(2,1)S(1)}, u32[]{:S(2)}, u32[]{:S(2)}) %collective-permute-start.7) | collective-permute-done | bytes 435232 | tf_op jit(solution)/shard_map/ppermute | solution.py:90
  27.6 1.7 %collective-permute-start.9 = (bf16[40,5440]{1,0:T(8,128)(2,1)S(1)}, bf16[40,5440]{1,0:T(8,128)(2,1)S(1)}, u32[]{:S(2)}, u32[]{:S(2)}) collective-permute-start(bf16[40,5440]{1,0:T(8,128)(2,1)S(1)} %collective-permute-done.7.refs_10_), channel_id=1, source_target_pairs={{0,8},{2,6},{8,16},{10,2},{16,24},{18,10},{24,28},{26,18},{28,20},... | collective-permute-start | bytes 1305608 | tf_op jit(solution)/shard_map/ppermute | solution.py:90
  29.3 0.6 reverse_select_fusion
  29.9 2.9 %shard_map.219 = (bf16[320,2048]{1,0:T(8,128)(2,1)}, f32[320,128]{1,0:T(8,128)}, f32[320,128]{1,0:T(8,128)}) custom-call(bf16[32,4,64]{2,1,0:T(4,128)(2,1)} %bitcast.45, bf16[320,48]{1,0:T(8,128)(2,1)} %pad.12.refs_1_), custom_call_target="tpu_custom_call" | custom-call | tf_op jit(solution)/shard_map/pallas_call | solution.py:594
  32.9 1.6 %collective-permute-start.4 = (bf16[40,4800]{1,0:T(8,128)(2,1)S(1)}, bf16[40,4800]{1,0:T(8,128)(2,1)S(1)}, u32[]{:S(2)}, u32[]{:S(2)}) collective-permute-start(bf16[40,4800]{1,0:T(8,128)(2,1)S(1)} %collective-permute-done.2.refs_8_), channel_id=1, source_target_pairs={{0,8},{2,6},{8,16},{10,2},{16,24},{18,10},{24,28},{26,18},{28,20},... | collective-permute-start | bytes 1152008 | tf_op jit(solution)/shard_map/ppermute | solution.py:102
  35.3 0.6 pad_bitcast_fusion.refs_8_
  37.3 1.6 %collective-permute-start.11 = (bf16[20,5440]{1,0:T(8,128)(2,1)S(1)}, bf16[20,5440]{1,0:T(8,128)(2,1)S(1)}, u32[]{:S(2)}, u32[]{:S(2)}) collective-permute-start(bf16[20,5440]{1,0:T(8,128)(2,1)S(1)} %slice.18), channel_id=1, source_target_pairs={{0,8},{2,6},{8,16},{10,2},{16,24},{18,10},{24,28},{26,18},{28,20},... | collective-permute-start | bytes 652808 | tf_op jit(solution)/shard_map/ppermute | solution.py:92
  39.0 1.6 %collective-permute-done.4.refs_10_ = bf16[40,4800]{1,0:T(8,128)(2,1)S(1)} collective-permute-done((bf16[40,4800]{1,0:T(8,128)(2,1)S(1)}, bf16[40,4800]{1,0:T(8,128)(2,1)S(1)}, u32[]{:S(2)}, u32[]{:S(2)}) %collective-permute-start.4) | collective-permute-done | bytes 384032 | tf_op jit(solution)/shard_map/ppermute | solution.py:102
  40.6 0.8 broadcast_in_dim.11.refs_5_
  42.0 1.6 %collective-permute-start.15 = (bf16[40,4800]{1,0:T(8,128)(2,1)S(1)}, bf16[40,4800]{1,0:T(8,128)(2,1)S(1)}, u32[]{:S(2)}, u32[]{:S(2)}) collective-permute-start(bf16[40,4800]{1,0:T(8,128)(2,1)S(1)} %collective-permute-done.4.refs_10_), channel_id=1, source_target_pairs={{0,8},{2,6},{8,16},{10,2},{16,24},{18,10},{24,28},{26,18},{28,20},... | collective-permute-start | bytes 1152008 | tf_op jit(solution)/shard_map/ppermute | solution.py:102
  44.2 5.5 %collective-permute-done.15.refs_12_ = bf16[40,4800]{1,0:T(8,128)(2,1)S(1)} collective-permute-done((bf16[40,4800]{1,0:T(8,128)(2,1)S(1)}, bf16[40,4800]{1,0:T(8,128)(2,1)S(1)}, u32[]{:S(2)}, u32[]{:S(2)}) %collective-permute-start.15) | collective-permute-done | bytes 384032 | tf_op jit(solution)/shard_map/ppermute | solution.py:102
  50.2 1.6 %collective-permute-start.17 = (bf16[40,4800]{1,0:T(8,128)(2,1)S(1)}, bf16[40,4800]{1,0:T(8,128)(2,1)S(1)}, u32[]{:S(2)}, u32[]{:S(2)}) collective-permute-start(bf16[40,4800]{1,0:T(8,128)(2,1)S(1)} %collective-permute-done.15.refs_12_), channel_id=1, source_target_pairs={{0,8},{2,6},{8,16},{10,2},{16,24},{18,10},{24,28},{26,18},{28,20},... | collective-permute-start | bytes 1152008 | tf_op jit(solution)/shard_map/ppermute | solution.py:105
  51.8 1.2 %dynamic-slice_bitcast_fusion.refs_0_ = s32[16]{0:T(128)} fusion(s32[16,16]{1,0:T(8,128)} %constant.40.clone, s32[]{:T(128)S(6)} %select_n.19), kind=kLoop, calls=%fused_computation.14 | loop fusion | bytes 132 | tf_op jit(solution)/shard_map/squeeze | solution.py:85
  53.0 14.9 %shard_map.220 = (bf16[320,2048]{1,0:T(8,128)(2,1)}, f32[320,128]{1,0:T(8,128)}, f32[320,128]{1,0:T(8,128)}) custom-call(s32[16]{0:T(128)} %dynamic-slice_bitcast_fusion.refs_0_, bf16[320,2048]{1,0:T(8,128)(2,1)} %get-tuple-element.38.refs_1_.refs_5_, f32[320,128]{1,0:T(8,128)} %get-tuple-element.39.refs_2_, f32[320,128]{1,0:T(8,128)} %get-tuple-element.40.refs_3_, ...), custom_call_target="tpu_custom_call" | custom-call | flops 3774873600 | tf_op jit(solution)/shard_map/pallas_call | solution.py:594
  68.0 0.7 copy-done.3
  69.1 40.0 %shard_map.221 = (bf16[320,1024]{1,0:T(8,128)(2,1)}, f32[320,128]{1,0:T(8,128)}, f32[320,128]{1,0:T(8,128)}, bf16[320,128]{1,0:T(8,128)(2,1)}) custom-call(s32[16]{0:T(128)} %dynamic-slice_bitcast_fusion.refs_0_, s32[1]{0:T(128)} %bitcast.refs_1_.refs_0_, bf16[320,2048]{1,0:T(8,128)(2,1)} %get-tuple-element.46.refs_2_, ...), custom_call_target="tpu_custom_call" | custom-call | tf_op jit(solution)/shard_map/pallas_call | solution.py:594
  109.1 1.5 %collective-permute-start.18 = (bf16[320,128]{1,0:T(8,128)(2,1)}, bf16[320,128]{1,0:T(8,128)(2,1)S(1)}, u32[]{:S(2)}, u32[]{:S(2)}) collective-permute-start(bf16[320,128]{1,0:T(8,128)(2,1)} %get-tuple-element.51), channel_id=1, source_target_pairs={{0,1},{1,0},{2,3},{3,2},{4,5},{5,4},{6,7},{7,6},{8,9},{9,8},{10,11... | collective-permute-start | bytes 245768 | tf_op jit(solution)/shard_map/ppermute | solution.py:739
  111.4 2.4 %collective-permute-done.18.refs_3_.refs_4_ = bf16[320,128]{1,0:T(8,128)(2,1)S(1)} collective-permute-done((bf16[320,128]{1,0:T(8,128)(2,1)}, bf16[320,128]{1,0:T(8,128)(2,1)S(1)}, u32[]{:S(2)}, u32[]{:S(2)}) %collective-permute-start.18) | collective-permute-done | bytes 81952 | tf_op jit(solution)/shard_map/ppermute | solution.py:739
  114.4 3.4 %shard_map.222 = f32[16,4,64]{2,1,0:T(4,128)} custom-call(s32[1]{0:T(128)} %bitcast.refs_1_.refs_0_, f32[1]{0:T(128)S(6)} %sub.16.refs_1_, bf16[320,1024]{1,0:T(8,128)(2,1)} %get-tuple-element.50.refs_2_, bf16[320,128]{1,0:T(8,128)(2,1)} %copy-done.7, bf16[320,128]{1,0:T(8,128)(2,1)} %copy-done.7, f32[320,128]{1,0:T(8,128)} %get-tuple-element.52.refs_5_, ...), custom_call_target="tpu_custom_call" | custom-call | tf_op jit(solution)/shard_map/pallas_call | solution.py:594
  (90 shorter events, 5.5 us)
Async XLA Ops:
  0.0 20.4 %copy-start.12 = (f32[1,16,64,4]{2,3,1,0:T(4,128)S(1)}, f32[1,16,64,4]{2,3,1,0:T(4,128)}, u32[]{:S(2)}) copy-start(f32[1,16,64,4]{2,3,1,0:T(4,128)} %param.23) | copy-start | bytes 49156
  0.0 34.4 %copy-start.15 = (f32[320]{0:T(512)S(1)}, f32[320]{0:T(512)}, u32[]{:S(2)}) copy-start(f32[320]{0:T(512)} %param.40) | copy-start | bytes 3844
  0.0 34.4 %copy-start.16 = (f32[320]{0:T(512)S(1)}, f32[320]{0:T(512)}, u32[]{:S(2)}) copy-start(f32[320]{0:T(512)} %param.41) | copy-start | bytes 3844
  0.0 34.4 %copy-start.17 = (f32[320]{0:T(512)S(1)}, f32[320]{0:T(512)}, u32[]{:S(2)}) copy-start(f32[320]{0:T(512)} %param.42) | copy-start | bytes 3844
  0.0 34.5 %copy-start.18 = (f32[320]{0:T(512)S(1)}, f32[320]{0:T(512)}, u32[]{:S(2)}) copy-start(f32[320]{0:T(512)} %param.43) | copy-start | bytes 3844
  0.0 34.5 %copy-start.19 = (f32[320]{0:T(512)S(1)}, f32[320]{0:T(512)}, u32[]{:S(2)}) copy-start(f32[320]{0:T(512)} %param.44) | copy-start | bytes 3844
  0.0 34.5 %copy-start.20 = (f32[320]{0:T(512)S(1)}, f32[320]{0:T(512)}, u32[]{:S(2)}) copy-start(f32[320]{0:T(512)} %param.30) | copy-start | bytes 3844
  0.0 34.5 %copy-start.13 = (bf16[2880,4]{0,1:T(4,128)(2,1)S(1)}, bf16[2880,4]{0,1:T(4,128)(2,1)}, u32[]{:S(2)}) copy-start(bf16[2880,4]{0,1:T(4,128)(2,1)} %param.39) | copy-start | bytes 69124
  2.1 3.2 %collective-permute-start = (bf16[20,5440]{1,0:T(8,128)(2,1)}, bf16[20,5440]{1,0:T(8,128)(2,1)S(1)}, u32[]{:S(2)}, u32[]{:S(2)}) collective-permute-start(bf16[20,5440]{1,0:T(8,128)(2,1)} %get-tuple-element.30.refs_0_), channel_id=1, source_target_pairs={{0,2},{2,0},{4,6},{6,4},{8,10},{10,8},{12,14},{14,12},{16,18},{18,... | collective-permute-start | bytes 652808 | tf_op jit(solution)/shard_map/ppermute | solution.py:83
  2.6 2.6 %collective-permute-start.1 = (bf16[20,4800]{1,0:T(8,128)(2,1)}, bf16[20,4800]{1,0:T(8,128)(2,1)S(1)}, u32[]{:S(2)}, u32[]{:S(2)}) collective-permute-start(bf16[20,4800]{1,0:T(8,128)(2,1)} %get-tuple-element.31.refs_1_), channel_id=1, source_target_pairs={{0,2},{2,0},{4,6},{6,4},{8,10},{10,8},{12,14},{14,12},{16,18},{18,... | collective-permute-start | bytes 576008 | tf_op jit(solution)/shard_map/ppermute | solution.py:83
  3.7 37.7 %copy-start.14 = (f32[1280]{0:T(1024)S(1)}, f32[1280]{0:T(1024)}, u32[]{:S(2)}) copy-start(f32[1280]{0:T(1024)} %param.28) | copy-start | bytes 15364
  8.8 9.5 %collective-permute-start.5 = (bf16[40,5440]{1,0:T(8,128)(2,1)}, bf16[40,5440]{1,0:T(8,128)(2,1)S(1)}, u32[]{:S(2)}, u32[]{:S(2)}) collective-permute-start(bf16[40,5440]{1,0:T(8,128)(2,1)} %get-tuple-element.45.refs_7_), channel_id=1, source_target_pairs={{0,8},{2,6},{8,16},{10,2},{16,24},{18,10},{24,28},{26,18},{28,20},... | collective-permute-start | bytes 1305608 | tf_op jit(solution)/shard_map/ppermute | solution.py:90
  14.9 18.0 %collective-permute-start.2 = (bf16[40,4800]{1,0:T(8,128)(2,1)}, bf16[40,4800]{1,0:T(8,128)(2,1)S(1)}, u32[]{:S(2)}, u32[]{:S(2)}) collective-permute-start(bf16[40,4800]{1,0:T(8,128)(2,1)} %get-tuple-element.32.refs_7_), channel_id=1, source_target_pairs={{0,8},{2,6},{8,16},{10,2},{16,24},{18,10},{24,28},{26,18},{28,20},... | collective-permute-start | bytes 1152008 | tf_op jit(solution)/shard_map/ppermute | solution.py:102
  18.3 34.7 %copy-start.21 = (bf16[40,5440]{1,0:T(8,128)(2,1)}, bf16[40,5440]{1,0:T(8,128)(2,1)S(1)}, u32[]{:S(2)}) copy-start(bf16[40,5440]{1,0:T(8,128)(2,1)S(1)} %collective-permute-done.5.refs_8_) | copy-start | bytes 1305604
  18.3 9.3 %collective-permute-start.7 = (bf16[40,5440]{1,0:T(8,128)(2,1)S(1)}, bf16[40,5440]{1,0:T(8,128)(2,1)S(1)}, u32[]{:S(2)}, u32[]{:S(2)}) collective-permute-start(bf16[40,5440]{1,0:T(8,128)(2,1)S(1)} %collective-permute-done.5.refs_8_), channel_id=1, source_target_pairs={{0,8},{2,6},{8,16},{10,2},{16,24},{18,10},{24,28},{26,18},{28,20},... | collective-permute-start | bytes 1305608 | tf_op jit(solution)/shard_map/ppermute | solution.py:90
  20.4 3.8 %collective-permute-start.3 = (bf16[16,4,64]{2,1,0:T(4,128)(2,1)S(1)}, bf16[16,4,64]{2,1,0:T(4,128)(2,1)S(1)}, u32[]{:S(2)}, u32[]{:S(2)}) collective-permute-start(bf16[16,4,64]{2,1,0:T(4,128)(2,1)S(1)} %fusion.1), channel_id=1, source_target_pairs={{0,1},{1,0},{2,3},{3,2},{4,5},{5,4},{6,7},{7,6},{8,9},{9,8},{10,11... | collective-permute-start | bytes 24584 | tf_op jit(solution)/shard_map/ppermute | solution.py:662
  27.6 22.1 %copy-start.22 = (bf16[40,5440]{1,0:T(8,128)(2,1)}, bf16[40,5440]{1,0:T(8,128)(2,1)S(1)}, u32[]{:S(2)}) copy-start(bf16[40,5440]{1,0:T(8,128)(2,1)S(1)} %collective-permute-done.7.refs_10_) | copy-start | bytes 1305604
  27.6 9.6 %collective-permute-start.9 = (bf16[40,5440]{1,0:T(8,128)(2,1)S(1)}, bf16[40,5440]{1,0:T(8,128)(2,1)S(1)}, u32[]{:S(2)}, u32[]{:S(2)}) collective-permute-start(bf16[40,5440]{1,0:T(8,128)(2,1)S(1)} %collective-permute-done.7.refs_10_), channel_id=1, source_target_pairs={{0,8},{2,6},{8,16},{10,2},{16,24},{18,10},{24,28},{26,18},{28,20},... | collective-permute-start | bytes 1305608 | tf_op jit(solution)/shard_map/ppermute | solution.py:90
  32.8 35.1 %copy-start = (bf16[40,4800]{1,0:T(8,128)(2,1)}, bf16[40,4800]{1,0:T(8,128)(2,1)S(1)}, u32[]{:S(2)}) copy-start(bf16[40,4800]{1,0:T(8,128)(2,1)S(1)} %collective-permute-done.2.refs_8_) | copy-start | bytes 1152004
  32.9 7.7 %collective-permute-start.4 = (bf16[40,4800]{1,0:T(8,128)(2,1)S(1)}, bf16[40,4800]{1,0:T(8,128)(2,1)S(1)}, u32[]{:S(2)}, u32[]{:S(2)}) collective-permute-start(bf16[40,4800]{1,0:T(8,128)(2,1)S(1)} %collective-permute-done.2.refs_8_), channel_id=1, source_target_pairs={{0,8},{2,6},{8,16},{10,2},{16,24},{18,10},{24,28},{26,18},{28,20},... | collective-permute-start | bytes 1152008 | tf_op jit(solution)/shard_map/ppermute | solution.py:102
  36.7 7.4 %collective-permute-start.6 = (bf16[40,5440]{1,0:T(8,128)(2,1)S(1)}, bf16[40,5440]{1,0:T(8,128)(2,1)}, u32[]{:S(2)}, u32[]{:S(2)}) collective-permute-start(bf16[40,5440]{1,0:T(8,128)(2,1)S(1)} %collective-permute-done.5.refs_8_), channel_id=1, source_target_pairs={{0,2},{2,0},{4,6},{6,4},{8,10},{10,8},{12,14},{14,12},{16,18},{18,... | collective-permute-start | bytes 1305608 | tf_op jit(solution)/shard_map/ppermute | solution.py:91
  36.7 13.0 %collective-permute-start.8 = (bf16[40,5440]{1,0:T(8,128)(2,1)S(1)}, bf16[40,5440]{1,0:T(8,128)(2,1)}, u32[]{:S(2)}, u32[]{:S(2)}) collective-permute-start(bf16[40,5440]{1,0:T(8,128)(2,1)S(1)} %collective-permute-done.7.refs_10_), channel_id=1, source_target_pairs={{0,2},{2,0},{4,6},{6,4},{8,10},{10,8},{12,14},{14,12},{16,18},{18,... | collective-permute-start | bytes 1305608 | tf_op jit(solution)/shard_map/ppermute | solution.py:91
  37.3 6.4 %collective-permute-start.11 = (bf16[20,5440]{1,0:T(8,128)(2,1)S(1)}, bf16[20,5440]{1,0:T(8,128)(2,1)S(1)}, u32[]{:S(2)}, u32[]{:S(2)}) collective-permute-start(bf16[20,5440]{1,0:T(8,128)(2,1)S(1)} %slice.18), channel_id=1, source_target_pairs={{0,8},{2,6},{8,16},{10,2},{16,24},{18,10},{24,28},{26,18},{28,20},... | collective-permute-start | bytes 652808 | tf_op jit(solution)/shard_map/ppermute | solution.py:92
  40.6 27.4 %copy-start.1 = (bf16[40,4800]{1,0:T(8,128)(2,1)}, bf16[40,4800]{1,0:T(8,128)(2,1)S(1)}, u32[]{:S(2)}) copy-start(bf16[40,4800]{1,0:T(8,128)(2,1)S(1)} %collective-permute-done.4.refs_10_) | copy-start | bytes 1152004
  42.0 7.7 %collective-permute-start.15 = (bf16[40,4800]{1,0:T(8,128)(2,1)S(1)}, bf16[40,4800]{1,0:T(8,128)(2,1)S(1)}, u32[]{:S(2)}, u32[]{:S(2)}) collective-permute-start(bf16[40,4800]{1,0:T(8,128)(2,1)S(1)} %collective-permute-done.4.refs_10_), channel_id=1, source_target_pairs={{0,8},{2,6},{8,16},{10,2},{16,24},{18,10},{24,28},{26,18},{28,20},... | collective-permute-start | bytes 1152008 | tf_op jit(solution)/shard_map/ppermute | solution.py:102
  43.6 9.5 %collective-permute-start.10 = (bf16[40,5440]{1,0:T(8,128)(2,1)S(1)}, bf16[40,5440]{1,0:T(8,128)(2,1)}, u32[]{:S(2)}, u32[]{:S(2)}) collective-permute-start(bf16[40,5440]{1,0:T(8,128)(2,1)S(1)} %collective-permute-done.9.refs_12_), channel_id=1, source_target_pairs={{0,2},{2,0},{4,6},{6,4},{8,10},{10,8},{12,14},{14,12},{16,18},{18,... | collective-permute-start | bytes 1305608 | tf_op jit(solution)/shard_map/ppermute | solution.py:91
  43.7 6.5 %collective-permute-start.12 = (bf16[20,5440]{1,0:T(8,128)(2,1)S(1)}, bf16[20,5440]{1,0:T(8,128)(2,1)}, u32[]{:S(2)}, u32[]{:S(2)}) collective-permute-start(bf16[20,5440]{1,0:T(8,128)(2,1)S(1)} %collective-permute-done.11.refs_14_), channel_id=1, source_target_pairs={{0,2},{2,0},{4,6},{6,4},{8,10},{10,8},{12,14},{14,12},{16,18},{18,... | collective-permute-start | bytes 652808 | tf_op jit(solution)/shard_map/ppermute | solution.py:93
  44.1 23.9 %collective-permute-start.13 = (bf16[40,4800]{1,0:T(8,128)(2,1)S(1)}, bf16[40,4800]{1,0:T(8,128)(2,1)S(1)}, u32[]{:S(2)}, u32[]{:S(2)}) collective-permute-start(bf16[40,4800]{1,0:T(8,128)(2,1)S(1)} %collective-permute-done.2.refs_8_), channel_id=1, source_target_pairs={{0,2},{2,0},{4,6},{6,4},{8,10},{10,8},{12,14},{14,12},{16,18},{18,... | collective-permute-start | bytes 1152008 | tf_op jit(solution)/shard_map/ppermute | solution.py:103
  49.7 18.3 %collective-permute-start.14 = (bf16[40,4800]{1,0:T(8,128)(2,1)S(1)}, bf16[40,4800]{1,0:T(8,128)(2,1)S(1)}, u32[]{:S(2)}, u32[]{:S(2)}) collective-permute-start(bf16[40,4800]{1,0:T(8,128)(2,1)S(1)} %collective-permute-done.4.refs_10_), channel_id=1, source_target_pairs={{0,2},{2,0},{4,6},{6,4},{8,10},{10,8},{12,14},{14,12},{16,18},{18,... | collective-permute-start | bytes 1152008 | tf_op jit(solution)/shard_map/ppermute | solution.py:103
  49.7 18.3 %collective-permute-start.16 = (bf16[40,4800]{1,0:T(8,128)(2,1)S(1)}, bf16[40,4800]{1,0:T(8,128)(2,1)S(1)}, u32[]{:S(2)}, u32[]{:S(2)}) collective-permute-start(bf16[40,4800]{1,0:T(8,128)(2,1)S(1)} %collective-permute-done.15.refs_12_), channel_id=1, source_target_pairs={{0,2},{2,0},{4,6},{6,4},{8,10},{10,8},{12,14},{14,12},{16,18},{18,... | collective-permute-start | bytes 1152008 | tf_op jit(solution)/shard_map/ppermute | solution.py:103
  50.2 17.8 %collective-permute-start.17 = (bf16[40,4800]{1,0:T(8,128)(2,1)S(1)}, bf16[40,4800]{1,0:T(8,128)(2,1)S(1)}, u32[]{:S(2)}, u32[]{:S(2)}) collective-permute-start(bf16[40,4800]{1,0:T(8,128)(2,1)S(1)} %collective-permute-done.15.refs_12_), channel_id=1, source_target_pairs={{0,8},{2,6},{8,16},{10,2},{16,24},{18,10},{24,28},{26,18},{28,20},... | collective-permute-start | bytes 1152008 | tf_op jit(solution)/shard_map/ppermute | solution.py:105
  109.1 4.7 %collective-permute-start.18 = (bf16[320,128]{1,0:T(8,128)(2,1)}, bf16[320,128]{1,0:T(8,128)(2,1)S(1)}, u32[]{:S(2)}, u32[]{:S(2)}) collective-permute-start(bf16[320,128]{1,0:T(8,128)(2,1)} %get-tuple-element.51), channel_id=1, source_target_pairs={{0,1},{1,0},{2,3},{3,2},{4,5},{5,4},{6,7},{7,6},{8,9},{9,8},{10,11... | collective-permute-start | bytes 245768 | tf_op jit(solution)/shard_map/ppermute | solution.py:739
  (11 other events, 69.4 us)
